TPU v7x, 32 devices: a whole 2x2x4 slice. The times are simulated.
32 devices in a mesh: fft: 8 (over z, y), band: 4 (over x, core).
Axes of the slice: x: 2, y: 2, z: 4, core: 2. Of those that a mesh axis runs over, the one named last changes fastest.
Arguments:
- coefficients: bfloat16 [48, 184320], P('band', 'fft'), may hold values from -0.078125 to 0.078125
- occupations: float32 [48], P('band'), may hold values from 0.5 to 2
- columns: int32 [1280], P('fft'), may hold values from 0 to 5183
- counts: int32 [8], P('fft'), may hold values from 1 to 160, 512 in all
- plane_slot: int32 [144], replicated, may hold values from -1 to 143, as said below
Outputs:
- density: float32 [144, 144, 144], P('fft', 'band')
Inputs may be any that keep to these rules, and one draw needn't show every extreme that they name: The counts sum to 512, and one of them equals 160. `plane_slot`: every plane 0 .. 143 stands in exactly one slot; the other slots hold -1.
All inputs are finite; a program needn't handle non-finite values. No bound on the sum of `counts` on one device may be relied on, other than what follows from the above.
Results may differ from a plain program's by a relative error of at most 0.0095.
Values may be sent and summed in bfloat16 or wider, within the bound.
No kernel may reach another device: no remote copies, remote signals or barrier semaphores. Data moves between devices by JAX's collectives and lax.ppermute only.
A program may use at most 192 MiB of HBM per device.

v0:
```python
import math

import jax
import jax.numpy as jnp
from jax import lax
from jax.sharding import PartitionSpec as P

N = 144
GB = 72


def phase_pair(freq_count, positions, grid):
    freqs = jnp.arange(freq_count, dtype=jnp.int32) - freq_count // 2
    turns = jnp.mod(freqs[:, None] * positions[None, :], grid)
    angles = turns.astype(jnp.float32) * (2.0 * math.pi / grid)
    return (jnp.cos(angles), jnp.sin(angles))


def stick_table(plane_slot):
    valid_slot = (plane_slot >= 0).astype(jnp.float32)
    cosine, sine_part = phase_pair(GB, jnp.maximum(plane_slot, 0), N)
    cosine = cosine * valid_slot[None, :]
    sine_part = sine_part * valid_slot[None, :]
    upper_rows = jnp.concatenate([cosine, sine_part], axis=1)
    lower_rows = jnp.concatenate([-sine_part, cosine], axis=1)
    return jnp.concatenate([upper_rows, lower_rows], axis=0).astype(jnp.bfloat16)


def row_table():
    cosine, sine_part = phase_pair(GB, jnp.arange(N, dtype=jnp.int32), N)
    upper_rows = jnp.concatenate([cosine, sine_part], axis=1)
    lower_rows = jnp.concatenate([-sine_part, cosine], axis=1)
    return jnp.concatenate([upper_rows, lower_rows], axis=0).astype(jnp.bfloat16)


def column_table():
    cosine, sine_part = phase_pair(GB, jnp.arange(N, dtype=jnp.int32), N)
    return jnp.concatenate([cosine.T, sine_part.T], axis=0).astype(jnp.bfloat16)


def grid_squares(received, row_pick, col_pick, row_tab, col_tab):
    bands_here, parts, planes, slot_total = received.shape
    flat_rows = bands_here * parts * planes
    by_slot = received.reshape(flat_rows, slot_total).T
    weighted = by_slot[:, :, None] * col_pick[:, None, :]
    placed = jnp.dot(
        row_pick.T, weighted.reshape(slot_total, flat_rows * GB), preferred_element_type=jnp.float32
    )
    placed = placed.reshape(GB, bands_here, parts, planes, GB)
    g_plane = (
        jnp.transpose(placed, (1, 3, 0, 2, 4))
        .reshape(bands_here, planes, GB, 2 * GB)
        .astype(jnp.bfloat16)
    )
    half_way = jnp.einsum(
        "bpgk,kj->bpgj", g_plane, row_tab, preferred_element_type=jnp.float32
    ).astype(jnp.bfloat16)
    full_grid = jnp.einsum("xg,bpgj->bpxj", col_tab, half_way, preferred_element_type=jnp.float32)
    real_part = full_grid[:, :, :N, :N] - full_grid[:, :, N:, N:]
    imag_part = full_grid[:, :, N:, :N] + full_grid[:, :, :N, N:]
    return real_part * real_part + imag_part * imag_part


def shards(coefficients, occupations, columns, counts, plane_slot):
    bands_here = coefficients.shape[0]
    coefficients = coefficients.reshape(bands_here, -1, 2 * GB)
    sticks_here = coefficients.shape[1]
    slot_count = plane_slot.shape[0]
    total_bands = bands_here * lax.axis_size("band")
    plane_tab = stick_table(plane_slot)
    row_tab = row_table()
    col_tab = column_table()
    stick_place = jnp.arange(sticks_here, dtype=jnp.int32)
    live_here = (stick_place < counts[0]).astype(jnp.bfloat16)
    coefficients = coefficients * live_here[None, :, None]
    every_column = lax.all_gather(columns, "fft", axis=0, tiled=True)
    freq_ids = jnp.arange(GB, dtype=jnp.int32)[None, :]
    row_pick = ((every_column // GB)[:, None] == freq_ids).astype(jnp.bfloat16)
    col_pick = ((every_column % GB)[:, None] == freq_ids).astype(jnp.bfloat16)
    weights = occupations / total_bands
    sticks = jnp.einsum("bsg,go->bos", coefficients, plane_tab, preferred_element_type=jnp.float32)
    outgoing = sticks.astype(jnp.bfloat16).reshape(
        coefficients.shape[0], 2, slot_count, sticks_here
    )
    squares = grid_squares(
        lax.all_to_all(outgoing, "fft", split_axis=2, concat_axis=3, tiled=True),
        row_pick,
        col_pick,
        row_tab,
        col_tab,
    )
    local_sum = jnp.einsum("b,bpxy->pxy", weights, squares)
    return lax.psum_scatter(
        local_sum.astype(jnp.bfloat16), "band", scatter_dimension=1, tiled=True
    ).astype(jnp.float32)


def solution(mesh):
    placed = (P("band", "fft"), P("band"), P("fft"), P("fft"), P())
    return jax.shard_map(
        shards, mesh=mesh, in_specs=placed, out_specs=P("fft", "band", None), check_vma=False
    )
```

profile of v0, /device:TPU:0, one launch (start us, length us, event | category | flops | bytes accessed | tf_op | source)
XLA Modules:
  0.0 325.2 jit_solution(15147241202249923715)
XLA Ops:
  6.5 0.7 broadcast_maximum_fusion
  7.2 0.7 compare_convert_fusion.1
  7.9 2.8 reshape.49
  11.4 1.3 fusion.48
  12.6 0.7 fusion.6
  13.4 1.0 copy.13
  14.4 2.6 copy.14
  17.0 7.3 %all-to-all-start = ((bf16[12,2,144,160]{3,1,0,2:T(2,128)(2,1)}), bf16[12,2,144,160]{3,1,0,2:T(2,128)(2,1)S(1)}, u32[]{:S(2)}, u32[]{:S(2)}) async-start(bf16[12,2,144,160]{3,1,0,2:T(2,128)(2,1)} %copy.14), calls=%async_computation | async-start | bytes 3538944 | tf_op jit(solution)/shard_map/all_to_all | solution.py:86
  24.3 0.0 all-reduce.4.cloned.1.call-start
  24.4 1.2 dynamic-slice
  26.3 0.9 dynamic-update-slice
  27.2 38.7 %all-reduce = s32[1280]{0:T(1024)S(1)} all-reduce(s32[1280]{0:T(1024)S(1)} %dynamic-update-slice), channel_id=1, replica_groups=mesh['fft'=8,'band'=4] {'fft'}, use_global_device_ids=true, to_apply=%add | all-reduce | flops 1280 | bytes 10240
  65.9 1.0 cosine_convert_fusion
  66.9 0.7 fusion.11
  67.6 0.0 all-to-all-done
  67.6 0.6 copy.16
  68.2 2.1 reshape.51
  70.3 26.9 %broadcast_multiply_fusion = bf16[1280,432,72]{0,2,1:T(8,128)(2,1)} fusion(bf16[1280,72]{0,1:T(8,128)(2,1)} %fusion.11, bf16[1280,432]{0,1:T(8,128)(2,1)S(1)} %bitcast.59), kind=kLoop, calls=%fused_computation | loop fusion | flops 39813120 | bytes 80916480 | tf_op jit(solution)/shard_map/mul | solution.py:45
  97.2 41.5 %convert_bitcast_fusion = bf16[12,18,72,2,72]{4,2,1,3,0:T(8,128)(2,1)} fusion(bf16[12,2,18,72,1280]{4,3,2,1,0:T(8,128)(2,1)} %bitcast.15, s32[1280]{0:T(1024)S(1)} %get-tuple-element.5), kind=kOutput, calls=%fused_computation.9 | convolution fusion | flops 5735420928 | bytes 84110336 | tf_op jit(solution)/shard_map/dot_general | solution.py:46
  138.8 0.0 copy-start
  138.8 0.0 copy-start.1
  138.8 0.0 copy-start.2
  138.8 0.0 copy-start.3
  138.8 0.0 copy-start.4
  138.8 11.3 %copy.17 = bf16[12,18,72,2,72]{2,4,3,1,0:T(8,128)(2,1)} copy(bf16[12,18,72,2,72]{4,2,1,3,0:T(8,128)(2,1)} %convert_bitcast_fusion) | data formatting | bytes 8957952 | tf_op jit(solution)/shard_map/convert_element_type | solution.py:53
  150.0 0.0 copy-done
  150.0 0.0 copy-done.1
  150.0 0.0 copy-done.2
  150.1 0.0 copy-done.3
  150.1 0.0 copy-done.4
  150.1 37.3 %convolution_bitcast_fusion = f32[12,18,288,288]{2,3,1,0:T(8,128)} fusion(bf16[12,18,72,144]{2,3,1,0:T(8,128)(2,1)} %bitcast.55, bf16[72,144]{1,0:T(8,128)(2,1)S(1)} %copy-done.2, bf16[72,144]{1,0:T(8,128)(2,1)S(1)} %copy-done.1, bf16[72,144]{1,0:T(8,128)(2,1)S(1)} %copy-done, bf16[144,72]{0,1:T(8,128)(2,1)S(1)} %copy-done.4, bf16[144,72]{0,1:T(8,128)(2,1)S(1)} %copy-done.3), kind=kOutput, calls=%fused_computation.1 | convolution fusion | flops 3874728960 | bytes 76246272 | tf_op jit(solution)/shard_map/xg,bpgj->bpxj/dot_general | solution.py:58
  187.4 46.4 %fusion.1 = bf16[12,18,144,144]{2,3,1,0:T(8,128)(2,1)} fusion(f32[12,18,288,288]{2,3,1,0:T(8,128)} %convolution_bitcast_fusion), kind=kLoop, calls=%fused_computation.4 | loop fusion | flops 26873856 | bytes 80621568 | tf_op jit(solution)/shard_map/add | solution.py:61
  233.8 0.0 copy-start.5
  233.8 34.0 %copy.25 = bf16[12,18,144,144]{3,0,2,1:T(8,128)(2,1)} copy(bf16[12,18,144,144]{2,3,1,0:T(8,128)(2,1)} %fusion.1) | data formatting | bytes 17915904 | tf_op jit(solution)/shard_map/add | solution.py:61
  267.7 0.0 copy-done.5
  267.7 0.0 copy-start.6
  267.7 8.6 %fusion.52 = bf16[1,18,144,144]{3,0,2,1:T(2,128)(2,1)S(1)} fusion(bf16[12,18,144,144]{3,0,2,1:T(8,128)(2,1)} %copy.25, f32[12]{0:T(128)S(1)} %copy-done.5), kind=kOutput, calls=%fused_computation.76 | convolution fusion | flops 8957964 | bytes 9704496 | tf_op jit(solution)/shard_map/b,bpxy->pxy/dot_general | solution.py:92
  276.3 1.4 copy.31
  277.7 0.0 all-reduce.4.cloned.1.call-update
  277.7 0.0 copy-done.6
  277.7 0.6 dynamic-slice.1
  279.0 37.4 %all-reduce.4.cloned.1.call-done = bf16[18,144,144]{2,1,0:T(8,128)(2,1)} async-done(((bf16[18,144,144]{2,1,0:T(8,128)(2,1)}), bf16[18,144,144]{2,1,0:T(8,128)(2,1)}) %all-reduce.4.cloned.1.call-update) | async-done | bytes 746512
  316.4 2.0 dynamic-slice_convert_fusion
  (4 shorter events, 0.0 us)
Async XLA Ops:
  17.0 50.6 %all-to-all-start = ((bf16[12,2,144,160]{3,1,0,2:T(2,128)(2,1)}), bf16[12,2,144,160]{3,1,0,2:T(2,128)(2,1)S(1)}, u32[]{:S(2)}, u32[]{:S(2)}) async-start(bf16[12,2,144,160]{3,1,0,2:T(2,128)(2,1)} %copy.14), calls=%async_computation | async-start | bytes 3538944 | tf_op jit(solution)/shard_map/all_to_all | solution.py:86
  24.3 292.1 %all-reduce.4.cloned.1.call-start = ((), (), s32[]{:S(2)}) async-start(), calls=%async_computation.1 | async-start | bytes 2654208
  138.8 11.3 %copy-start = (bf16[72,144]{1,0:T(8,128)(2,1)S(1)}, bf16[72,144]{1,0:T(8,128)(2,1)}, u32[]{:S(2)}) copy-start(bf16[72,144]{1,0:T(8,128)(2,1)} %get-tuple-element.12) | copy-start | bytes 62212
  138.8 11.3 %copy-start.1 = (bf16[72,144]{1,0:T(8,128)(2,1)S(1)}, bf16[72,144]{1,0:T(8,128)(2,1)}, u32[]{:S(2)}) copy-start(bf16[72,144]{1,0:T(8,128)(2,1)} %get-tuple-element.13) | copy-start | bytes 62212
  138.8 11.3 %copy-start.2 = (bf16[72,144]{1,0:T(8,128)(2,1)S(1)}, bf16[72,144]{1,0:T(8,128)(2,1)}, u32[]{:S(2)}) copy-start(bf16[72,144]{1,0:T(8,128)(2,1)} %get-tuple-element.14) | copy-start | bytes 62212
  138.8 11.3 %copy-start.3 = (bf16[144,72]{0,1:T(8,128)(2,1)S(1)}, bf16[144,72]{0,1:T(8,128)(2,1)}, u32[]{:S(2)}) copy-start(bf16[144,72]{0,1:T(8,128)(2,1)} %get-tuple-element.10) | copy-start | bytes 62212
  138.8 11.3 %copy-start.4 = (bf16[144,72]{0,1:T(8,128)(2,1)S(1)}, bf16[144,72]{0,1:T(8,128)(2,1)}, u32[]{:S(2)}) copy-start(bf16[144,72]{0,1:T(8,128)(2,1)} %get-tuple-element.11) | copy-start | bytes 62212
  233.8 34.0 %copy-start.5 = (f32[12]{0:T(128)S(1)}, f32[12]{0:T(128)}, u32[]{:S(2)}) copy-start(f32[12]{0:T(128)} %param.6) | copy-start | bytes 148
  267.7 10.0 %copy-start.6 = (u32[32]{0:T(128)S(1)}, u32[32]{0:T(128)}, u32[]{:S(2)}) copy-start(u32[32]{0:T(128)} %constant.55) | copy-start | bytes 388
Sparse Core Ops, SparseCore 0:
  277.9 38.5 all-reduce.3
where the time goes:
time: 327 us; the launch traced here: 325 us
  matrix products  88.1 us (27%)
  other arithmetic  79.7 us (24%)
  local copies, waits for them, and re-layouts  58.4 us (18%)
  blocking collectives  38.7 us (12%)
  waiting for transfers between devices  37.5 us (11%)
  between operations  15.5 us (5%)
  starting transfers between devices  7.35 us (2%)
    add x1, other arithmetic, grid_squares(): return real_part * real_part + imag_part * imag_part  46.4 us
    dot_general x1, matrix products, grid_squares(): jnp.dot(row_pick.T, weighted.reshape(slot_total, flat_rows * GB), preferr...  41.5 us
    unnamed x1, blocking collectives  38.7 us
    unnamed x2, waiting for transfers between devices  37.5 us
    dot_general x1, matrix products, grid_squares(): jnp.einsum('xg,bpgj->bpxj', col_tab, half_way, preferred_element_type=jnp...  37.3 us
    add x1, local copies, waits for them, and re-layouts, grid_squares(): return real_part * real_part + imag_part * imag_part  34 us
    mul x1, other arithmetic, grid_squares(): weighted = by_slot[:, :, None] * col_pick[:, None, :]  26.9 us
    convert_element_type x1, local copies, waits for them, and re-layouts, grid_squares(): g_plane = jnp.transpose(placed, (1, 3, 0, 2, 4)).reshape(bands_here, plan...  11.3 us
  transfers between devices with their start and end apart: 2, of which 1 were waited for; matrix products, arithmetic and copies ran while one was open for 1% of the time, Pallas kernels for 0%

commit v1 on v0

v1 whole, which is shorter than its diff:
```python
import functools
import math

import jax
import jax.numpy as jnp
import numpy as np
from jax import lax
from jax.experimental import pallas as pl
from jax.experimental.pallas import tpu as pltpu
from jax.sharding import PartitionSpec as P

N = 144
GB = 72
LANES = 128
TAIL = N - LANES
INFO = 16
GROUPS = 3


def wave_tables():
    freqs = np.arange(GB) - GB // 2
    angles = (freqs[:, None] * np.arange(N)[None, :] % N) * (2.0 * math.pi / N)
    cosine, sine = np.cos(angles), np.sin(angles)
    rows = np.zeros((2 * LANES, 4 * LANES), np.float32)
    for col, real_from, imag_from in ((0, cosine, -sine), (1, sine, cosine)):
        rows[:GB, col * LANES : (col + 1) * LANES] = real_from[:, :LANES]
        rows[LANES : LANES + GB, col * LANES : (col + 1) * LANES] = imag_from[:, :LANES]
        at = (2 + col) * LANES
        rows[:GB, at : at + TAIL] = real_from[:, LANES:]
        rows[LANES : LANES + GB, at : at + TAIL] = imag_from[:, LANES:]
    cols = np.block([[cosine.T, -sine.T], [sine.T, cosine.T]])
    return jnp.asarray(rows, jnp.bfloat16), jnp.asarray(cols, jnp.bfloat16)


def plane_table(plane_slot, chunks, ranks, group):
    held = plane_slot.reshape(ranks, chunks, -1).swapaxes(0, 1)
    planes = held.shape[2]
    held = jnp.concatenate(
        [held, held, jnp.full((chunks, ranks, group - 2 * planes), -1, jnp.int32)], axis=2
    )
    imag_row = jnp.arange(group, dtype=jnp.int32) >= planes
    col = jnp.arange(2 * GB, dtype=jnp.int32)
    imag_col = col >= GB
    freq = col % GB - GB // 2
    quarter = jnp.where(
        imag_row[:, None] == imag_col[None, :], 0, jnp.where(imag_col[None, :], N // 4, 3 * N // 4)
    )
    turns = jnp.mod(freq * jnp.maximum(held, 0)[..., None] + quarter, N)
    table = jnp.cos(turns.astype(jnp.float32) * (2.0 * math.pi / N))
    table = table * (held >= 0).astype(jnp.float32)[..., None]
    return table.reshape(chunks * ranks * group, 2 * GB).astype(jnp.bfloat16)


def lane_group(rows, dtype):
    group = lax.broadcasted_iota(jnp.int32, (rows, LANES), 1) // 32
    return [(group == g).astype(jnp.float32).astype(dtype) for g in range(GROUPS + 1)]


def stick_kernel(bands, chunks, ranks, planes, group, span, coef, tab, info, *refs):
    outs, (main, rest) = refs[:chunks], refs[chunks:]
    live = 2 * planes * bands
    rows = GROUPS * span
    if live < rows:
        main[...] = jnp.zeros_like(main)
        rest[...] = jnp.zeros_like(rest)
    table = tab[...]
    for b in range(bands):
        x = coef[b]
        x = jnp.concatenate([x[:LANES]] + [x[LANES:]] * 4, axis=0)
        val = lax.dot_general(
            table, x, (((1,), (1,)), ((), ())), preferred_element_type=jnp.float32
        )
        for i in range(chunks * ranks):
            part = val[i * group : i * group + 2 * planes]
            main[i, pl.ds(b, 2 * planes, stride=bands), :] = part[:, :LANES]
            rest[i, pl.ds(b, 2 * planes, stride=bands), :] = part[:, LANES:]
    masks = lane_group(span, jnp.float32)
    for i in range(chunks * ranks):
        c, d = divmod(i, ranks)
        outs[c][d, :rows, :] = main[i].astype(jnp.bfloat16)
        packed = rest[i, :span, :] * masks[0]
        for g in range(1, GROUPS):
            packed = packed + rest[i, g * span : (g + 1) * span, :] * masks[g]
        at = rows
        if c == 0:
            outs[c][d, rows : rows + INFO, :] = info[:, :LANES].astype(jnp.bfloat16)
            tail_info = jnp.concatenate(
                [info[:, LANES:], jnp.zeros((span - INFO, LANES), jnp.float32)], axis=0
            )
            packed = packed + tail_info * masks[GROUPS]
            at = rows + INFO
        outs[c][d, at : at + span, :] = packed.astype(jnp.bfloat16)


def plane_kernel(first, bands, ranks, planes, span, owners, own_rows, *refs):
    if first:
        recv, row_tab, col_tab, weight, dens, turn, gx_of, gy_hot = refs[:8]
        scratch = refs[8:]
    else:
        recv, row_tab, col_tab, weight, turn, gx_of, gy_hot, dens = refs[:8]
        scratch = refs[8:]
    lhs, pick, sticks, real, imag, half, tail, acc, acc_tail = scratch
    rows = GROUPS * span
    total = rows + INFO if first else rows
    live = planes * bands
    cap = turn.shape[1]

    if first:
        place = lax.broadcasted_iota(jnp.int32, (1, cap), 1).astype(jnp.float32)
        start = jnp.zeros((1, 1), jnp.float32)
        for src in range(ranks):
            count = recv[src, rows : rows + INFO, :].astype(jnp.float32)[2:3, 0:1]
            t = place - start
            turn[src : src + 1, :] = jnp.where(jnp.logical_and(t >= 0, t < count), t, -1.0)
            start = start + count

    masks = lane_group(span, jnp.bfloat16)
    k = lax.broadcasted_iota(jnp.int32, (2 * LANES, cap), 0)
    slot = jnp.where(k < LANES, k, LANES + k % 32).astype(jnp.float32)
    for src in range(ranks):
        at = src * 2 * LANES
        pick[at : at + 2 * LANES, :] = jnp.where(slot == turn[src : src + 1, :], 1.0, 0.0).astype(
            jnp.bfloat16
        )
        packed = recv[src, total : total + span, :]
        pieces = [packed * masks[g] for g in range(GROUPS)]
        if first:
            pieces.append((packed * masks[GROUPS])[:INFO])
        lhs[:, at : at + LANES] = recv[src, :total, :]
        lhs[:, at + LANES : at + 2 * LANES] = jnp.concatenate(pieces, axis=0)
    compact = jnp.dot(lhs[...], pick[...], preferred_element_type=jnp.float32)
    sticks[...] = compact[:rows].astype(jnp.bfloat16)

    if first:
        info = jnp.concatenate(
            [compact[rows:], jnp.zeros((LANES - INFO, cap), jnp.float32)], axis=0
        ).T
        lane = lax.broadcasted_iota(jnp.int32, (cap, LANES), 1).astype(jnp.float32)
        gx_of[...] = jnp.broadcast_to(info[:, 0:1], (cap, LANES)).astype(jnp.bfloat16)
        gy_hot[...] = jnp.where(info[:, 1:2] == lane, 1.0, 0.0).astype(jnp.bfloat16)

    def put(pair, carry):
        hot = []
        for side in range(2):
            gx = (2 * pair + side).astype(jnp.float32).astype(jnp.bfloat16)
            hot.append(jnp.where(gx_of[...] == gx, gy_hot[...], jnp.zeros((), jnp.bfloat16)))
        placed = jnp.dot(
            sticks[...], jnp.concatenate(hot, axis=1), preferred_element_type=jnp.float32
        )
        for side in range(2):
            lanes = slice(side * LANES, (side + 1) * LANES)
            real[pl.ds(2 * pair + side, live, stride=GB), :] = placed[:live, lanes]
            imag[pl.ds(2 * pair + side, live, stride=GB), :] = placed[live : 2 * live, lanes]
        return carry

    lax.fori_loop(0, GB // 2, put, 0)

    tail[...] = jnp.zeros_like(tail)
    acc[...] = jnp.zeros_like(acc)
    acc_tail[...] = jnp.zeros_like(acc_tail)

    def rows_of(j, carry):
        at = pl.ds(pl.multiple_of(j * (bands * GB), 8), bands * GB)
        both = jnp.concatenate(
            [real[at, :].astype(jnp.bfloat16), imag[at, :].astype(jnp.bfloat16)], axis=1
        )
        h = jnp.dot(both, row_tab[...], preferred_element_type=jnp.float32)
        for b in range(bands):
            piece = h[b * GB : (b + 1) * GB]
            half[j, b] = jnp.concatenate(
                [piece[:, :LANES], piece[:, LANES : 2 * LANES]], axis=0
            ).astype(jnp.bfloat16)
            end = jnp.concatenate(
                [piece[:, 2 * LANES : 3 * LANES], piece[:, 3 * LANES :]], axis=0
            )
            tail[b] = tail[b] + pltpu.roll(end, TAIL * j, 1)
        return carry

    lax.fori_loop(0, planes, rows_of, 0)

    def columns_of(b, carry):
        w = weight[b]

        def square(x):
            wave = jnp.dot(col_tab[...], x, preferred_element_type=jnp.float32)
            a, c = wave[:N], wave[N:]
            return (a * a + c * c) * w

        for j in range(0, planes, 2):
            if j + 1 < planes:
                sq = square(jnp.concatenate([half[j, b], half[j + 1, b]], axis=1))
                acc[j] = acc[j] + sq[:, :LANES]
                acc[j + 1] = acc[j + 1] + sq[:, LANES:]
            else:
                acc[j] = acc[j] + square(half[j, b])
        acc_tail[...] = acc_tail[...] + square(tail[b].astype(jnp.bfloat16))
        return carry

    lax.fori_loop(0, bands, columns_of, 0)

    for o in range(owners):
        mine = slice(o * own_rows, (o + 1) * own_rows)
        for j in range(planes):
            dens[o, j, :own_rows, :] = acc[j, mine, :].astype(jnp.bfloat16)
        dens[o, planes, :own_rows, :] = acc_tail[mine, :].astype(jnp.bfloat16)


def sum_kernel(chunks, owners, planes, own_rows, *refs):
    parts, out = refs[:chunks], refs[chunks]
    for c in range(chunks):
        total = parts[c][0].astype(jnp.float32)
        for o in range(1, owners):
            total = total + parts[c][o].astype(jnp.float32)
        for j in range(planes):
            out[c * planes + j, :, :LANES] = total[j, :own_rows]
            out[c * planes + j, :, LANES:] = total[planes, :own_rows, j * TAIL : (j + 1) * TAIL]


def up(n, m):
    return -(-n // m) * m


def vmem_call(kernel, out_shape, n_in, scratch=(), flops=1, smem=()):
    vmem = pl.BlockSpec(memory_space=pltpu.VMEM)
    scalar = pl.BlockSpec(memory_space=pltpu.SMEM)
    many = isinstance(out_shape, list)
    return pl.pallas_call(
        kernel,
        out_shape=out_shape,
        in_specs=[scalar if i in smem else vmem for i in range(n_in)],
        out_specs=[vmem] * len(out_shape) if many else vmem,
        scratch_shapes=list(scratch),
        compiler_params=pltpu.CompilerParams(vmem_limit_bytes=60 * 2**20),
        cost_estimate=pl.CostEstimate(flops=flops, bytes_accessed=1 << 20, transcendentals=0),
    )


def shards(coefficients, occupations, columns, counts, plane_slot):
    bands = coefficients.shape[0]
    ranks = lax.axis_size("fft")
    owners = lax.axis_size("band")
    slots = columns.shape[0]
    held = plane_slot.shape[0] // ranks
    chunks = next(c for c in range(1, held + 1) if held % c == 0 and held // c * TAIL <= LANES)
    planes = held // chunks
    group = up(2 * planes, 16)
    span = up(-(-2 * planes * bands // GROUPS), 16)
    rows = GROUPS * span
    cap = up(ranks * slots * 2 // 5, LANES)
    own_rows = N // owners
    bf16, f32 = jnp.bfloat16, jnp.float32

    coef = coefficients.reshape(bands, slots, 2 * GB)
    table = plane_table(plane_slot, chunks, ranks, group)
    spread = jnp.concatenate([columns[:LANES]] + [columns[LANES:]] * 4)
    row = jnp.arange(INFO, dtype=jnp.int32)[:, None]
    info = jnp.where(
        row == 0, spread // GB, jnp.where(row == 1, spread % GB, jnp.where(row == 2, counts[0], 0))
    ).astype(f32)
    weight = occupations / (bands * owners)
    row_tab, col_tab = wave_tables()

    shapes = [
        jax.ShapeDtypeStruct((ranks, rows + span + (INFO if c == 0 else 0), LANES), bf16)
        for c in range(chunks)
    ]
    outgoing = vmem_call(
        functools.partial(stick_kernel, bands, chunks, ranks, planes, group, span),
        shapes,
        3,
        [pltpu.VMEM((chunks * ranks, rows, LANES), f32)] * 2,
        flops=4 * 10**9,
    )(coef, table, info)
    dens_shape = jax.ShapeDtypeStruct((owners, planes + 1, up(own_rows, 8), LANES), bf16)
    kept_shapes = [
        jax.ShapeDtypeStruct((ranks, cap), f32),
        jax.ShapeDtypeStruct((cap, LANES), bf16),
        jax.ShapeDtypeStruct((cap, LANES), bf16),
    ]
    kept, summed = [], []
    for c in range(chunks):
        first = c == 0
        received = lax.all_to_all(outgoing[c], "fft", split_axis=0, concat_axis=0, tiled=True)
        total = rows + (INFO if first else 0)
        results = vmem_call(
            functools.partial(plane_kernel, first, bands, ranks, planes, span, owners, own_rows),
            [dens_shape] + (kept_shapes if first else []),
            4 if first else 7,
            [
                pltpu.VMEM((total, ranks * 2 * LANES), bf16),
                pltpu.VMEM((ranks * 2 * LANES, cap), bf16),
                pltpu.VMEM((rows, cap), bf16),
                pltpu.VMEM((planes * bands * GB, LANES), f32),
                pltpu.VMEM((planes * bands * GB, LANES), f32),
                pltpu.VMEM((planes, bands, 2 * GB, LANES), bf16),
                pltpu.VMEM((bands, 2 * GB, LANES), f32),
                pltpu.VMEM((planes, N, LANES), f32),
                pltpu.VMEM((N, LANES), f32),
            ],
            flops=16 * 10**9,
            smem=(3,),
        )(received, row_tab, col_tab, weight, *kept)
        if first:
            kept = list(results[1:])
        summed.append(
            lax.all_to_all(results[0], "band", split_axis=0, concat_axis=0, tiled=True)
        )
    return vmem_call(
        functools.partial(sum_kernel, chunks, owners, planes, own_rows),
        jax.ShapeDtypeStruct((held, own_rows, N), f32),
        chunks,
    )(*summed)


def solution(mesh):
    placed = (P("band", "fft"), P("band"), P("fft"), P("fft"), P())
    return jax.shard_map(
        shards, mesh=mesh, in_specs=placed, out_specs=P("fft", "band", None), check_vma=False
    )
```

time: 327 us -> 120 us (0.37)
  matrix products: 88.1 us -> 0 us
  other arithmetic: 79.7 us -> 3.87 us
  Pallas kernels: 0 us -> 56.1 us
  local copies, waits for them, and re-layouts: 58.4 us -> 6.16 us
  waiting for transfers between devices: 37.5 us -> 11.8 us
  blocking collectives: 38.7 us -> 19.9 us
  between operations: 15.5 us -> 0.75 us
  starting transfers between devices: 7.35 us -> 20.5 us
    dot_general x4 -> x0, matrix products: 88.1 us -> none  [the longest x1 41.5 us: grid_squares(): jnp.dot(row_pick.T, weighted.reshape(slot_total, flat_rows * GB), preferr...]
    pallas_call x0 -> x5, Pallas kernels: none -> 56.1 us  [the longest x3 50.7 us: shards(): vmem_call(functools.partial(plane_kernel, first, bands, ranks, planes, sp...]
    add x1 -> x0, other arithmetic: 46.4 us -> none  [grid_squares(): return real_part * real_part + imag_part * imag_part]
    unnamed x1 -> x0, blocking collectives: 38.7 us -> none
    unnamed x2 -> x0, waiting for transfers between devices: 37.5 us -> none
    add x1 -> x0, local copies, waits for them, and re-layouts: 34 us -> none  [grid_squares(): return real_part * real_part + imag_part * imag_part]
    mul x1 -> x0, other arithmetic: 26.9 us -> none  [grid_squares(): weighted = by_slot[:, :, None] * col_pick[:, None, :]]
    all_to_all x0 -> x2, blocking collectives: none -> 19.9 us  [shards(): lax.all_to_all(results[0], 'band', split_axis=0, concat_axis=0, tiled=True)]
  transfers between devices with their start and end apart: 2 -> 4, of which waited for: 1 -> 1; matrix products, arithmetic and copies ran while one was open for 1% -> 0% of each run, Pallas kernels for 0% -> 43%
where the time goes in v1:
time: 120 us; the launch traced here: 119 us
  Pallas kernels  56.1 us (47%)
  starting transfers between devices  20.5 us (17%)
  blocking collectives  19.9 us (17%)
  waiting for transfers between devices  11.8 us (10%)
  local copies, waits for them, and re-layouts  6.16 us (5%)
  other arithmetic  3.87 us (3%)
    pallas_call x3, Pallas kernels, shards(): vmem_call(functools.partial(plane_kernel, first, bands, ranks, planes, sp...  50.7 us
    all_to_all x2, blocking collectives, shards(): lax.all_to_all(results[0], 'band', split_axis=0, concat_axis=0, tiled=True)  19.9 us
    all_to_all x3, starting transfers between devices, shards(): lax.all_to_all(outgoing[c], 'fft', split_axis=0, concat_axis=0, tiled=True)  17.1 us
    all_to_all x3, waiting for transfers between devices, shards(): lax.all_to_all(outgoing[c], 'fft', split_axis=0, concat_axis=0, tiled=True)  11.8 us
    reshape x1, local copies, waits for them, and re-layouts, shards(): coef = coefficients.reshape(bands, slots, 2 * GB)  3.77 us
    all_to_all x1, starting transfers between devices, shards(): lax.all_to_all(results[0], 'band', split_axis=0, concat_axis=0, tiled=True)  3.46 us
    pallas_call x1, Pallas kernels, shards(): vmem_call(functools.partial(stick_kernel, bands, chunks, ranks, planes, g...  3.18 us
  transfers between devices with their start and end apart: 4, of which 1 were waited for; matrix products, arithmetic and copies ran while one was open for 0% of the time, Pallas kernels for 43%

profile of v1, /device:TPU:0, one launch (start us, length us, event | category | flops | bytes accessed | tf_op | source)
XLA Modules:
  0.0 119.2 jit_solution(7565882734655375019)
XLA Ops:
  0.0 0.8 reshape.131
  0.8 0.1 pad.6.clone
  0.9 0.1 fusion.9
  1.0 0.1 compare_convert_fusion
  1.1 0.1 max.11
  1.2 0.0 copy-start.5
  1.2 0.1 reshape.132
  1.2 0.6 copy-done.5
  1.9 0.1 and_select_fusion.1
  2.6 3.8 %reshape.130.coef = bf16[12,160,144]{2,1,0:T(8,128)(2,1)} reshape(bf16[12,23040]{1,0:T(8,128)(2,1)} %param.7) | data formatting | bytes 1105920 | tf_op jit(solution)/shard_map/reshape | solution.py:253
  6.4 0.1 compare_select_fusion
  6.5 2.3 %fusion.4.tab = bf16[384,144]{1,0:T(8,128)(2,1)} fusion(f32[384]{0:T(512)S(1)} %reshape.132, s32[16,144]{1,0:T(8,128)S(1)} %compare_select_fusion, s32[384]{0:T(512)S(1)} %max.11, s32[144]{0:T(256)S(1)} %fusion.10), kind=kLoop, calls=%fused_computation.5 | loop fusion | flops 663552 | bytes 123456 | tf_op jit(solution)/shard_map/convert_element_type | solution.py:51
  8.8 0.7 select_convert_fusion.info
  9.4 3.2 %shard_map.73 = (bf16[8,208,128]{2,1,0:T(8,128)(2,1)}, bf16[8,192,128]{2,1,0:T(8,128)(2,1)}, bf16[8,192,128]{2,1,0:T(8,128)(2,1)}) custom-call(bf16[12,160,144]{2,1,0:T(8,128)(2,1)} %reshape.130.coef, bf16[384,144]{1,0:T(8,128)(2,1)} %fusion.4.tab, f32[16,256]{1,0:T(8,128)} %select_convert_fusion.info), custom_call_target="tpu_custom_call" | custom-call | flops 4000000000 | bytes 1048576 | tf_op jit(solution)/shard_map/pallas_call | solution.py:267
  12.6 0.0 copy-start.6
  12.6 7.4 %all-to-all-start = ((bf16[8,208,128]{2,1,0:T(8,128)(2,1)}), bf16[8,208,128]{2,1,0:T(8,128)(2,1)S(1)}, u32[]{:S(2)}, u32[]{:S(2)}) async-start(bf16[8,208,128]{2,1,0:T(8,128)(2,1)} %get-tuple-element.12), calls=%async_computation | async-start | bytes 851968 | tf_op jit(solution)/shard_map/all_to_all | solution.py:283
  20.1 0.0 copy-done.6
  20.1 0.5 broadcast_multiply_fusion.refs_3_
  20.6 11.8 %all-to-all-done.refs_0_ = bf16[8,208,128]{2,1,0:T(8,128)(2,1)S(1)} async-done(((bf16[8,208,128]{2,1,0:T(8,128)(2,1)}), bf16[8,208,128]{2,1,0:T(8,128)(2,1)S(1)}, u32[]{:S(2)}, u32[]{:S(2)}) %all-to-all-start) | async-done | bytes 426016 | tf_op jit(solution)/shard_map/all_to_all | solution.py:283
  32.4 0.0 copy-start.1
  32.4 3.6 %all-to-all-start.4 = ((bf16[8,192,128]{2,1,0:T(8,128)(2,1)}), bf16[8,192,128]{2,1,0:T(8,128)(2,1)S(1)}, u32[]{:S(2)}, u32[]{:S(2)}) async-start(bf16[8,192,128]{2,1,0:T(8,128)(2,1)} %get-tuple-element.18), calls=%async_computation.4 | async-start | bytes 786432 | tf_op jit(solution)/shard_map/all_to_all | solution.py:283
  36.1 0.0 copy-done.1
  36.1 17.3 %shard_map.74 = (bf16[4,7,40,128]{3,2,1,0:T(8,128)(2,1)}, f32[8,512]{1,0:T(8,128)}, bf16[512,128]{1,0:T(8,128)(2,1)}, bf16[512,128]{1,0:T(8,128)(2,1)}) custom-call(bf16[8,208,128]{2,1,0:T(8,128)(2,1)} %copy-done.1, bf16[256,512]{1,0:T(8,128)(2,1)} %constant.63.clone.refs_1_, bf16[288,144]{1,0:T(8,128)(2,1)} %constant.64.clone.refs_2_, ...), custom_call_target="tpu_custom_call" | custom-call | flops 16000000000 | bytes 1048576 | tf_op jit(solution)/shard_map/pallas_call | solution.py:285
  53.4 0.0 all-to-all-done.4.refs_0_
  53.4 0.0 copy-start.3
  53.4 0.7 copy-done.3
  54.1 6.0 %all-to-all-start.2 = ((bf16[8,192,128]{2,1,0:T(8,128)(2,1)}), bf16[8,192,128]{2,1,0:T(8,128)(2,1)S(1)}, u32[]{:S(2)}, u32[]{:S(2)}) async-start(bf16[8,192,128]{2,1,0:T(8,128)(2,1)} %get-tuple-element.14), calls=%async_computation.2 | async-start | bytes 786432 | tf_op jit(solution)/shard_map/all_to_all | solution.py:283
  60.1 16.6 %shard_map.76 = bf16[4,7,40,128]{3,2,1,0:T(8,128)(2,1)} custom-call(bf16[8,192,128]{2,1,0:T(8,128)(2,1)} %copy-done.3, bf16[256,512]{1,0:T(8,128)(2,1)} %constant.63.clone.refs_1_, bf16[288,144]{1,0:T(8,128)(2,1)} %constant.64.clone.refs_2_, f32[12]{0:T(128)} %broadcast_multiply_fusion.refs_3_, f32[8,512]{1,0:T(8,128)} %get-tuple-element.15.refs_4_, ...), custom_call_target="tpu_custom_call" | custom-call | flops 16000000000 | bytes 1048576 | tf_op jit(solution)/shard_map/pallas_call | solution.py:285
  76.7 0.0 all-to-all-done.2.refs_0_
  76.7 0.0 copy-start.2
  76.7 3.5 %all-to-all-start.5 = ((bf16[4,7,40,128]{3,2,1,0:T(8,128)(2,1)}), bf16[4,7,40,128]{3,2,1,0:T(8,128)(2,1)S(1)}, u32[]{:S(2)}, u32[]{:S(2)}) async-start(bf16[4,7,40,128]{3,2,1,0:T(8,128)(2,1)} %shard_map.76), calls=%async_computation.5 | async-start | bytes 573440 | tf_op jit(solution)/shard_map/all_to_all | solution.py:306
  80.1 0.0 copy-done.2
  80.2 16.9 %shard_map.75 = bf16[4,7,40,128]{3,2,1,0:T(8,128)(2,1)} custom-call(bf16[8,192,128]{2,1,0:T(8,128)(2,1)} %copy-done.2, bf16[256,512]{1,0:T(8,128)(2,1)} %constant.63.clone.refs_1_, bf16[288,144]{1,0:T(8,128)(2,1)} %constant.64.clone.refs_2_, f32[12]{0:T(128)} %broadcast_multiply_fusion.refs_3_, f32[8,512]{1,0:T(8,128)} %get-tuple-element.15.refs_4_, ...), custom_call_target="tpu_custom_call" | custom-call | flops 16000000000 | bytes 1048576 | tf_op jit(solution)/shard_map/pallas_call | solution.py:285
  97.0 0.0 copy-start.4
  97.0 0.0 all-to-all-done.5.refs_2_
  97.0 0.0 copy-start
  97.0 10.6 %all_to_all.30.refs_1_ = bf16[4,7,40,128]{3,2,1,0:T(8,128)(2,1)} all-to-all(bf16[4,7,40,128]{3,2,1,0:T(8,128)(2,1)} %shard_map.75), channel_id=1, replica_groups=mesh['fft'=8,'band'=4] {'band'}, dimensions={0} | all-to-all | bytes 573440 | tf_op jit(solution)/shard_map/all_to_all | solution.py:306
  107.6 0.0 copy-done
  107.6 0.0 copy-done.4
  107.6 9.3 %all_to_all.31.refs_0_ = bf16[4,7,40,128]{3,2,1,0:T(8,128)(2,1)} all-to-all(bf16[4,7,40,128]{3,2,1,0:T(8,128)(2,1)S(1)} %copy-done.4), channel_id=1, replica_groups=mesh['fft'=8,'band'=4] {'band'}, dimensions={0} | all-to-all | bytes 573440 | tf_op jit(solution)/shard_map/all_to_all | solution.py:306
  117.0 2.2 %shard_map.77 = f32[18,36,144]{2,1,0:T(8,128)} custom-call(bf16[4,7,40,128]{3,2,1,0:T(8,128)(2,1)} %all_to_all.31.refs_0_, bf16[4,7,40,128]{3,2,1,0:T(8,128)(2,1)} %all_to_all.30.refs_1_, bf16[4,7,40,128]{3,2,1,0:T(8,128)(2,1)} %copy-done), custom_call_target="tpu_custom_call" | custom-call | flops 1 | bytes 1048576 | tf_op jit(solution)/shard_map/pallas_call | solution.py:308
  (9 shorter events, 0.0 us)
Async XLA Ops:
  1.2 0.7 copy-start.5
  12.6 7.4 %copy-start.6 = (f32[12]{0:T(128)S(1)}, f32[12]{0:T(128)}, u32[]{:S(2)}) copy-start(f32[12]{0:T(128)} %param.8) | copy-start | bytes 148
  12.6 19.8 %all-to-all-start = ((bf16[8,208,128]{2,1,0:T(8,128)(2,1)}), bf16[8,208,128]{2,1,0:T(8,128)(2,1)S(1)}, u32[]{:S(2)}, u32[]{:S(2)}) async-start(bf16[8,208,128]{2,1,0:T(8,128)(2,1)} %get-tuple-element.12), calls=%async_computation | async-start | bytes 851968 | tf_op jit(solution)/shard_map/all_to_all | solution.py:283
  32.4 3.6 %copy-start.1 = (bf16[8,208,128]{2,1,0:T(8,128)(2,1)}, bf16[8,208,128]{2,1,0:T(8,128)(2,1)S(1)}, u32[]{:S(2)}) copy-start(bf16[8,208,128]{2,1,0:T(8,128)(2,1)S(1)} %all-to-all-done.refs_0_) | copy-start | bytes 1277956
  32.4 20.9 %all-to-all-start.4 = ((bf16[8,192,128]{2,1,0:T(8,128)(2,1)}), bf16[8,192,128]{2,1,0:T(8,128)(2,1)S(1)}, u32[]{:S(2)}, u32[]{:S(2)}) async-start(bf16[8,192,128]{2,1,0:T(8,128)(2,1)} %get-tuple-element.18), calls=%async_computation.4 | async-start | bytes 786432 | tf_op jit(solution)/shard_map/all_to_all | solution.py:283
  53.4 0.7 copy-start.3
  54.1 22.6 %all-to-all-start.2 = ((bf16[8,192,128]{2,1,0:T(8,128)(2,1)}), bf16[8,192,128]{2,1,0:T(8,128)(2,1)S(1)}, u32[]{:S(2)}, u32[]{:S(2)}) async-start(bf16[8,192,128]{2,1,0:T(8,128)(2,1)} %get-tuple-element.14), calls=%async_computation.2 | async-start | bytes 786432 | tf_op jit(solution)/shard_map/all_to_all | solution.py:283
  76.7 3.5 %copy-start.2 = (bf16[8,192,128]{2,1,0:T(8,128)(2,1)}, bf16[8,192,128]{2,1,0:T(8,128)(2,1)S(1)}, u32[]{:S(2)}) copy-start(bf16[8,192,128]{2,1,0:T(8,128)(2,1)S(1)} %all-to-all-done.2.refs_0_) | copy-start | bytes 1179652
  76.7 20.4 %all-to-all-start.5 = ((bf16[4,7,40,128]{3,2,1,0:T(8,128)(2,1)}), bf16[4,7,40,128]{3,2,1,0:T(8,128)(2,1)S(1)}, u32[]{:S(2)}, u32[]{:S(2)}) async-start(bf16[4,7,40,128]{3,2,1,0:T(8,128)(2,1)} %shard_map.76), calls=%async_computation.5 | async-start | bytes 573440 | tf_op jit(solution)/shard_map/all_to_all | solution.py:306
  97.0 10.6 %copy-start.4 = (bf16[4,7,40,128]{3,2,1,0:T(8,128)(2,1)S(1)}, bf16[4,7,40,128]{3,2,1,0:T(8,128)(2,1)}, u32[]{:S(2)}) copy-start(bf16[4,7,40,128]{3,2,1,0:T(8,128)(2,1)} %get-tuple-element.13) | copy-start | bytes 860164
  97.0 10.6 %copy-start = (bf16[4,7,40,128]{3,2,1,0:T(8,128)(2,1)}, bf16[4,7,40,128]{3,2,1,0:T(8,128)(2,1)S(1)}, u32[]{:S(2)}) copy-start(bf16[4,7,40,128]{3,2,1,0:T(8,128)(2,1)S(1)} %all-to-all-done.5.refs_2_) | copy-start | bytes 860164

commit v2 on v1

v2 whole, which is shorter than its diff:
```python
import functools
import math

import jax
import jax.numpy as jnp
import numpy as np
from jax import lax
from jax.experimental import pallas as pl
from jax.experimental.pallas import tpu as pltpu
from jax.sharding import PartitionSpec as P

N = 144
GB = 72
LANES = 128
TAIL = N - LANES
SHARE = LANES // TAIL
PAIRS = 4
INFO = 16
GROUPS = 3


def wave_tables():
    freqs = np.arange(GB) - GB // 2
    angles = (freqs[:, None] * np.arange(N)[None, :] % N) * (2.0 * math.pi / N)
    cosine, sine = np.cos(angles), np.sin(angles)
    rows = np.zeros((2 * LANES, 2 * LANES), np.float32)
    ends = np.zeros((SHARE, 2 * LANES, 2 * LANES), np.float32)
    for col, real_from, imag_from in ((0, cosine, -sine), (1, sine, cosine)):
        rows[:GB, col * LANES : (col + 1) * LANES] = real_from[:, :LANES]
        rows[LANES : LANES + GB, col * LANES : (col + 1) * LANES] = imag_from[:, :LANES]
        for j in range(SHARE):
            at = col * LANES + j * TAIL
            ends[j, :GB, at : at + TAIL] = real_from[:, LANES:]
            ends[j, LANES : LANES + GB, at : at + TAIL] = imag_from[:, LANES:]
    cols = np.block([[cosine.T, -sine.T], [sine.T, cosine.T]])
    ends = ends.reshape(SHARE * 2 * LANES, 2 * LANES)
    return [jnp.asarray(x, jnp.bfloat16) for x in (rows, ends, cols)]


def plane_table(plane_slot, planes, ranks):
    held = plane_slot.reshape(ranks, -1)
    rows, imag_rows, base = [], [], 0
    for count in planes:
        group = up(2 * count, 16)
        part = held[:, base : base + count]
        empty = jnp.full((ranks, group - 2 * count), -1, jnp.int32)
        rows.append(jnp.concatenate([part, part, empty], axis=1).reshape(-1))
        imag_rows.append(np.tile(np.arange(group) >= count, ranks))
        base += count
    held = jnp.concatenate(rows)[:, None]
    imag_row = np.concatenate(imag_rows)[:, None]
    col = np.arange(2 * GB)
    imag_col = (col >= GB)[None, :]
    freq = col % GB - GB // 2
    quarter = np.where(imag_row == imag_col, 0, np.where(imag_col, N // 4, 3 * N // 4))
    turns = jnp.mod(freq * jnp.maximum(held, 0) + quarter.astype(np.int32), N)
    table = jnp.cos(turns.astype(jnp.float32) * (2.0 * math.pi / N))
    return jnp.where(held >= 0, table, 0.0).astype(jnp.bfloat16)


def lane_group(rows, dtype):
    group = lax.broadcasted_iota(jnp.int32, (rows, LANES), 1) // 32
    return [(group == g).astype(jnp.float32).astype(dtype) for g in range(GROUPS + 1)]


def stick_kernel(bands, planes, ranks, coef, tab, info, *refs):
    chunks = len(planes)
    outs, mains, rests = refs[:chunks], refs[chunks : 2 * chunks], refs[2 * chunks :]
    for main, rest, count in zip(mains, rests, planes):
        if 2 * count * bands < main.shape[1]:
            main[...] = jnp.zeros_like(main)
            rest[...] = jnp.zeros_like(rest)
    table = tab[...]
    for b in range(bands):
        x = coef[b]
        x = jnp.concatenate([x[:LANES]] + [x[LANES:]] * 4, axis=0)
        val = lax.dot_general(
            table, x, (((1,), (1,)), ((), ())), preferred_element_type=jnp.float32
        )
        at = 0
        for main, rest, count in zip(mains, rests, planes):
            for d in range(ranks):
                part = val[at : at + 2 * count]
                main[d, pl.ds(b, 2 * count, stride=bands), :] = part[:, :LANES]
                rest[d, pl.ds(b, 2 * count, stride=bands), :] = part[:, LANES:]
                at += up(2 * count, 16)
    for c, (out, main, rest) in enumerate(zip(outs, mains, rests)):
        rows = main.shape[1]
        span = rows // GROUPS
        masks = lane_group(span, jnp.float32)
        at = rows + (INFO if c == 0 else 0)
        for d in range(ranks):
            out[d, :rows, :] = main[d].astype(jnp.bfloat16)
            packed = rest[d, :span, :] * masks[0]
            for g in range(1, GROUPS):
                packed = packed + rest[d, g * span : (g + 1) * span, :] * masks[g]
            if c == 0:
                out[d, rows:at, :] = info[:, :LANES].astype(jnp.bfloat16)
                tail_info = jnp.concatenate(
                    [info[:, LANES:], jnp.zeros((span - INFO, LANES), jnp.float32)], axis=0
                )
                packed = packed + tail_info * masks[GROUPS]
            out[d, at:, :] = packed.astype(jnp.bfloat16)


def plane_kernel(first, bands, ranks, planes, span, owners, own_rows, *refs):
    if first:
        recv, row_tab, end_tab, col_tab, weight, dens, turn, gx_of, gy_hot = refs[:9]
    else:
        recv, row_tab, end_tab, col_tab, weight, turn, gx_of, gy_hot, dens = refs[:9]
    lhs, pick, sticks, real, imag, both, half, tail, acc, acc_tail = refs[9:]
    rows = GROUPS * span
    total = rows + INFO if first else rows
    live = planes * bands
    cap = turn.shape[1]

    if first:
        place = lax.broadcasted_iota(jnp.int32, (1, cap), 1).astype(jnp.float32)
        start = jnp.zeros((1, 1), jnp.float32)
        for src in range(ranks):
            count = recv[src, rows : rows + INFO, :].astype(jnp.float32)[2:3, 0:1]
            t = place - start
            turn[src : src + 1, :] = jnp.where(jnp.logical_and(t >= 0, t < count), t, -1.0)
            start = start + count

    masks = lane_group(span, jnp.bfloat16)
    k = lax.broadcasted_iota(jnp.int32, (2 * LANES, cap), 0)
    slot = jnp.where(k < LANES, k, LANES + k % 32).astype(jnp.float32)
    for src in range(ranks):
        at = src * 2 * LANES
        pick[at : at + 2 * LANES, :] = jnp.where(slot == turn[src : src + 1, :], 1.0, 0.0).astype(
            jnp.bfloat16
        )
        packed = recv[src, total : total + span, :]
        pieces = [packed * masks[g] for g in range(GROUPS)]
        if first:
            pieces.append((packed * masks[GROUPS])[:INFO])
        lhs[:, at : at + LANES] = recv[src, :total, :]
        lhs[:, at + LANES : at + 2 * LANES] = jnp.concatenate(pieces, axis=0)
    compact = jnp.dot(lhs[...], pick[...], preferred_element_type=jnp.float32)
    sticks[...] = compact[:rows].astype(jnp.bfloat16)

    if first:
        info = jnp.concatenate(
            [compact[rows:], jnp.zeros((LANES - INFO, cap), jnp.float32)], axis=0
        ).T
        lane = lax.broadcasted_iota(jnp.int32, (cap, LANES), 1).astype(jnp.float32)
        gx_of[...] = jnp.broadcast_to(info[:, 0:1], (cap, LANES)).astype(jnp.bfloat16)
        gy_hot[...] = jnp.where(info[:, 1:2] == lane, 1.0, 0.0).astype(jnp.bfloat16)

    def put(step, carry):
        for u in range(PAIRS):
            pair = PAIRS * step + u
            hot = []
            for side in range(2):
                gx = (2 * pair + side).astype(jnp.float32).astype(jnp.bfloat16)
                hot.append(jnp.where(gx_of[...] == gx, gy_hot[...], jnp.zeros((), jnp.bfloat16)))
            placed = jnp.dot(
                sticks[...], jnp.concatenate(hot, axis=1), preferred_element_type=jnp.float32
            )
            for side in range(2):
                lanes = slice(side * LANES, (side + 1) * LANES)
                at = 2 * pair + side
                real[pl.ds(at, live, stride=GB), :] = placed[:live, lanes]
                imag[pl.ds(at, live, stride=GB), :] = placed[live : 2 * live, lanes]
        return carry

    lax.fori_loop(0, GB // 2 // PAIRS, put, 0)

    acc[...] = jnp.zeros_like(acc)
    acc_tail[...] = jnp.zeros_like(acc_tail)

    def stacked(piece):
        return jnp.concatenate([piece[:, :LANES], piece[:, LANES:]], axis=0).astype(jnp.bfloat16)

    def rows_of(j, carry):
        at = pl.ds(pl.multiple_of(j * (bands * GB), 8), bands * GB)
        x = jnp.concatenate(
            [real[at, :].astype(jnp.bfloat16), imag[at, :].astype(jnp.bfloat16)], axis=1
        )
        both[j] = x
        h = jnp.dot(x, row_tab[...], preferred_element_type=jnp.float32)
        for b in range(bands):
            half[j, b] = stacked(h[b * GB : (b + 1) * GB])
        return carry

    lax.fori_loop(0, planes, rows_of, 0)

    tails = tail.shape[0]
    for t in range(tails):
        js = range(t * SHARE, min(planes, (t + 1) * SHARE))
        x = jnp.concatenate([both[j] for j in js], axis=1)
        h = jnp.dot(x, end_tab[: len(js) * 2 * LANES, :], preferred_element_type=jnp.float32)
        for b in range(bands):
            tail[t, b] = stacked(h[b * GB : (b + 1) * GB])

    def columns_of(step, carry):
        for u in range(2):
            b = 2 * step + u
            w = weight[b]
            pieces = [(acc, j, half) for j in range(planes)]
            pieces += [(acc_tail, t, tail) for t in range(tails)]
            for i in range(0, len(pieces), 2):
                two = pieces[i : i + 2]
                x = jnp.concatenate([src[j, b] for _, j, src in two], axis=1)
                wave = jnp.dot(col_tab[...], x, preferred_element_type=jnp.float32)
                re, im = wave[:N], wave[N:]
                sq = (re * re + im * im) * w
                for side, (to, j, _) in enumerate(two):
                    to[j] = to[j] + sq[:, side * LANES : (side + 1) * LANES]
        return carry

    lax.fori_loop(0, bands // 2, columns_of, 0)

    for o in range(owners):
        mine = slice(o * own_rows, (o + 1) * own_rows)
        for j in range(planes):
            dens[o, j, :own_rows, :] = acc[j, mine, :].astype(jnp.bfloat16)
        for t in range(tails):
            dens[o, planes + t, :own_rows, :] = acc_tail[t, mine, :].astype(jnp.bfloat16)


def sum_kernel(planes, own_rows, *refs):
    *parts, out = refs
    base = 0
    for c, count in enumerate(planes):
        total = parts[2 * c][...].astype(jnp.float32) + parts[2 * c + 1][...].astype(jnp.float32)
        for j in range(count):
            at = j % SHARE * TAIL
            out[base + j, :, :LANES] = total[j, :own_rows]
            out[base + j, :, LANES:] = total[count + j // SHARE, :own_rows, at : at + TAIL]
        base += count


def up(n, m):
    return -(-n // m) * m


def vmem_call(kernel, out_shape, n_in, scratch=(), flops=1, smem=()):
    vmem = pl.BlockSpec(memory_space=pltpu.VMEM)
    scalar = pl.BlockSpec(memory_space=pltpu.SMEM)
    many = isinstance(out_shape, list)
    return pl.pallas_call(
        kernel,
        out_shape=out_shape,
        in_specs=[scalar if i in smem else vmem for i in range(n_in)],
        out_specs=[vmem] * len(out_shape) if many else vmem,
        scratch_shapes=list(scratch),
        compiler_params=pltpu.CompilerParams(vmem_limit_bytes=60 * 2**20),
        cost_estimate=pl.CostEstimate(flops=flops, bytes_accessed=1 << 20, transcendentals=0),
    )


def halve(whole, axis):
    bit = 0
    while True:
        here = lax.axis_index(axis) >> bit & 1
        pairs = whole.reshape((whole.shape[0] // 2, 2) + whole.shape[1:])
        keep = lax.dynamic_index_in_dim(pairs, here, 1, keepdims=False)
        send = lax.dynamic_index_in_dim(pairs, 1 - here, 1, keepdims=False)
        partners = [(i, i ^ (1 << bit)) for i in range(lax.axis_size(axis))]
        got = lax.ppermute(send, axis, partners)
        if keep.shape[0] == 1:
            return keep[0], got[0]
        whole = (keep.astype(jnp.float32) + got.astype(jnp.float32)).astype(whole.dtype)
        bit += 1


def shards(coefficients, occupations, columns, counts, plane_slot):
    bands = coefficients.shape[0]
    ranks = lax.axis_size("fft")
    owners = lax.axis_size("band")
    slots = columns.shape[0]
    held = plane_slot.shape[0] // ranks
    planes = (held - held // 3, held // 3)
    cap = up(ranks * slots * 2 // 5, LANES)
    own_rows = N // owners
    bf16, f32 = jnp.bfloat16, jnp.float32

    coef = coefficients.reshape(bands, slots, 2 * GB)
    table = plane_table(plane_slot, planes, ranks)
    spread = jnp.concatenate([columns[:LANES]] + [columns[LANES:]] * 4)
    row = jnp.arange(INFO, dtype=jnp.int32)[:, None]
    info = jnp.where(
        row == 0, spread // GB, jnp.where(row == 1, spread % GB, jnp.where(row == 2, counts[0], 0))
    ).astype(f32)
    weight = occupations / (bands * owners)
    tables = wave_tables()

    spans = [up(-(-2 * count * bands // GROUPS), 16) for count in planes]
    outgoing = vmem_call(
        functools.partial(stick_kernel, bands, planes, ranks),
        [
            jax.ShapeDtypeStruct((ranks, 4 * span + (INFO if c == 0 else 0), LANES), bf16)
            for c, span in enumerate(spans)
        ],
        3,
        [pltpu.VMEM((ranks, GROUPS * span, LANES), f32) for span in spans * 2],
        flops=4 * 10**9,
    )(coef, table, info)
    kept_shapes = [
        jax.ShapeDtypeStruct((ranks, cap), f32),
        jax.ShapeDtypeStruct((cap, LANES), bf16),
        jax.ShapeDtypeStruct((cap, LANES), bf16),
    ]
    kept, halves = [], []
    for c, (count, span) in enumerate(zip(planes, spans)):
        first = c == 0
        received = lax.all_to_all(outgoing[c], "fft", split_axis=0, concat_axis=0, tiled=True)
        rows = GROUPS * span
        tails = -(-count // SHARE)
        dens_shape = jax.ShapeDtypeStruct((owners, count + tails, up(own_rows, 8), LANES), bf16)
        results = vmem_call(
            functools.partial(plane_kernel, first, bands, ranks, count, span, owners, own_rows),
            [dens_shape] + (kept_shapes if first else []),
            5 if first else 8,
            [
                pltpu.VMEM((rows + (INFO if first else 0), ranks * 2 * LANES), bf16),
                pltpu.VMEM((ranks * 2 * LANES, cap), bf16),
                pltpu.VMEM((rows, cap), bf16),
                pltpu.VMEM((count * bands * GB, LANES), f32),
                pltpu.VMEM((count * bands * GB, LANES), f32),
                pltpu.VMEM((count, bands * GB, 2 * LANES), bf16),
                pltpu.VMEM((count, bands, 2 * GB, LANES), bf16),
                pltpu.VMEM((tails, bands, 2 * GB, LANES), bf16),
                pltpu.VMEM((count, N, LANES), f32),
                pltpu.VMEM((tails, N, LANES), f32),
            ],
            flops=16 * 10**9,
            smem=(4,),
        )(received, *tables, weight, *kept)
        if first:
            kept = list(results[1:])
        halves += halve(results[0], "band")
    return vmem_call(
        functools.partial(sum_kernel, planes, own_rows),
        jax.ShapeDtypeStruct((held, own_rows, N), f32),
        len(halves),
    )(*halves)


def solution(mesh):
    placed = (P("band", "fft"), P("band"), P("fft"), P("fft"), P())
    return jax.shard_map(
        shards, mesh=mesh, in_specs=placed, out_specs=P("fft", "band", None), check_vma=False
    )
```

time: 120 us -> 89.2 us (0.74)
  Pallas kernels: 56.1 us -> 34.5 us
  blocking collectives: 19.9 us -> 0 us
  waiting for transfers between devices: 11.8 us -> 25.7 us
  starting transfers between devices: 20.5 us -> 13.5 us
  local copies, waits for them, and re-layouts: 6.16 us -> 10.1 us
    pallas_call x5 -> x4, Pallas kernels: 56.1 us -> 34.5 us  [the longest x2 29.2 us: shards(): vmem_call(functools.partial(plane_kernel, first, bands, ranks, count, spa...]
    all_to_all x2 -> x0, blocking collectives: 19.9 us -> none  [shards(): lax.all_to_all(results[0], 'band', split_axis=0, concat_axis=0, tiled=True)]
    all_to_all x3 -> x2, waiting for transfers between devices: 11.8 us -> 19.7 us  [shards(): lax.all_to_all(outgoing[c], 'fft', split_axis=0, concat_axis=0, tiled=True)]
    all_to_all x3 -> x2, starting transfers between devices: 17.1 us -> 10.9 us  [shards(): lax.all_to_all(outgoing[c], 'fft', split_axis=0, concat_axis=0, tiled=True)]
    ppermute x0 -> x4, waiting for transfers between devices: none -> 6.06 us  [halve(): got = lax.ppermute(send, axis, partners)]
    all_to_all x1 -> x0, starting transfers between devices: 3.46 us -> none  [shards(): lax.all_to_all(results[0], 'band', split_axis=0, concat_axis=0, tiled=True)]
    ppermute x0 -> x4, starting transfers between devices: none -> 2.62 us  [halve(): got = lax.ppermute(send, axis, partners)]
    squeeze x0 -> x4, local copies, waits for them, and re-layouts: none -> 2.28 us  [halve(): send = lax.dynamic_index_in_dim(pairs, 1 - here, 1, keepdims=False)]
  transfers between devices with their start and end apart: 4 -> 6, of which waited for: 1 -> 4; matrix products, arithmetic and copies ran while one was open for 0% -> 1% of each run, Pallas kernels for 43% -> 20%
where the time goes in v2:
time: 89.2 us; the launch traced here: 88.7 us
  Pallas kernels  34.5 us (39%)
  waiting for transfers between devices  25.7 us (29%)
  starting transfers between devices  13.5 us (15%)
  local copies, waits for them, and re-layouts  10.1 us (11%)
  other arithmetic  4.14 us (5%)
    pallas_call x2, Pallas kernels, shards(): vmem_call(functools.partial(plane_kernel, first, bands, ranks, count, spa...  29.2 us
    all_to_all x2, waiting for transfers between devices, shards(): lax.all_to_all(outgoing[c], 'fft', split_axis=0, concat_axis=0, tiled=True)  19.7 us
    all_to_all x2, starting transfers between devices, shards(): lax.all_to_all(outgoing[c], 'fft', split_axis=0, concat_axis=0, tiled=True)  10.9 us
    ppermute x4, waiting for transfers between devices, halve(): got = lax.ppermute(send, axis, partners)  6.06 us
    reshape x1, local copies, waits for them, and re-layouts, shards(): coef = coefficients.reshape(bands, slots, 2 * GB)  3.83 us
    unnamed x23, local copies, waits for them, and re-layouts  3.46 us
    pallas_call x1, Pallas kernels, shards(): vmem_call(functools.partial(stick_kernel, bands, planes, ranks), [jax.Sha...  3.23 us
    ppermute x4, starting transfers between devices, halve(): got = lax.ppermute(send, axis, partners)  2.62 us
  transfers between devices with their start and end apart: 6, of which 4 were waited for; matrix products, arithmetic and copies ran while one was open for 1% of the time, Pallas kernels for 20%

profile of v2, /device:TPU:0, one launch (start us, length us, event | category | flops | bytes accessed | tf_op | source)
XLA Modules:
  0.0 88.7 jit_solution(7973126618492416736)
XLA Ops:
  0.0 0.0 copy-start.8
  0.0 0.7 copy-done.8
  0.7 0.1 reshape.85
  0.8 0.1 slice.12
  0.8 0.1 pad.9.clone
  0.9 0.1 add_add_fusion
  1.0 0.1 concatenate.26
  1.1 0.1 pad.6.clone
  1.2 0.1 add_add_fusion.1
  1.2 0.1 concatenate.28
  1.4 0.0 copy-start.9
  1.4 0.7 copy-done.9
  2.0 0.1 and_select_fusion.1
  2.8 0.0 copy-start.3
  2.8 0.0 copy-start.7
  2.8 3.8 %reshape.84.coef = bf16[12,160,144]{2,1,0:T(8,128)(2,1)} reshape(bf16[12,23040]{1,0:T(8,128)(2,1)} %param.10) | data formatting | bytes 1105920 | tf_op jit(solution)/shard_map/reshape | solution.py:280
  6.7 0.0 copy-done.3
  6.7 0.0 copy-done.7
  6.7 2.5 %fusion.5.tab = bf16[384,144]{1,0:T(8,128)(2,1)} fusion(s32[384,144]{1,0:T(8,128)S(1)} %copy-done.3, s32[384]{0:T(512)S(1)} %broadcast_maximum_fusion, s32[144]{0:T(256)S(1)} %copy-done.7, pred[384]{0:T(512)(128)(4,1)S(1)} %broadcast_compare_fusion), kind=kLoop, calls=%fused_computation.7 | loop fusion | flops 663552 | bytes 334272 | tf_op jit(solution)/shard_map/convert_element_type | solution.py:58
  9.2 0.7 select_convert_fusion.info
  9.8 3.2 %shard_map.100 = (bf16[8,400,128]{2,1,0:T(8,128)(2,1)}, bf16[8,192,128]{2,1,0:T(8,128)(2,1)}) custom-call(bf16[12,160,144]{2,1,0:T(8,128)(2,1)} %reshape.84.coef, bf16[384,144]{1,0:T(8,128)(2,1)} %fusion.5.tab, f32[16,256]{1,0:T(8,128)} %select_convert_fusion.info), custom_call_target="tpu_custom_call" | custom-call | flops 4000000000 | bytes 1048576 | tf_op jit(solution)/shard_map/pallas_call | solution.py:291
  13.1 7.3 %all-to-all-start = ((bf16[8,400,128]{2,1,0:T(8,128)(2,1)}), bf16[8,400,128]{2,1,0:T(8,128)(2,1)S(1)}, u32[]{:S(2)}, u32[]{:S(2)}) async-start(bf16[8,400,128]{2,1,0:T(8,128)(2,1)} %get-tuple-element.11), calls=%async_computation | async-start | bytes 1638400 | tf_op jit(solution)/shard_map/all_to_all | solution.py:309
  20.4 0.0 copy-start.10
  20.4 0.7 copy-done.10
  21.0 0.6 broadcast_multiply_fusion.refs_4_
  21.6 19.7 %all-to-all-done.refs_0_ = bf16[8,400,128]{2,1,0:T(8,128)(2,1)S(1)} async-done(((bf16[8,400,128]{2,1,0:T(8,128)(2,1)}), bf16[8,400,128]{2,1,0:T(8,128)(2,1)S(1)}, u32[]{:S(2)}, u32[]{:S(2)}) %all-to-all-start) | async-done | bytes 819232 | tf_op jit(solution)/shard_map/all_to_all | solution.py:309
  41.3 0.0 copy-start
  41.3 3.5 %all-to-all-start.1 = ((bf16[8,192,128]{2,1,0:T(8,128)(2,1)}), bf16[8,192,128]{2,1,0:T(8,128)(2,1)S(1)}, u32[]{:S(2)}, u32[]{:S(2)}) async-start(bf16[8,192,128]{2,1,0:T(8,128)(2,1)} %get-tuple-element.13), calls=%async_computation.1 | async-start | bytes 786432 | tf_op jit(solution)/shard_map/all_to_all | solution.py:309
  44.8 0.0 copy-done
  44.8 17.7 %shard_map.101 = (bf16[4,14,40,128]{3,2,1,0:T(8,128)(2,1)}, f32[8,512]{1,0:T(8,128)}, bf16[512,128]{1,0:T(8,128)(2,1)}, bf16[512,128]{1,0:T(8,128)(2,1)}) custom-call(bf16[8,400,128]{2,1,0:T(8,128)(2,1)} %copy-done, bf16[256,256]{1,0:T(8,128)(2,1)} %constant.90.clone.refs_1_, bf16[2048,256]{1,0:T(8,128)(2,1)} %constant.91.clone.refs_2_, ...), custom_call_target="tpu_custom_call" | custom-call | flops 16000000000 | bytes 1048576 | tf_op jit(solution)/shard_map/pallas_call | solution.py:313
  62.5 0.0 all-to-all-done.1.refs_0_
  62.5 0.0 copy-start.2
  62.5 0.7 copy-done.2
  63.3 0.0 copy-start.1
  63.3 11.5 %shard_map.102 = bf16[4,7,40,128]{3,2,1,0:T(8,128)(2,1)} custom-call(bf16[8,192,128]{2,1,0:T(8,128)(2,1)} %copy-done.2, bf16[256,256]{1,0:T(8,128)(2,1)} %constant.90.clone.refs_1_, bf16[2048,256]{1,0:T(8,128)(2,1)} %constant.91.clone.refs_2_, bf16[288,144]{1,0:T(8,128)(2,1)} %constant.92.clone.refs_3_, f32[12]{0:T(128)} %broadcast_multiply_fusion.refs_4_, ...), custom_call_target="tpu_custom_call" | custom-call | flops 16000000000 | bytes 1048576 | tf_op jit(solution)/shard_map/pallas_call | solution.py:313
  74.8 0.9 %dynamic-slice_bitcast_fusion.1 = bf16[2,7,40,128]{3,2,1,0:T(8,128)(2,1)S(1)} fusion(bf16[2,2,7,40,128]{4,3,2,1,0:T(8,128)(2,1)} %bitcast.27, s32[]{:T(128)S(6)} %select_n.67), kind=kLoop, calls=%fused_computation.15 | loop fusion | bytes 286724 | tf_op jit(solution)/shard_map/jit(dynamic_index_in_dim)/squeeze | solution.py:260
  75.7 0.1 collective-permute-start.2
  75.8 0.0 copy-done.1
  75.8 0.0 copy-start.4
  75.8 0.5 collective-permute-start
  76.4 0.8 collective-permute-done.2
  77.1 0.0 copy-done.4
  77.2 0.4 collective-permute-done
  77.6 0.1 fusion
  77.7 0.7 constant_dynamic-slice_fusion.1
  78.3 1.5 %collective-permute-start.1 = (bf16[1,14,40,128]{3,2,1,0:T(8,128)(2,1)S(1)}, bf16[1,14,40,128]{3,2,1,0:T(8,128)(2,1)S(1)}, u32[]{:S(2)}, u32[]{:S(2)}) collective-permute-start(bf16[1,14,40,128]{3,2,1,0:T(8,128)(2,1)S(1)} %get-tuple-element.17), channel_id=1, source_target_pairs={{0,2},{1,3},{2,0},{3,1},{4,6},{5,7},{6,4},{7,5},{8,10},{9,11},{10,... | collective-permute-start | bytes 430088 | tf_op jit(solution)/shard_map/ppermute | solution.py:262
  79.8 0.6 constant_dynamic-slice_fusion
  80.4 0.6 collective-permute-start.3
  81.0 4.9 %collective-permute-done.3 = bf16[1,7,40,128]{3,2,1,0:T(8,128)(2,1)S(1)} collective-permute-done((bf16[1,7,40,128]{3,2,1,0:T(8,128)(2,1)S(1)}, bf16[1,7,40,128]{3,2,1,0:T(8,128)(2,1)S(1)}, u32[]{:S(2)}, u32[]{:S(2)}) %collective-permute-start.3) | collective-permute-done | bytes 71712 | tf_op jit(solution)/shard_map/ppermute | solution.py:262
  85.9 0.0 copy-start.6
  85.9 0.0 collective-permute-done.1
  85.9 0.0 copy-start.5
  85.9 0.6 copy-done.6
  86.5 0.1 copy-done.5
  86.6 2.1 %shard_map.103 = f32[18,36,144]{2,1,0:T(8,128)} custom-call(bf16[14,40,128]{2,1,0:T(8,128)(2,1)} %get-tuple-element.18.refs_0_, bf16[14,40,128]{2,1,0:T(8,128)(2,1)} %bitcast.29, bf16[7,40,128]{2,1,0:T(8,128)(2,1)} %get-tuple-element.20.refs_2_, bf16[7,40,128]{2,1,0:T(8,128)(2,1)} %bitcast.30), custom_call_target="tpu_custom_call" | custom-call | flops 1 | bytes 1048576 | tf_op jit(solution)/shard_map/pallas_call | solution.py:335
  (12 shorter events, 0.1 us)
Async XLA Ops:
  0.0 0.7 copy-start.8
  1.4 0.7 copy-start.9
  2.8 3.9 %copy-start.3 = (s32[384,144]{1,0:T(8,128)S(1)}, s32[384,144]{1,0:T(8,128)}, u32[]{:S(2)}) copy-start(s32[384,144]{1,0:T(8,128)} %constant.89.clone) | copy-start | bytes 663556
  2.8 3.8 %copy-start.7 = (s32[144]{0:T(256)S(1)}, s32[144]{0:T(256)}, u32[]{:S(2)}) copy-start(s32[144]{0:T(256)} %constant.88.clone) | copy-start | bytes 1732
  13.1 28.2 %all-to-all-start = ((bf16[8,400,128]{2,1,0:T(8,128)(2,1)}), bf16[8,400,128]{2,1,0:T(8,128)(2,1)S(1)}, u32[]{:S(2)}, u32[]{:S(2)}) async-start(bf16[8,400,128]{2,1,0:T(8,128)(2,1)} %get-tuple-element.11), calls=%async_computation | async-start | bytes 1638400 | tf_op jit(solution)/shard_map/all_to_all | solution.py:309
  20.4 0.7 copy-start.10
  41.3 3.6 %copy-start = (bf16[8,400,128]{2,1,0:T(8,128)(2,1)}, bf16[8,400,128]{2,1,0:T(8,128)(2,1)S(1)}, u32[]{:S(2)}) copy-start(bf16[8,400,128]{2,1,0:T(8,128)(2,1)S(1)} %all-to-all-done.refs_0_) | copy-start | bytes 2457604
  41.3 21.2 %all-to-all-start.1 = ((bf16[8,192,128]{2,1,0:T(8,128)(2,1)}), bf16[8,192,128]{2,1,0:T(8,128)(2,1)S(1)}, u32[]{:S(2)}, u32[]{:S(2)}) async-start(bf16[8,192,128]{2,1,0:T(8,128)(2,1)} %get-tuple-element.13), calls=%async_computation.1 | async-start | bytes 786432 | tf_op jit(solution)/shard_map/all_to_all | solution.py:309
  62.5 0.8 copy-start.2
  63.3 12.5 %copy-start.1 = (bf16[4,14,40,128]{3,2,1,0:T(8,128)(2,1)S(1)}, bf16[4,14,40,128]{3,2,1,0:T(8,128)(2,1)}, u32[]{:S(2)}) copy-start(bf16[4,14,40,128]{3,2,1,0:T(8,128)(2,1)} %get-tuple-element.12) | copy-start | bytes 1720324
  75.7 1.4 %collective-permute-start.2 = (bf16[2,7,40,128]{3,2,1,0:T(8,128)(2,1)S(1)}, bf16[2,7,40,128]{3,2,1,0:T(8,128)(2,1)S(1)}, u32[]{:S(2)}, u32[]{:S(2)}) collective-permute-start(bf16[2,7,40,128]{3,2,1,0:T(8,128)(2,1)S(1)} %dynamic-slice_bitcast_fusion.1), channel_id=1, source_target_pairs={{0,1},{1,0},{2,3},{3,2},{4,5},{5,4},{6,7},{7,6},{8,9},{9,8},{10,11... | collective-permute-start | bytes 430088 | tf_op jit(solution)/shard_map/ppermute | solution.py:262
  75.8 1.3 %copy-start.4 = (bf16[4,7,40,128]{3,2,1,0:T(8,128)(2,1)S(1)}, bf16[4,7,40,128]{3,2,1,0:T(8,128)(2,1)}, u32[]{:S(2)}) copy-start(bf16[4,7,40,128]{3,2,1,0:T(8,128)(2,1)} %shard_map.102) | copy-start | bytes 860164
  75.8 1.7 %collective-permute-start = (bf16[2,14,40,128]{3,2,1,0:T(8,128)(2,1)S(1)}, bf16[2,14,40,128]{3,2,1,0:T(8,128)(2,1)S(1)}, u32[]{:S(2)}, u32[]{:S(2)}) collective-permute-start(bf16[2,14,40,128]{3,2,1,0:T(8,128)(2,1)S(1)} %dynamic-slice_bitcast_fusion), channel_id=1, source_target_pairs={{0,1},{1,0},{2,3},{3,2},{4,5},{5,4},{6,7},{7,6},{8,9},{9,8},{10,11... | collective-permute-start | bytes 860168 | tf_op jit(solution)/shard_map/ppermute | solution.py:262
  78.3 7.6 %collective-permute-start.1 = (bf16[1,14,40,128]{3,2,1,0:T(8,128)(2,1)S(1)}, bf16[1,14,40,128]{3,2,1,0:T(8,128)(2,1)S(1)}, u32[]{:S(2)}, u32[]{:S(2)}) collective-permute-start(bf16[1,14,40,128]{3,2,1,0:T(8,128)(2,1)S(1)} %get-tuple-element.17), channel_id=1, source_target_pairs={{0,2},{1,3},{2,0},{3,1},{4,6},{5,7},{6,4},{7,5},{8,10},{9,11},{10,... | collective-permute-start | bytes 430088 | tf_op jit(solution)/shard_map/ppermute | solution.py:262
  80.4 5.5 %collective-permute-start.3 = (bf16[1,7,40,128]{3,2,1,0:T(8,128)(2,1)S(1)}, bf16[1,7,40,128]{3,2,1,0:T(8,128)(2,1)S(1)}, u32[]{:S(2)}, u32[]{:S(2)}) collective-permute-start(bf16[1,7,40,128]{3,2,1,0:T(8,128)(2,1)S(1)} %get-tuple-element.19), channel_id=1, source_target_pairs={{0,2},{1,3},{2,0},{3,1},{4,6},{5,7},{6,4},{7,5},{8,10},{9,11},{10,... | collective-permute-start | bytes 215048 | tf_op jit(solution)/shard_map/ppermute | solution.py:262
  85.9 0.6 copy-start.6
  85.9 0.7 copy-start.5

commit v3 on v2

--- a/solution.py
+++ b/solution.py
@@ -9,12 +9,13 @@
 from jax.experimental.pallas import tpu as pltpu
 from jax.sharding import PartitionSpec as P
 
+
 N = 144
 GB = 72
 LANES = 128
 TAIL = N - LANES
 SHARE = LANES // TAIL
-PAIRS = 4
+PAIRS = 12
 INFO = 16
 GROUPS = 3
 
@@ -41,7 +42,7 @@
     held = plane_slot.reshape(ranks, -1)
     rows, imag_rows, base = [], [], 0
     for count in planes:
-        group = up(2 * count, 16)
+        group = up(2 * count, 8)
         part = held[:, base : base + count]
         empty = jnp.full((ranks, group - 2 * count), -1, jnp.int32)
         rows.append(jnp.concatenate([part, part, empty], axis=1).reshape(-1))
@@ -83,7 +84,7 @@
                 part = val[at : at + 2 * count]
                 main[d, pl.ds(b, 2 * count, stride=bands), :] = part[:, :LANES]
                 rest[d, pl.ds(b, 2 * count, stride=bands), :] = part[:, LANES:]
-                at += up(2 * count, 16)
+                at += up(2 * count, 8)
     for c, (out, main, rest) in enumerate(zip(outs, mains, rests)):
         rows = main.shape[1]
         span = rows // GROUPS
@@ -105,10 +106,10 @@
 
 def plane_kernel(first, bands, ranks, planes, span, owners, own_rows, *refs):
     if first:
-        recv, row_tab, end_tab, col_tab, weight, dens, turn, gx_of, gy_hot = refs[:9]
+        recv, row_tab, end_tab, col_tab, weight, core, keep, send, turn, gx_of, gy_hot = refs[:11]
     else:
-        recv, row_tab, end_tab, col_tab, weight, turn, gx_of, gy_hot, dens = refs[:9]
-    lhs, pick, sticks, real, imag, both, half, tail, acc, acc_tail = refs[9:]
+        recv, row_tab, end_tab, col_tab, weight, core, turn, gx_of, gy_hot, keep, send = refs[:11]
+    lhs, pick, sticks, real, imag, both, half, tail, acc, acc_tail = refs[11:]
     rows = GROUPS * span
     total = rows + INFO if first else rows
     live = planes * bands
@@ -173,18 +174,21 @@
     def stacked(piece):
         return jnp.concatenate([piece[:, :LANES], piece[:, LANES:]], axis=0).astype(jnp.bfloat16)
 
-    def rows_of(j, carry):
-        at = pl.ds(pl.multiple_of(j * (bands * GB), 8), bands * GB)
-        x = jnp.concatenate(
-            [real[at, :].astype(jnp.bfloat16), imag[at, :].astype(jnp.bfloat16)], axis=1
-        )
-        both[j] = x
-        h = jnp.dot(x, row_tab[...], preferred_element_type=jnp.float32)
-        for b in range(bands):
-            half[j, b] = stacked(h[b * GB : (b + 1) * GB])
+    def rows_of(step, carry):
+        for u in range(deep):
+            j = step * deep + u
+            at = pl.ds(pl.multiple_of(j * (bands * GB), 8), bands * GB)
+            x = jnp.concatenate(
+                [real[at, :].astype(jnp.bfloat16), imag[at, :].astype(jnp.bfloat16)], axis=1
+            )
+            both[j] = x
+            h = jnp.dot(x, row_tab[...], preferred_element_type=jnp.float32)
+            for b in range(bands):
+                half[j, b] = stacked(h[b * GB : (b + 1) * GB])
         return carry
 
-    lax.fori_loop(0, planes, rows_of, 0)
+    deep = largest(planes, 3)
+    lax.fori_loop(0, planes // deep, rows_of, 0)
 
     tails = tail.shape[0]
     for t in range(tails):
@@ -194,30 +198,43 @@
         for b in range(bands):
             tail[t, b] = stacked(h[b * GB : (b + 1) * GB])
 
+    wide = largest(bands, 4)
+
     def columns_of(step, carry):
-        for u in range(2):
-            b = 2 * step + u
-            w = weight[b]
-            pieces = [(acc, j, half) for j in range(planes)]
-            pieces += [(acc_tail, t, tail) for t in range(tails)]
-            for i in range(0, len(pieces), 2):
-                two = pieces[i : i + 2]
-                x = jnp.concatenate([src[j, b] for _, j, src in two], axis=1)
-                wave = jnp.dot(col_tab[...], x, preferred_element_type=jnp.float32)
-                re, im = wave[:N], wave[N:]
-                sq = (re * re + im * im) * w
-                for side, (to, j, _) in enumerate(two):
-                    to[j] = to[j] + sq[:, side * LANES : (side + 1) * LANES]
+        pieces = []
+        for u in range(wide):
+            b = wide * step + u
+            pieces += [(acc, j, half, b) for j in range(planes)]
+        for t in range(tails):
+            pieces += [(acc_tail, t, tail, wide * step + u) for u in range(wide)]
+        for i in range(0, len(pieces), 2):
+            two = pieces[i : i + 2]
+            x = jnp.concatenate([src[j, b] for _, j, src, b in two], axis=1)
+            wave = jnp.dot(col_tab[...], x, preferred_element_type=jnp.float32)
+            re, im = wave[:N], wave[N:]
+            sq = re * re + im * im
+            for side, (to, j, _, b) in enumerate(two):
+                to[j] = to[j] + sq[:, side * LANES : (side + 1) * LANES] * weight[b]
         return carry
 
-    lax.fori_loop(0, bands // 2, columns_of, 0)
-
-    for o in range(owners):
-        mine = slice(o * own_rows, (o + 1) * own_rows)
-        for j in range(planes):
-            dens[o, j, :own_rows, :] = acc[j, mine, :].astype(jnp.bfloat16)
-        for t in range(tails):
-            dens[o, planes + t, :own_rows, :] = acc_tail[t, mine, :].astype(jnp.bfloat16)
+    lax.fori_loop(0, bands // wide, columns_of, 0)
+
+    def deal(mine_bit):
+        for o in range(owners):
+            to = keep if o % 2 == mine_bit else send
+            mine = slice(o * own_rows, (o + 1) * own_rows)
+            for j in range(planes):
+                to[o // 2, j, :own_rows, :] = acc[j, mine, :].astype(jnp.bfloat16)
+            for t in range(tails):
+                to[o // 2, planes + t, :own_rows, :] = acc_tail[t, mine, :].astype(jnp.bfloat16)
+
+    @pl.when(core[0] == 0)
+    def _():
+        deal(0)
+
+    @pl.when(core[0] != 0)
+    def _():
+        deal(1)
 
 
 def sum_kernel(planes, own_rows, *refs):
@@ -236,7 +253,12 @@
     return -(-n // m) * m
 
 
+def largest(n, most):
+    return max(d for d in range(1, most + 1) if n % d == 0)
+
+
 def vmem_call(kernel, out_shape, n_in, scratch=(), flops=1, smem=()):
+    used = sum(math.prod(m.shape) * jnp.dtype(m.dtype).itemsize for m in scratch)
     vmem = pl.BlockSpec(memory_space=pltpu.VMEM)
     scalar = pl.BlockSpec(memory_space=pltpu.SMEM)
     many = isinstance(out_shape, list)
@@ -246,24 +268,27 @@
         in_specs=[scalar if i in smem else vmem for i in range(n_in)],
         out_specs=[vmem] * len(out_shape) if many else vmem,
         scratch_shapes=list(scratch),
-        compiler_params=pltpu.CompilerParams(vmem_limit_bytes=60 * 2**20),
+        compiler_params=pltpu.CompilerParams(vmem_limit_bytes=min(63 * 2**20, used + 12 * 2**20)),
         cost_estimate=pl.CostEstimate(flops=flops, bytes_accessed=1 << 20, transcendentals=0),
     )
 
 
-def halve(whole, axis):
+def partners(axis, bit):
+    return [(i, i ^ (1 << bit)) for i in range(lax.axis_size(axis))]
+
+
+def halve(keep, send, axis):
     bit = 0
     while True:
+        got = lax.ppermute(send, axis, partners(axis, bit))
+        if keep.shape[0] == 1:
+            return keep[0], got[0]
+        whole = (keep.astype(jnp.float32) + got.astype(jnp.float32)).astype(keep.dtype)
+        bit += 1
         here = lax.axis_index(axis) >> bit & 1
         pairs = whole.reshape((whole.shape[0] // 2, 2) + whole.shape[1:])
         keep = lax.dynamic_index_in_dim(pairs, here, 1, keepdims=False)
         send = lax.dynamic_index_in_dim(pairs, 1 - here, 1, keepdims=False)
-        partners = [(i, i ^ (1 << bit)) for i in range(lax.axis_size(axis))]
-        got = lax.ppermute(send, axis, partners)
-        if keep.shape[0] == 1:
-            return keep[0], got[0]
-        whole = (keep.astype(jnp.float32) + got.astype(jnp.float32)).astype(whole.dtype)
-        bit += 1
 
 
 def shards(coefficients, occupations, columns, counts, plane_slot):
@@ -272,7 +297,8 @@
     owners = lax.axis_size("band")
     slots = columns.shape[0]
     held = plane_slot.shape[0] // ranks
-    planes = (held - held // 3, held // 3)
+    last = min(SHARE, held // 2)
+    planes = (held - last, last)
     cap = up(ranks * slots * 2 // 5, LANES)
     own_rows = N // owners
     bf16, f32 = jnp.bfloat16, jnp.float32
@@ -285,6 +311,7 @@
         row == 0, spread // GB, jnp.where(row == 1, spread % GB, jnp.where(row == 2, counts[0], 0))
     ).astype(f32)
     weight = occupations / (bands * owners)
+    core = (lax.axis_index("band") & 1)[None]
     tables = wave_tables()
 
     spans = [up(-(-2 * count * bands // GROUPS), 16) for count in planes]
@@ -309,11 +336,13 @@
         received = lax.all_to_all(outgoing[c], "fft", split_axis=0, concat_axis=0, tiled=True)
         rows = GROUPS * span
         tails = -(-count // SHARE)
-        dens_shape = jax.ShapeDtypeStruct((owners, count + tails, up(own_rows, 8), LANES), bf16)
-        results = vmem_call(
+        dens_shape = jax.ShapeDtypeStruct(
+            (owners // 2, count + tails, up(own_rows, 8), LANES), bf16
+        )
+        run = vmem_call(
             functools.partial(plane_kernel, first, bands, ranks, count, span, owners, own_rows),
-            [dens_shape] + (kept_shapes if first else []),
-            5 if first else 8,
+            [dens_shape] * 2 + (kept_shapes if first else []),
+            6 if first else 9,
             [
                 pltpu.VMEM((rows + (INFO if first else 0), ranks * 2 * LANES), bf16),
                 pltpu.VMEM((ranks * 2 * LANES, cap), bf16),
@@ -327,11 +356,12 @@
                 pltpu.VMEM((tails, N, LANES), f32),
             ],
             flops=16 * 10**9,
-            smem=(4,),
-        )(received, *tables, weight, *kept)
+            smem=(4, 5),
+        )
+        results = run(received, *tables, weight, core, *kept)
         if first:
-            kept = list(results[1:])
-        halves += halve(results[0], "band")
+            kept = list(results[2:])
+        halves += halve(results[0], results[1], "band")
     return vmem_call(
         functools.partial(sum_kernel, planes, own_rows),
         jax.ShapeDtypeStruct((held, own_rows, N), f32),
@@ -341,6 +371,7 @@
 
 def solution(mesh):
     placed = (P("band", "fft"), P("band"), P("fft"), P("fft"), P())
+
     return jax.shard_map(
         shards, mesh=mesh, in_specs=placed, out_specs=P("fft", "band", None), check_vma=False
     )

time: 89.2 us -> 73.4 us (0.82)
  Pallas kernels: 34.5 us -> 23.9 us
  local copies, waits for them, and re-layouts: 10.1 us -> 5.33 us
  other arithmetic: 4.14 us -> 2.22 us
  waiting for transfers between devices: 25.7 us -> 26.9 us
    pallas_call x2, Pallas kernels: 29.2 us -> 21 us  [shards(): results = run(received, *tables, weight, core, *kept)]
    squeeze x4 -> x2, local copies, waits for them, and re-layouts: 2.28 us -> 0.06 us  [halve(): send = lax.dynamic_index_in_dim(pairs, 1 - here, 1, keepdims=False)]
    unnamed x23 -> x14, local copies, waits for them, and re-layouts: 3.46 us -> 1.35 us
    pallas_call x1, Pallas kernels: 3.23 us -> 1.86 us  [shards(): vmem_call(functools.partial(stick_kernel, bands, planes, ranks), [jax.Sha...]
    pallas_call x1, Pallas kernels: 2.08 us -> 1.02 us  [shards(): vmem_call(functools.partial(sum_kernel, planes, own_rows), jax.ShapeDtype...]
    reshape x1, local copies, waits for them, and re-layouts: 3.83 us -> 2.85 us  [shards(): coef = coefficients.reshape(bands, slots, 2 * GB)]
    convert_element_type x1, other arithmetic: 2.49 us -> 1.59 us  [plane_table(): return jnp.where(held >= 0, table, 0.0).astype(jnp.bfloat16)]
  transfers between devices with their start and end apart: 6 -> 6, of which waited for: 4 -> 5; matrix products, arithmetic and copies ran while one was open for 1% -> 0% of each run, Pallas kernels for 20% -> 16%
where the time goes in v3:
time: 73.4 us; the launch traced here: 73 us
  waiting for transfers between devices  26.9 us (37%)
  Pallas kernels  23.9 us (33%)
  starting transfers between devices  13.9 us (19%)
  local copies, waits for them, and re-layouts  5.33 us (7%)
  other arithmetic  2.22 us (3%)
  between operations  0.79 us (1%)
    pallas_call x2, Pallas kernels, shards(): results = run(received, *tables, weight, core, *kept)  21 us
    all_to_all x2, waiting for transfers between devices, shards(): lax.all_to_all(outgoing[c], 'fft', split_axis=0, concat_axis=0, tiled=True)  20.3 us
    all_to_all x2, starting transfers between devices, shards(): lax.all_to_all(outgoing[c], 'fft', split_axis=0, concat_axis=0, tiled=True)  11.2 us
    ppermute x4, waiting for transfers between devices, halve(): got = lax.ppermute(send, axis, partners(axis, bit))  6.54 us
    reshape x1, local copies, waits for them, and re-layouts, shards(): coef = coefficients.reshape(bands, slots, 2 * GB)  2.85 us
    ppermute x4, starting transfers between devices, halve(): got = lax.ppermute(send, axis, partners(axis, bit))  2.73 us
    pallas_call x1, Pallas kernels, shards(): vmem_call(functools.partial(stick_kernel, bands, planes, ranks), [jax.Sha...  1.86 us
    convert_element_type x1, other arithmetic, plane_table(): return jnp.where(held >= 0, table, 0.0).astype(jnp.bfloat16)  1.59 us
  transfers between devices with their start and end apart: 6, of which 5 were waited for; matrix products, arithmetic and copies ran while one was open for 0% of the time, Pallas kernels for 16%

profile of v3, /device:TPU:0, one launch (start us, length us, event | category | flops | bytes accessed | tf_op | source)
XLA Modules:
  0.0 73.0 jit_solution(14182446373852608943)
XLA Ops:
  0.0 0.8 %reshape.75 = s32[8,18]{1,0:T(8,128)S(1)} reshape(s32[144]{0:T(256)} %param.14) | data formatting | bytes 1152 | tf_op jit(solution)/shard_map/reshape | solution.py:42
  0.8 0.1 slice.12
  0.8 0.1 pad_add_fusion
  0.9 0.1 concatenate.28
  1.0 0.1 pad.10.clone
  1.1 0.1 add_add_fusion
  1.1 0.1 concatenate.26
  1.2 0.1 fusion.8
  1.3 0.1 fusion.9
  1.4 0.0 copy-start.5
  1.4 0.7 copy-done.5
  2.1 0.1 and_select_fusion.1
  2.8 0.0 copy-start.3
  2.9 0.0 copy-start.4
  2.9 2.8 %reshape.74.coef = bf16[12,160,144]{2,1,0:T(8,128)(2,1)S(1)} reshape(bf16[12,23040]{1,0:T(8,128)(2,1)} %param.10) | data formatting | bytes 1105920 | tf_op jit(solution)/shard_map/reshape | solution.py:306
  5.7 0.0 copy-done.3
  5.7 0.0 copy-done.4
  5.7 1.6 %fusion.4.tab = bf16[320,144]{1,0:T(8,128)(2,1)S(1)} fusion(s32[320,144]{1,0:T(8,128)S(1)} %copy-done.3, s32[320]{0:T(512)S(1)} %fusion.8, s32[144]{0:T(256)S(1)} %copy-done.4, pred[320]{0:T(512)(128)(4,1)S(1)} %fusion.9), kind=kLoop, calls=%fused_computation.7 | loop fusion | flops 552960 | bytes 278656 | tf_op jit(solution)/shard_map/convert_element_type | solution.py:59
  7.3 0.1 select_convert_fusion.info
  7.4 1.9 %shard_map.100 = (bf16[8,336,128]{2,1,0:T(8,128)(2,1)}, bf16[8,256,128]{2,1,0:T(8,128)(2,1)}) custom-call(bf16[12,160,144]{2,1,0:T(8,128)(2,1)S(1)} %reshape.74.coef, bf16[320,144]{1,0:T(8,128)(2,1)S(1)} %fusion.4.tab, f32[16,256]{1,0:T(8,128)S(1)} %select_convert_fusion.info), custom_call_target="tpu_custom_call" | custom-call | flops 4000000000 | bytes 1048576 | tf_op jit(solution)/shard_map/pallas_call | solution.py:318
  9.3 0.0 copy-start
  9.3 7.4 %all-to-all-start = ((bf16[8,336,128]{2,1,0:T(8,128)(2,1)}), bf16[8,336,128]{2,1,0:T(8,128)(2,1)S(1)}, u32[]{:S(2)}, u32[]{:S(2)}) async-start(bf16[8,336,128]{2,1,0:T(8,128)(2,1)} %get-tuple-element.14), calls=%async_computation | async-start | bytes 1376256 | tf_op jit(solution)/shard_map/all_to_all | solution.py:336
  16.7 0.0 copy-start.6
  16.7 0.7 copy-done.6
  17.4 17.3 %all-to-all-done.refs_0_ = bf16[8,336,128]{2,1,0:T(8,128)(2,1)S(1)} async-done(((bf16[8,336,128]{2,1,0:T(8,128)(2,1)}), bf16[8,336,128]{2,1,0:T(8,128)(2,1)S(1)}, u32[]{:S(2)}, u32[]{:S(2)}) %all-to-all-start) | async-done | bytes 688160 | tf_op jit(solution)/shard_map/all_to_all | solution.py:336
  34.7 0.0 copy-start.1
  34.7 0.0 copy-start.2
  34.7 3.8 %all-to-all-start.1 = ((bf16[8,256,128]{2,1,0:T(8,128)(2,1)}), bf16[8,256,128]{2,1,0:T(8,128)(2,1)S(1)}, u32[]{:S(2)}, u32[]{:S(2)}) async-start(bf16[8,256,128]{2,1,0:T(8,128)(2,1)} %get-tuple-element.17), calls=%async_computation.1 | async-start | bytes 1048576 | tf_op jit(solution)/shard_map/all_to_all | solution.py:336
  38.5 0.0 copy-done
  38.5 0.0 copy-done.1
  38.5 0.0 copy-done.2
  38.5 11.7 %shard_map.101 = (bf16[2,12,40,128]{3,2,1,0:T(8,128)(2,1)S(1)}, bf16[2,12,40,128]{3,2,1,0:T(8,128)(2,1)S(1)}, f32[8,512]{1,0:T(8,128)S(1)}, bf16[512,128]{1,0:T(8,128)(2,1)S(1)}, bf16[512,128]{1,0:T(8,128)(2,1)S(1)}) custom-call(bf16[8,336,128]{2,1,0:T(8,128)(2,1)S(1)} %all-to-all-done.refs_0_, bf16[256,256]{1,0:T(8,128)(2,1)S(1)} %copy-done.2, ...), custom_call_target="tpu_custom_call" | custom-call | flops 16000000000 | bytes 1048576 | tf_op jit(solution)/shard_map/pallas_call | solution.py:361
  50.2 3.0 %all-to-all-done.1.refs_0_ = bf16[8,256,128]{2,1,0:T(8,128)(2,1)S(1)} async-done(((bf16[8,256,128]{2,1,0:T(8,128)(2,1)}), bf16[8,256,128]{2,1,0:T(8,128)(2,1)S(1)}, u32[]{:S(2)}, u32[]{:S(2)}) %all-to-all-start.1) | async-done | bytes 524320 | tf_op jit(solution)/shard_map/all_to_all | solution.py:336
  53.2 9.3 %shard_map.102 = (bf16[2,9,40,128]{3,2,1,0:T(8,128)(2,1)S(1)}, bf16[2,9,40,128]{3,2,1,0:T(8,128)(2,1)S(1)}) custom-call(bf16[8,256,128]{2,1,0:T(8,128)(2,1)S(1)} %all-to-all-done.1.refs_0_, bf16[256,256]{1,0:T(8,128)(2,1)S(1)} %copy-done.2, bf16[2048,256]{1,0:T(8,128)(2,1)S(1)} %copy-done, bf16[288,144]{1,0:T(8,128)(2,1)S(1)} %copy-done.1, ...), custom_call_target="tpu_custom_call" | custom-call | flops 16000000000 | bytes 1048576 | tf_op jit(solution)/shard_map/pallas_call | solution.py:361
  62.5 0.1 collective-permute-start.2
  62.6 0.5 collective-permute-start
  63.1 0.9 %collective-permute-done.2 = bf16[2,9,40,128]{3,2,1,0:T(8,128)(2,1)S(1)} collective-permute-done((bf16[2,9,40,128]{3,2,1,0:T(8,128)(2,1)S(1)}, bf16[2,9,40,128]{3,2,1,0:T(8,128)(2,1)S(1)}, u32[]{:S(2)}, u32[]{:S(2)}) %collective-permute-start.2) | collective-permute-done | bytes 184352 | tf_op jit(solution)/shard_map/ppermute | solution.py:283
  64.0 0.1 add_convert_fusion.1
  64.1 0.3 collective-permute-done
  64.4 0.1 add_convert_fusion
  64.5 1.6 %collective-permute-start.1 = (bf16[1,12,40,128]{3,2,1,0:T(8,128)(2,1)S(1)}, bf16[1,12,40,128]{3,2,1,0:T(8,128)(2,1)S(1)}, u32[]{:S(2)}, u32[]{:S(2)}) collective-permute-start(bf16[1,12,40,128]{3,2,1,0:T(8,128)(2,1)S(1)} %get-tuple-element.23), channel_id=1, source_target_pairs={{0,2},{1,3},{2,0},{3,1},{4,6},{5,7},{6,4},{7,5},{8,10},{9,11},{10,... | collective-permute-start | bytes 368648 | tf_op jit(solution)/shard_map/ppermute | solution.py:283
  66.1 0.6 collective-permute-start.3
  66.7 5.3 %collective-permute-done.3 = bf16[1,9,40,128]{3,2,1,0:T(8,128)(2,1)S(1)} collective-permute-done((bf16[1,9,40,128]{3,2,1,0:T(8,128)(2,1)S(1)}, bf16[1,9,40,128]{3,2,1,0:T(8,128)(2,1)S(1)}, u32[]{:S(2)}, u32[]{:S(2)}) %collective-permute-start.3) | collective-permute-done | bytes 92192 | tf_op jit(solution)/shard_map/ppermute | solution.py:283
  72.0 0.0 collective-permute-done.1
  72.0 1.0 %shard_map.103 = f32[18,36,144]{2,1,0:T(8,128)} custom-call(bf16[12,40,128]{2,1,0:T(8,128)(2,1)S(1)} %get-tuple-element.24.refs_0_, bf16[12,40,128]{2,1,0:T(8,128)(2,1)S(1)} %bitcast.10, bf16[9,40,128]{2,1,0:T(8,128)(2,1)S(1)} %get-tuple-element.26.refs_2_, bf16[9,40,128]{2,1,0:T(8,128)(2,1)S(1)} %bitcast.11), custom_call_target="tpu_custom_call" | custom-call | flops 1 | bytes 1048576 | tf_op jit(solution)/shard_map/pallas_call | solution.py:365
  (7 shorter events, 0.1 us)
Async XLA Ops:
  1.4 0.7 copy-start.5
  2.8 2.9 %copy-start.3 = (s32[320,144]{1,0:T(8,128)S(1)}, s32[320,144]{1,0:T(8,128)}, u32[]{:S(2)}) copy-start(s32[320,144]{1,0:T(8,128)} %constant.75.clone) | copy-start | bytes 552964
  2.9 2.9 %copy-start.4 = (s32[144]{0:T(256)S(1)}, s32[144]{0:T(256)}, u32[]{:S(2)}) copy-start(s32[144]{0:T(256)} %constant.74.clone) | copy-start | bytes 1732
  9.3 29.2 %copy-start = (bf16[2048,256]{1,0:T(8,128)(2,1)S(1)}, bf16[2048,256]{1,0:T(8,128)(2,1)}, u32[]{:S(2)}) copy-start(bf16[2048,256]{1,0:T(8,128)(2,1)} %constant.77.clone.refs_2_) | copy-start | bytes 3145732
  9.3 25.4 %all-to-all-start = ((bf16[8,336,128]{2,1,0:T(8,128)(2,1)}), bf16[8,336,128]{2,1,0:T(8,128)(2,1)S(1)}, u32[]{:S(2)}, u32[]{:S(2)}) async-start(bf16[8,336,128]{2,1,0:T(8,128)(2,1)} %get-tuple-element.14), calls=%async_computation | async-start | bytes 1376256 | tf_op jit(solution)/shard_map/all_to_all | solution.py:336
  16.7 0.7 copy-start.6
  34.7 3.8 %copy-start.1 = (bf16[288,144]{1,0:T(8,128)(2,1)S(1)}, bf16[288,144]{1,0:T(8,128)(2,1)}, u32[]{:S(2)}) copy-start(bf16[288,144]{1,0:T(8,128)(2,1)} %constant.78.clone.refs_3_) | copy-start | bytes 248836
  34.7 3.8 %copy-start.2 = (bf16[256,256]{1,0:T(8,128)(2,1)S(1)}, bf16[256,256]{1,0:T(8,128)(2,1)}, u32[]{:S(2)}) copy-start(bf16[256,256]{1,0:T(8,128)(2,1)} %constant.76.clone.refs_1_) | copy-start | bytes 393220
  34.7 18.4 %all-to-all-start.1 = ((bf16[8,256,128]{2,1,0:T(8,128)(2,1)}), bf16[8,256,128]{2,1,0:T(8,128)(2,1)S(1)}, u32[]{:S(2)}, u32[]{:S(2)}) async-start(bf16[8,256,128]{2,1,0:T(8,128)(2,1)} %get-tuple-element.17), calls=%async_computation.1 | async-start | bytes 1048576 | tf_op jit(solution)/shard_map/all_to_all | solution.py:336
  62.5 1.5 %collective-permute-start.2 = (bf16[2,9,40,128]{3,2,1,0:T(8,128)(2,1)S(1)}, bf16[2,9,40,128]{3,2,1,0:T(8,128)(2,1)S(1)}, u32[]{:S(2)}, u32[]{:S(2)}) collective-permute-start(bf16[2,9,40,128]{3,2,1,0:T(8,128)(2,1)S(1)} %get-tuple-element.22), channel_id=1, source_target_pairs={{0,1},{1,0},{2,3},{3,2},{4,5},{5,4},{6,7},{7,6},{8,9},{9,8},{10,11... | collective-permute-start | bytes 552968 | tf_op jit(solution)/shard_map/ppermute | solution.py:283
  62.6 1.8 %collective-permute-start = (bf16[2,12,40,128]{3,2,1,0:T(8,128)(2,1)S(1)}, bf16[2,12,40,128]{3,2,1,0:T(8,128)(2,1)S(1)}, u32[]{:S(2)}, u32[]{:S(2)}) collective-permute-start(bf16[2,12,40,128]{3,2,1,0:T(8,128)(2,1)S(1)} %get-tuple-element.16), channel_id=1, source_target_pairs={{0,1},{1,0},{2,3},{3,2},{4,5},{5,4},{6,7},{7,6},{8,9},{9,8},{10,11... | collective-permute-start | bytes 737288 | tf_op jit(solution)/shard_map/ppermute | solution.py:283
  64.5 7.5 %collective-permute-start.1 = (bf16[1,12,40,128]{3,2,1,0:T(8,128)(2,1)S(1)}, bf16[1,12,40,128]{3,2,1,0:T(8,128)(2,1)S(1)}, u32[]{:S(2)}, u32[]{:S(2)}) collective-permute-start(bf16[1,12,40,128]{3,2,1,0:T(8,128)(2,1)S(1)} %get-tuple-element.23), channel_id=1, source_target_pairs={{0,2},{1,3},{2,0},{3,1},{4,6},{5,7},{6,4},{7,5},{8,10},{9,11},{10,... | collective-permute-start | bytes 368648 | tf_op jit(solution)/shard_map/ppermute | solution.py:283
  66.1 5.9 %collective-permute-start.3 = (bf16[1,9,40,128]{3,2,1,0:T(8,128)(2,1)S(1)}, bf16[1,9,40,128]{3,2,1,0:T(8,128)(2,1)S(1)}, u32[]{:S(2)}, u32[]{:S(2)}) collective-permute-start(bf16[1,9,40,128]{3,2,1,0:T(8,128)(2,1)S(1)} %get-tuple-element.25), channel_id=1, source_target_pairs={{0,2},{1,3},{2,0},{3,1},{4,6},{5,7},{6,4},{7,5},{8,10},{9,11},{10,... | collective-permute-start | bytes 276488 | tf_op jit(solution)/shard_map/ppermute | solution.py:283

commit v4 on v3

--- a/solution.py
+++ b/solution.py
@@ -38,25 +38,24 @@
     return [jnp.asarray(x, jnp.bfloat16) for x in (rows, ends, cols)]
 
 
-def plane_table(plane_slot, planes, ranks):
-    held = plane_slot.reshape(ranks, -1)
-    rows, imag_rows, base = [], [], 0
+def stick_constants(planes, ranks):
+    freqs = np.arange(GB) - GB // 2
+    angles = (np.arange(N)[:, None] * freqs[None, :] % N) * (2.0 * math.pi / N)
+    cosine, sine = np.cos(angles), np.sin(angles)
+    held = sum(planes)
+    ordered = sum(ranks * up(2 * count, 8) for count in planes)
+    fixed = np.zeros((2, N + ordered, up(max(2 * LANES, ranks * held), LANES)), np.float32)
+    fixed[0, :N, : 2 * GB] = np.concatenate([cosine, -sine], axis=1)
+    fixed[1, :N, : 2 * GB] = np.concatenate([sine, cosine], axis=1)
+    row, base = N, 0
     for count in planes:
-        group = up(2 * count, 8)
-        part = held[:, base : base + count]
-        empty = jnp.full((ranks, group - 2 * count), -1, jnp.int32)
-        rows.append(jnp.concatenate([part, part, empty], axis=1).reshape(-1))
-        imag_rows.append(np.tile(np.arange(group) >= count, ranks))
+        for d in range(ranks):
+            for part in range(2):
+                for j in range(count):
+                    fixed[part, row + part * count + j, d * held + base + j] = 1
+            row += up(2 * count, 8)
         base += count
-    held = jnp.concatenate(rows)[:, None]
-    imag_row = np.concatenate(imag_rows)[:, None]
-    col = np.arange(2 * GB)
-    imag_col = (col >= GB)[None, :]
-    freq = col % GB - GB // 2
-    quarter = np.where(imag_row == imag_col, 0, np.where(imag_col, N // 4, 3 * N // 4))
-    turns = jnp.mod(freq * jnp.maximum(held, 0) + quarter.astype(np.int32), N)
-    table = jnp.cos(turns.astype(jnp.float32) * (2.0 * math.pi / N))
-    return jnp.where(held >= 0, table, 0.0).astype(jnp.bfloat16)
+    return jnp.asarray(fixed.reshape(-1, fixed.shape[2]), jnp.bfloat16)
 
 
 def lane_group(rows, dtype):
@@ -64,20 +63,56 @@
     return [(group == g).astype(jnp.float32).astype(dtype) for g in range(GROUPS + 1)]
 
 
-def stick_kernel(bands, planes, ranks, coef, tab, info, *refs):
+def stick_kernel(planes, ranks, *refs):
     chunks = len(planes)
-    outs, mains, rests = refs[:chunks], refs[chunks : 2 * chunks], refs[2 * chunks :]
+    outs, scratch = refs[5 : 5 + chunks], refs[5 + chunks :]
+    count_here, slot_of, fixed, coef, column, done, low, high, ends = scratch[:9]
+    mains, rests = scratch[9 : 9 + chunks], scratch[9 + chunks :]
+    bands, slots = coef.shape[0], column.shape[0]
+    inside = (count_here, slot_of, fixed, coef, column)
+    copies = [
+        pltpu.make_async_copy(src, to, done.at[i]) for i, (src, to) in enumerate(zip(refs, inside))
+    ]
+    for copy in copies:
+        copy.start()
     for main, rest, count in zip(mains, rests, planes):
         if 2 * count * bands < main.shape[1]:
             main[...] = jnp.zeros_like(main)
             rest[...] = jnp.zeros_like(rest)
-    table = tab[...]
+
+    def product(x, y, dims):
+        return lax.dot_general(x, y, (dims, ((), ())), preferred_element_type=jnp.float32)
+
+    copies[1].wait()
+    copies[2].wait()
+    held = slot_of[...].reshape(1, -1)
+    at_pos = lax.broadcasted_iota(jnp.int32, (N, held.shape[1]), 0) == held
+    at_pos = jnp.where(at_pos, 1.0, 0.0).astype(jnp.bfloat16)
+    table = 0.0
+    ordered = fixed.shape[0] // 2 - N
+    for part in range(2):
+        at = part * (N + ordered)
+        pos = fixed[at : at + N]
+        order = fixed[at + N : at + N + ordered, : held.shape[1]]
+        rows_of_slot = product(at_pos, pos, ((0,), (0,))).astype(jnp.bfloat16)
+        table = table + product(order, rows_of_slot, ((1,), (0,)))
+    table = table.astype(jnp.bfloat16)
+
+    stride = low.shape[0] // bands
+    copies[3].wait()
+    for s in range(slots):
+        tile, shift = divmod(s * 2 * GB, LANES)
+        x = coef[:, tile * LANES : (tile + 2) * LANES].astype(jnp.float32)
+        if shift:
+            x = pltpu.roll(x, 2 * LANES - shift, 1)
+        low[pl.ds(s, bands, stride=stride), :] = x[:, :LANES]
+        high[pl.ds(s, bands, stride=stride), :] = x[:, LANES:]
+
     for b in range(bands):
-        x = coef[b]
+        here = slice(b * stride, b * stride + slots)
+        x = jnp.concatenate([low[here], high[here]], axis=1).astype(jnp.bfloat16)
         x = jnp.concatenate([x[:LANES]] + [x[LANES:]] * 4, axis=0)
-        val = lax.dot_general(
-            table, x, (((1,), (1,)), ((), ())), preferred_element_type=jnp.float32
-        )
+        val = product(table, x, ((1,), (1,)))
         at = 0
         for main, rest, count in zip(mains, rests, planes):
             for d in range(ranks):
@@ -85,6 +120,20 @@
                 main[d, pl.ds(b, 2 * count, stride=bands), :] = part[:, :LANES]
                 rest[d, pl.ds(b, 2 * count, stride=bands), :] = part[:, LANES:]
                 at += up(2 * count, 8)
+
+    copies[0].wait()
+    copies[4].wait()
+    c = column[...].reshape(1, -1).astype(jnp.float32)
+    gx = jnp.floor((c + 0.5) * (1.0 / GB))
+    row = lax.broadcasted_iota(jnp.int32, (INFO, slots), 0)
+    live = count_here[0].astype(jnp.float32)
+    info = jnp.where(
+        row == 0, gx, jnp.where(row == 1, c - GB * gx, jnp.where(row == 2, live, 0.0))
+    )
+    ends[...] = jnp.zeros_like(ends)
+    ends[:, : slots - LANES] = info[:, LANES:]
+    tail_info = pltpu.roll(ends[...], 96, 1)
+
     for c, (out, main, rest) in enumerate(zip(outs, mains, rests)):
         rows = main.shape[1]
         span = rows // GROUPS
@@ -97,10 +146,9 @@
                 packed = packed + rest[d, g * span : (g + 1) * span, :] * masks[g]
             if c == 0:
                 out[d, rows:at, :] = info[:, :LANES].astype(jnp.bfloat16)
-                tail_info = jnp.concatenate(
-                    [info[:, LANES:], jnp.zeros((span - INFO, LANES), jnp.float32)], axis=0
+                packed = packed + jnp.concatenate(
+                    [tail_info, jnp.zeros((span - INFO, LANES), jnp.float32)], axis=0
                 )
-                packed = packed + tail_info * masks[GROUPS]
             out[d, at:, :] = packed.astype(jnp.bfloat16)
 
 
@@ -257,18 +305,20 @@
     return max(d for d in range(1, most + 1) if n % d == 0)
 
 
-def vmem_call(kernel, out_shape, n_in, scratch=(), flops=1, smem=()):
-    used = sum(math.prod(m.shape) * jnp.dtype(m.dtype).itemsize for m in scratch)
+def vmem_call(kernel, out_shape, n_in, scratch=(), flops=1, smem=(), far=()):
+    vmem_scratch = [m for m in scratch if m.memory_space == pltpu.VMEM]
+    used = sum(math.prod(m.shape) * jnp.dtype(m.dtype).itemsize for m in vmem_scratch)
     vmem = pl.BlockSpec(memory_space=pltpu.VMEM)
     scalar = pl.BlockSpec(memory_space=pltpu.SMEM)
+    hbm = pl.BlockSpec(memory_space=pltpu.HBM)
     many = isinstance(out_shape, list)
     return pl.pallas_call(
         kernel,
         out_shape=out_shape,
-        in_specs=[scalar if i in smem else vmem for i in range(n_in)],
+        in_specs=[scalar if i in smem else hbm if i in far else vmem for i in range(n_in)],
         out_specs=[vmem] * len(out_shape) if many else vmem,
         scratch_shapes=list(scratch),
-        compiler_params=pltpu.CompilerParams(vmem_limit_bytes=min(63 * 2**20, used + 12 * 2**20)),
+        compiler_params=pltpu.CompilerParams(vmem_limit_bytes=62 * 2**20 if far else min(62 * 2**20, used + 12 * 2**20)),
         cost_estimate=pl.CostEstimate(flops=flops, bytes_accessed=1 << 20, transcendentals=0),
     )
 
@@ -303,28 +353,34 @@
     own_rows = N // owners
     bf16, f32 = jnp.bfloat16, jnp.float32
 
-    coef = coefficients.reshape(bands, slots, 2 * GB)
-    table = plane_table(plane_slot, planes, ranks)
-    spread = jnp.concatenate([columns[:LANES]] + [columns[LANES:]] * 4)
-    row = jnp.arange(INFO, dtype=jnp.int32)[:, None]
-    info = jnp.where(
-        row == 0, spread // GB, jnp.where(row == 1, spread % GB, jnp.where(row == 2, counts[0], 0))
-    ).astype(f32)
     weight = occupations / (bands * owners)
     core = (lax.axis_index("band") & 1)[None]
     tables = wave_tables()
 
     spans = [up(-(-2 * count * bands // GROUPS), 16) for count in planes]
+    fixed = stick_constants(planes, ranks)
+    stride = up(slots, 8) + 8
     outgoing = vmem_call(
-        functools.partial(stick_kernel, bands, planes, ranks),
+        functools.partial(stick_kernel, planes, ranks),
         [
             jax.ShapeDtypeStruct((ranks, 4 * span + (INFO if c == 0 else 0), LANES), bf16)
             for c, span in enumerate(spans)
         ],
-        3,
-        [pltpu.VMEM((ranks, GROUPS * span, LANES), f32) for span in spans * 2],
+        5,
+        [
+            pltpu.SMEM(counts.shape, jnp.int32),
+            pltpu.VMEM(plane_slot.shape, jnp.int32),
+            pltpu.VMEM(fixed.shape, bf16),
+            pltpu.VMEM(coefficients.shape, bf16),
+            pltpu.VMEM(columns.shape, jnp.int32),
+            pltpu.SemaphoreType.DMA((5,)),
+        ]
+        + [pltpu.VMEM((bands * stride, LANES), f32)] * 2
+        + [pltpu.VMEM((INFO, LANES), f32)]
+        + [pltpu.VMEM((ranks, GROUPS * span, LANES), f32) for span in spans * 2],
         flops=4 * 10**9,
-    )(coef, table, info)
+        far=range(5),
+    )(counts, plane_slot, fixed, coefficients, columns)
     kept_shapes = [
         jax.ShapeDtypeStruct((ranks, cap), f32),
         jax.ShapeDtypeStruct((cap, LANES), bf16),

time: 73.4 us -> 68.6 us (0.935)
  local copies, waits for them, and re-layouts: 5.33 us -> 0.73 us
  Pallas kernels: 23.9 us -> 26.1 us
  other arithmetic: 2.22 us -> 0.12 us
    reshape x2 -> x0, local copies, waits for them, and re-layouts: 3.6 us -> none  [the longest x1 2.85 us: shards(): coef = coefficients.reshape(bands, slots, 2 * GB)]
    pallas_call x1, Pallas kernels: 1.86 us -> 3.81 us  [shards(): vmem_call(functools.partial(stick_kernel, planes, ranks), [jax.ShapeDtype...]
    convert_element_type x2 -> x0, other arithmetic: 1.67 us -> none  [the longest x1 1.59 us: plane_table(): return jnp.where(held >= 0, table, 0.0).astype(jnp.bfloat16)]
  transfers between devices with their start and end apart: 6 -> 6, of which waited for: 5 -> 5; matrix products, arithmetic and copies ran while one was open for 0% -> 0% of each run, Pallas kernels for 16% -> 17%
where the time goes in v4:
time: 68.6 us; the launch traced here: 68.3 us
  waiting for transfers between devices  26.7 us (39%)
  Pallas kernels  26.1 us (38%)
  starting transfers between devices  14 us (20%)
  between operations  0.74 us (1%)
  local copies, waits for them, and re-layouts  0.73 us (1%)
    pallas_call x2, Pallas kernels, shards(): results = run(received, *tables, weight, core, *kept)  21.2 us
    all_to_all x2, waiting for transfers between devices, shards(): lax.all_to_all(outgoing[c], 'fft', split_axis=0, concat_axis=0, tiled=True)  20.2 us
    all_to_all x2, starting transfers between devices, shards(): lax.all_to_all(outgoing[c], 'fft', split_axis=0, concat_axis=0, tiled=True)  11.2 us
    ppermute x4, waiting for transfers between devices, halve(): got = lax.ppermute(send, axis, partners(axis, bit))  6.54 us
    pallas_call x1, Pallas kernels, shards(): vmem_call(functools.partial(stick_kernel, planes, ranks), [jax.ShapeDtype...  3.81 us
    ppermute x4, starting transfers between devices, halve(): got = lax.ppermute(send, axis, partners(axis, bit))  2.73 us
  transfers between devices with their start and end apart: 6, of which 5 were waited for; matrix products, arithmetic and copies ran while one was open for 0% of the time, Pallas kernels for 17%

profile of v4, /device:TPU:0, one launch (start us, length us, event | category | flops | bytes accessed | tf_op | source)
XLA Modules:
  0.0 68.3 jit_solution(10854337058911766116)
XLA Ops:
  0.7 3.8 %shard_map.91 = (bf16[8,336,128]{2,1,0:T(8,128)(2,1)}, bf16[8,256,128]{2,1,0:T(8,128)(2,1)}) custom-call(s32[1]{0:T(128)S(6)} %copy.10.refs_0_, s32[144]{0:T(256)} %refs_1_.3, bf16[928,256]{1,0:T(8,128)(2,1)} %constant.36.clone.refs_2_, bf16[12,23040]{1,0:T(8,128)(2,1)} %refs_3_.3, s32[160]{0:T(256)} %refs_4_.1), custom_call_target="tpu_custom_call" | custom-call | flops 4000000000 | bytes 1048576 | tf_op jit(solution)/shard_map/pallas_call | solution.py:363
  4.5 0.0 copy-start
  4.5 7.5 %all-to-all-start = ((bf16[8,336,128]{2,1,0:T(8,128)(2,1)}), bf16[8,336,128]{2,1,0:T(8,128)(2,1)S(1)}, u32[]{:S(2)}, u32[]{:S(2)}) async-start(bf16[8,336,128]{2,1,0:T(8,128)(2,1)} %get-tuple-element.14), calls=%async_computation | async-start | bytes 1376256 | tf_op jit(solution)/shard_map/all_to_all | solution.py:392
  11.9 0.0 copy-start.3
  11.9 0.7 copy-done.3
  12.6 17.3 %all-to-all-done.refs_0_ = bf16[8,336,128]{2,1,0:T(8,128)(2,1)S(1)} async-done(((bf16[8,336,128]{2,1,0:T(8,128)(2,1)}), bf16[8,336,128]{2,1,0:T(8,128)(2,1)S(1)}, u32[]{:S(2)}, u32[]{:S(2)}) %all-to-all-start) | async-done | bytes 688160 | tf_op jit(solution)/shard_map/all_to_all | solution.py:392
  29.9 0.0 copy-start.1
  29.9 0.0 copy-start.2
  29.9 3.8 %all-to-all-start.1 = ((bf16[8,256,128]{2,1,0:T(8,128)(2,1)}), bf16[8,256,128]{2,1,0:T(8,128)(2,1)S(1)}, u32[]{:S(2)}, u32[]{:S(2)}) async-start(bf16[8,256,128]{2,1,0:T(8,128)(2,1)} %get-tuple-element.17), calls=%async_computation.1 | async-start | bytes 1048576 | tf_op jit(solution)/shard_map/all_to_all | solution.py:392
  33.7 0.0 copy-done
  33.7 0.0 copy-done.1
  33.7 0.0 copy-done.2
  33.7 11.8 %shard_map.92 = (bf16[2,12,40,128]{3,2,1,0:T(8,128)(2,1)S(1)}, bf16[2,12,40,128]{3,2,1,0:T(8,128)(2,1)S(1)}, f32[8,512]{1,0:T(8,128)S(1)}, bf16[512,128]{1,0:T(8,128)(2,1)S(1)}, bf16[512,128]{1,0:T(8,128)(2,1)S(1)}) custom-call(bf16[8,336,128]{2,1,0:T(8,128)(2,1)S(1)} %all-to-all-done.refs_0_, bf16[256,256]{1,0:T(8,128)(2,1)S(1)} %copy-done.2, ...), custom_call_target="tpu_custom_call" | custom-call | flops 16000000000 | bytes 1048576 | tf_op jit(solution)/shard_map/pallas_call | solution.py:417
  45.5 2.9 %all-to-all-done.1.refs_0_ = bf16[8,256,128]{2,1,0:T(8,128)(2,1)S(1)} async-done(((bf16[8,256,128]{2,1,0:T(8,128)(2,1)}), bf16[8,256,128]{2,1,0:T(8,128)(2,1)S(1)}, u32[]{:S(2)}, u32[]{:S(2)}) %all-to-all-start.1) | async-done | bytes 524320 | tf_op jit(solution)/shard_map/all_to_all | solution.py:392
  48.4 9.4 %shard_map.93 = (bf16[2,9,40,128]{3,2,1,0:T(8,128)(2,1)S(1)}, bf16[2,9,40,128]{3,2,1,0:T(8,128)(2,1)S(1)}) custom-call(bf16[8,256,128]{2,1,0:T(8,128)(2,1)S(1)} %all-to-all-done.1.refs_0_, bf16[256,256]{1,0:T(8,128)(2,1)S(1)} %copy-done.2, bf16[2048,256]{1,0:T(8,128)(2,1)S(1)} %copy-done, bf16[288,144]{1,0:T(8,128)(2,1)S(1)} %copy-done.1, ...), custom_call_target="tpu_custom_call" | custom-call | flops 16000000000 | bytes 1048576 | tf_op jit(solution)/shard_map/pallas_call | solution.py:417
  57.8 0.1 collective-permute-start.2
  57.9 0.5 collective-permute-start
  58.4 0.9 %collective-permute-done.2 = bf16[2,9,40,128]{3,2,1,0:T(8,128)(2,1)S(1)} collective-permute-done((bf16[2,9,40,128]{3,2,1,0:T(8,128)(2,1)S(1)}, bf16[2,9,40,128]{3,2,1,0:T(8,128)(2,1)S(1)}, u32[]{:S(2)}, u32[]{:S(2)}) %collective-permute-start.2) | collective-permute-done | bytes 184352 | tf_op jit(solution)/shard_map/ppermute | solution.py:333
  59.3 0.1 add_convert_fusion.1
  59.4 0.3 collective-permute-done
  59.7 0.1 add_convert_fusion
  59.8 1.6 %collective-permute-start.1 = (bf16[1,12,40,128]{3,2,1,0:T(8,128)(2,1)S(1)}, bf16[1,12,40,128]{3,2,1,0:T(8,128)(2,1)S(1)}, u32[]{:S(2)}, u32[]{:S(2)}) collective-permute-start(bf16[1,12,40,128]{3,2,1,0:T(8,128)(2,1)S(1)} %get-tuple-element.23), channel_id=1, source_target_pairs={{0,2},{1,3},{2,0},{3,1},{4,6},{5,7},{6,4},{7,5},{8,10},{9,11},{10,... | collective-permute-start | bytes 368648 | tf_op jit(solution)/shard_map/ppermute | solution.py:333
  61.4 0.6 collective-permute-start.3
  62.0 5.3 %collective-permute-done.3 = bf16[1,9,40,128]{3,2,1,0:T(8,128)(2,1)S(1)} collective-permute-done((bf16[1,9,40,128]{3,2,1,0:T(8,128)(2,1)S(1)}, bf16[1,9,40,128]{3,2,1,0:T(8,128)(2,1)S(1)}, u32[]{:S(2)}, u32[]{:S(2)}) %collective-permute-start.3) | collective-permute-done | bytes 92192 | tf_op jit(solution)/shard_map/ppermute | solution.py:333
  67.3 0.0 collective-permute-done.1
  67.3 1.0 %shard_map.94 = f32[18,36,144]{2,1,0:T(8,128)} custom-call(bf16[12,40,128]{2,1,0:T(8,128)(2,1)S(1)} %get-tuple-element.24.refs_0_, bf16[12,40,128]{2,1,0:T(8,128)(2,1)S(1)} %bitcast.7, bf16[9,40,128]{2,1,0:T(8,128)(2,1)S(1)} %get-tuple-element.26.refs_2_, bf16[9,40,128]{2,1,0:T(8,128)(2,1)S(1)} %bitcast.8), custom_call_target="tpu_custom_call" | custom-call | flops 1 | bytes 1048576 | tf_op jit(solution)/shard_map/pallas_call | solution.py:421
  (3 shorter events, 0.1 us)
Async XLA Ops:
  4.5 29.2 %copy-start = (bf16[2048,256]{1,0:T(8,128)(2,1)S(1)}, bf16[2048,256]{1,0:T(8,128)(2,1)}, u32[]{:S(2)}) copy-start(bf16[2048,256]{1,0:T(8,128)(2,1)} %constant.34.clone.refs_2_) | copy-start | bytes 3145732
  4.5 25.4 %all-to-all-start = ((bf16[8,336,128]{2,1,0:T(8,128)(2,1)}), bf16[8,336,128]{2,1,0:T(8,128)(2,1)S(1)}, u32[]{:S(2)}, u32[]{:S(2)}) async-start(bf16[8,336,128]{2,1,0:T(8,128)(2,1)} %get-tuple-element.14), calls=%async_computation | async-start | bytes 1376256 | tf_op jit(solution)/shard_map/all_to_all | solution.py:392
  11.9 0.7 copy-start.3
  29.9 3.8 %copy-start.1 = (bf16[288,144]{1,0:T(8,128)(2,1)S(1)}, bf16[288,144]{1,0:T(8,128)(2,1)}, u32[]{:S(2)}) copy-start(bf16[288,144]{1,0:T(8,128)(2,1)} %constant.35.clone.refs_3_) | copy-start | bytes 248836
  29.9 3.8 %copy-start.2 = (bf16[256,256]{1,0:T(8,128)(2,1)S(1)}, bf16[256,256]{1,0:T(8,128)(2,1)}, u32[]{:S(2)}) copy-start(bf16[256,256]{1,0:T(8,128)(2,1)} %constant.33.clone.refs_1_) | copy-start | bytes 393220
  29.9 18.4 %all-to-all-start.1 = ((bf16[8,256,128]{2,1,0:T(8,128)(2,1)}), bf16[8,256,128]{2,1,0:T(8,128)(2,1)S(1)}, u32[]{:S(2)}, u32[]{:S(2)}) async-start(bf16[8,256,128]{2,1,0:T(8,128)(2,1)} %get-tuple-element.17), calls=%async_computation.1 | async-start | bytes 1048576 | tf_op jit(solution)/shard_map/all_to_all | solution.py:392
  57.8 1.5 %collective-permute-start.2 = (bf16[2,9,40,128]{3,2,1,0:T(8,128)(2,1)S(1)}, bf16[2,9,40,128]{3,2,1,0:T(8,128)(2,1)S(1)}, u32[]{:S(2)}, u32[]{:S(2)}) collective-permute-start(bf16[2,9,40,128]{3,2,1,0:T(8,128)(2,1)S(1)} %get-tuple-element.22), channel_id=1, source_target_pairs={{0,1},{1,0},{2,3},{3,2},{4,5},{5,4},{6,7},{7,6},{8,9},{9,8},{10,11... | collective-permute-start | bytes 552968 | tf_op jit(solution)/shard_map/ppermute | solution.py:333
  57.9 1.8 %collective-permute-start = (bf16[2,12,40,128]{3,2,1,0:T(8,128)(2,1)S(1)}, bf16[2,12,40,128]{3,2,1,0:T(8,128)(2,1)S(1)}, u32[]{:S(2)}, u32[]{:S(2)}) collective-permute-start(bf16[2,12,40,128]{3,2,1,0:T(8,128)(2,1)S(1)} %get-tuple-element.16), channel_id=1, source_target_pairs={{0,1},{1,0},{2,3},{3,2},{4,5},{5,4},{6,7},{7,6},{8,9},{9,8},{10,11... | collective-permute-start | bytes 737288 | tf_op jit(solution)/shard_map/ppermute | solution.py:333
  59.8 7.5 %collective-permute-start.1 = (bf16[1,12,40,128]{3,2,1,0:T(8,128)(2,1)S(1)}, bf16[1,12,40,128]{3,2,1,0:T(8,128)(2,1)S(1)}, u32[]{:S(2)}, u32[]{:S(2)}) collective-permute-start(bf16[1,12,40,128]{3,2,1,0:T(8,128)(2,1)S(1)} %get-tuple-element.23), channel_id=1, source_target_pairs={{0,2},{1,3},{2,0},{3,1},{4,6},{5,7},{6,4},{7,5},{8,10},{9,11},{10,... | collective-permute-start | bytes 368648 | tf_op jit(solution)/shard_map/ppermute | solution.py:333
  61.4 5.9 %collective-permute-start.3 = (bf16[1,9,40,128]{3,2,1,0:T(8,128)(2,1)S(1)}, bf16[1,9,40,128]{3,2,1,0:T(8,128)(2,1)S(1)}, u32[]{:S(2)}, u32[]{:S(2)}) collective-permute-start(bf16[1,9,40,128]{3,2,1,0:T(8,128)(2,1)S(1)} %get-tuple-element.25), channel_id=1, source_target_pairs={{0,2},{1,3},{2,0},{3,1},{4,6},{5,7},{6,4},{7,5},{8,10},{9,11},{10,... | collective-permute-start | bytes 276488 | tf_op jit(solution)/shard_map/ppermute | solution.py:333

commit v5 on v4

--- a/solution.py
+++ b/solution.py
@@ -65,7 +65,8 @@
 
 def stick_kernel(planes, ranks, *refs):
     chunks = len(planes)
-    outs, scratch = refs[5 : 5 + chunks], refs[5 + chunks :]
+    outs, scratch = refs[5 : 6 + (chunks - 1) * ranks], refs[6 + (chunks - 1) * ranks :]
+    me = lax.axis_index("fft")
     count_here, slot_of, fixed, coef, column, done, low, high, ends = scratch[:9]
     mains, rests = scratch[9 : 9 + chunks], scratch[9 + chunks :]
     bands, slots = coef.shape[0], column.shape[0]
@@ -134,29 +135,34 @@
     ends[:, : slots - LANES] = info[:, LANES:]
     tail_info = pltpu.roll(ends[...], 96, 1)
 
-    for c, (out, main, rest) in enumerate(zip(outs, mains, rests)):
+    for c, (main, rest) in enumerate(zip(mains, rests)):
         rows = main.shape[1]
         span = rows // GROUPS
         masks = lane_group(span, jnp.float32)
         at = rows + (INFO if c == 0 else 0)
-        for d in range(ranks):
-            out[d, :rows, :] = main[d].astype(jnp.bfloat16)
+        for k in range(ranks):
+            out, d = (outs[0].at[k], k) if c == 0 else (outs[1 + (c - 1) * ranks + k], me ^ k)
+            out[:rows, :] = main[d].astype(jnp.bfloat16)
             packed = rest[d, :span, :] * masks[0]
             for g in range(1, GROUPS):
                 packed = packed + rest[d, g * span : (g + 1) * span, :] * masks[g]
             if c == 0:
-                out[d, rows:at, :] = info[:, :LANES].astype(jnp.bfloat16)
+                out[rows:at, :] = info[:, :LANES].astype(jnp.bfloat16)
                 packed = packed + jnp.concatenate(
                     [tail_info, jnp.zeros((span - INFO, LANES), jnp.float32)], axis=0
                 )
-            out[d, at:, :] = packed.astype(jnp.bfloat16)
+            out[at:, :] = packed.astype(jnp.bfloat16)
 
 
 def plane_kernel(first, bands, ranks, planes, span, owners, own_rows, *refs):
     if first:
         recv, row_tab, end_tab, col_tab, weight, core, keep, send, turn, gx_of, gy_hot = refs[:11]
+        blocks, source = [recv.at[src] for src in range(ranks)], lambda k: slice(k, k + 1)
     else:
-        recv, row_tab, end_tab, col_tab, weight, core, turn, gx_of, gy_hot, keep, send = refs[:11]
+        blocks, refs = refs[:ranks], refs[ranks - 1 :]
+        _, row_tab, end_tab, col_tab, weight, core, turn, gx_of, gy_hot, keep, send = refs[:11]
+        me = lax.axis_index("fft")
+        source = lambda k: pl.ds(me ^ k, 1)
     lhs, pick, sticks, real, imag, both, half, tail, acc, acc_tail = refs[11:]
     rows = GROUPS * span
     total = rows + INFO if first else rows
@@ -167,7 +173,7 @@
         place = lax.broadcasted_iota(jnp.int32, (1, cap), 1).astype(jnp.float32)
         start = jnp.zeros((1, 1), jnp.float32)
         for src in range(ranks):
-            count = recv[src, rows : rows + INFO, :].astype(jnp.float32)[2:3, 0:1]
+            count = blocks[src][rows : rows + INFO, :].astype(jnp.float32)[2:3, 0:1]
             t = place - start
             turn[src : src + 1, :] = jnp.where(jnp.logical_and(t >= 0, t < count), t, -1.0)
             start = start + count
@@ -177,14 +183,14 @@
     slot = jnp.where(k < LANES, k, LANES + k % 32).astype(jnp.float32)
     for src in range(ranks):
         at = src * 2 * LANES
-        pick[at : at + 2 * LANES, :] = jnp.where(slot == turn[src : src + 1, :], 1.0, 0.0).astype(
+        pick[at : at + 2 * LANES, :] = jnp.where(slot == turn[source(src), :], 1.0, 0.0).astype(
             jnp.bfloat16
         )
-        packed = recv[src, total : total + span, :]
+        packed = blocks[src][total : total + span, :]
         pieces = [packed * masks[g] for g in range(GROUPS)]
         if first:
             pieces.append((packed * masks[GROUPS])[:INFO])
-        lhs[:, at : at + LANES] = recv[src, :total, :]
+        lhs[:, at : at + LANES] = blocks[src][:total, :]
         lhs[:, at + LANES : at + 2 * LANES] = jnp.concatenate(pieces, axis=0)
     compact = jnp.dot(lhs[...], pick[...], preferred_element_type=jnp.float32)
     sticks[...] = compact[:rows].astype(jnp.bfloat16)
@@ -362,10 +368,8 @@
     stride = up(slots, 8) + 8
     outgoing = vmem_call(
         functools.partial(stick_kernel, planes, ranks),
-        [
-            jax.ShapeDtypeStruct((ranks, 4 * span + (INFO if c == 0 else 0), LANES), bf16)
-            for c, span in enumerate(spans)
-        ],
+        [jax.ShapeDtypeStruct((ranks, 4 * spans[0] + INFO, LANES), bf16)]
+        + [jax.ShapeDtypeStruct((4 * spans[1], LANES), bf16)] * ranks,
         5,
         [
             pltpu.SMEM(counts.shape, jnp.int32),
@@ -389,7 +393,13 @@
     kept, halves = [], []
     for c, (count, span) in enumerate(zip(planes, spans)):
         first = c == 0
-        received = lax.all_to_all(outgoing[c], "fft", split_axis=0, concat_axis=0, tiled=True)
+        if first:
+            received = [lax.all_to_all(outgoing[0], "fft", split_axis=0, concat_axis=0, tiled=True)]
+        else:
+            received = [outgoing[1]]
+            for k in range(1, ranks):
+                pairs = [(i, i ^ k) for i in range(ranks)]
+                received.append(lax.ppermute(outgoing[1 + k], "fft", pairs))
         rows = GROUPS * span
         tails = -(-count // SHARE)
         dens_shape = jax.ShapeDtypeStruct(
@@ -398,7 +408,7 @@
         run = vmem_call(
             functools.partial(plane_kernel, first, bands, ranks, count, span, owners, own_rows),
             [dens_shape] * 2 + (kept_shapes if first else []),
-            6 if first else 9,
+            len(received) + (5 if first else 8),
             [
                 pltpu.VMEM((rows + (INFO if first else 0), ranks * 2 * LANES), bf16),
                 pltpu.VMEM((ranks * 2 * LANES, cap), bf16),
@@ -412,9 +422,9 @@
                 pltpu.VMEM((tails, N, LANES), f32),
             ],
             flops=16 * 10**9,
-            smem=(4, 5),
+            smem=(len(received) + 3, len(received) + 4),
         )
-        results = run(received, *tables, weight, core, *kept)
+        results = run(*received, *tables, weight, core, *kept)
         if first:
             kept = list(results[2:])
         halves += halve(results[0], results[1], "band")

time: 68.6 us -> 68.7 us (level)
  starting transfers between devices: 14 us -> 27 us
  waiting for transfers between devices: 26.7 us -> 14.7 us
    ppermute x0 -> x7, starting transfers between devices: none -> 16.9 us  [shards(): received.append(lax.ppermute(outgoing[1 + k], 'fft', pairs))]
    all_to_all x2 -> x1, waiting for transfers between devices: 20.2 us -> 6.4 us  [shards(): lax.all_to_all(outgoing[0], 'fft', split_axis=0, concat_axis=0, tiled=True)]
    all_to_all x2 -> x1, starting transfers between devices: 11.2 us -> 7.45 us  [shards(): lax.all_to_all(outgoing[0], 'fft', split_axis=0, concat_axis=0, tiled=True)]
    ppermute x0 -> x7, waiting for transfers between devices: none -> 1.78 us  [shards(): received.append(lax.ppermute(outgoing[1 + k], 'fft', pairs))]
  transfers between devices with their start and end apart: 6 -> 12, of which waited for: 5 -> 6; matrix products, arithmetic and copies ran while one was open for 0% -> 0% of each run, Pallas kernels for 17% -> 17%
where the time goes in v5:
time: 68.7 us; the launch traced here: 68.5 us
  starting transfers between devices  27 us (39%)
  Pallas kernels  25.7 us (37%)
  waiting for transfers between devices  14.7 us (21%)
  between operations  0.81 us (1%)
    pallas_call x2, Pallas kernels, shards(): results = run(*received, *tables, weight, core, *kept)  20.9 us
    ppermute x7, starting transfers between devices, shards(): received.append(lax.ppermute(outgoing[1 + k], 'fft', pairs))  16.9 us
    all_to_all x1, starting transfers between devices, shards(): lax.all_to_all(outgoing[0], 'fft', split_axis=0, concat_axis=0, tiled=True)  7.45 us
    ppermute x4, waiting for transfers between devices, halve(): got = lax.ppermute(send, axis, partners(axis, bit))  6.54 us
    all_to_all x1, waiting for transfers between devices, shards(): lax.all_to_all(outgoing[0], 'fft', split_axis=0, concat_axis=0, tiled=True)  6.4 us
    pallas_call x1, Pallas kernels, shards(): vmem_call(functools.partial(stick_kernel, planes, ranks), [jax.ShapeDtype...  3.78 us
    ppermute x4, starting transfers between devices, halve(): got = lax.ppermute(send, axis, partners(axis, bit))  2.73 us
    ppermute x7, waiting for transfers between devices, shards(): received.append(lax.ppermute(outgoing[1 + k], 'fft', pairs))  1.78 us
  transfers between devices with their start and end apart: 12, of which 6 were waited for; matrix products, arithmetic and copies ran while one was open for 0% of the time, Pallas kernels for 17%

profile of v5, /device:TPU:0, one launch (start us, length us, event | category | flops | bytes accessed | tf_op | source)
XLA Modules:
  0.0 68.5 jit_solution(18369050374147081916)
XLA Ops:
  0.7 0.0 copy-start.5
  0.7 3.8 %shard_map.91 = (bf16[8,336,128]{2,1,0:T(8,128)(2,1)}, bf16[256,128]{1,0:T(8,128)(2,1)}, bf16[256,128]{1,0:T(8,128)(2,1)}, bf16[256,128]{1,0:T(8,128)(2,1)}, bf1...) custom-call(s32[1]{0:T(128)S(6)} %copy.10.refs_0_, ...), custom_call_target="tpu_custom_call" | custom-call | flops 4000000000 | bytes 1048576 | tf_op jit(solution)/shard_map/pallas_call | solution.py:369
  4.5 0.0 copy-start
  4.5 0.0 copy-start.4
  4.5 0.0 copy-start.1
  4.5 0.0 copy-start.2
  4.5 7.5 %all-to-all-start = ((bf16[8,336,128]{2,1,0:T(8,128)(2,1)}), bf16[8,336,128]{2,1,0:T(8,128)(2,1)S(1)}, u32[]{:S(2)}, u32[]{:S(2)}) async-start(bf16[8,336,128]{2,1,0:T(8,128)(2,1)} %get-tuple-element.21), calls=%async_computation | async-start | bytes 1376256 | tf_op jit(solution)/shard_map/all_to_all | solution.py:397
  12.0 2.0 %collective-permute-start.2 = (bf16[256,128]{1,0:T(8,128)(2,1)}, bf16[256,128]{1,0:T(8,128)(2,1)S(1)}, u32[]{:S(2)}, u32[]{:S(2)}) collective-permute-start(bf16[256,128]{1,0:T(8,128)(2,1)} %get-tuple-element.25), channel_id=1, source_target_pairs={{0,4},{4,0},{8,12},{12,8},{16,20},{20,16},{24,28},{28,24},{1,5},{5... | collective-permute-start | bytes 196616 | tf_op jit(solution)/shard_map/ppermute | solution.py:402
  14.0 1.5 %collective-permute-start.3 = (bf16[256,128]{1,0:T(8,128)(2,1)}, bf16[256,128]{1,0:T(8,128)(2,1)S(1)}, u32[]{:S(2)}, u32[]{:S(2)}) collective-permute-start(bf16[256,128]{1,0:T(8,128)(2,1)} %get-tuple-element.26), channel_id=1, source_target_pairs={{0,8},{4,12},{8,0},{12,4},{16,24},{20,28},{24,16},{28,20},{1,9},{5... | collective-permute-start | bytes 196616 | tf_op jit(solution)/shard_map/ppermute | solution.py:402
  15.4 0.0 collective-permute-start.4
  15.5 2.9 %collective-permute-start.5 = (bf16[256,128]{1,0:T(8,128)(2,1)}, bf16[256,128]{1,0:T(8,128)(2,1)S(1)}, u32[]{:S(2)}, u32[]{:S(2)}) collective-permute-start(bf16[256,128]{1,0:T(8,128)(2,1)} %get-tuple-element.28), channel_id=1, source_target_pairs={{0,16},{4,20},{8,24},{12,28},{16,0},{20,4},{24,8},{28,12},{1,17},{... | collective-permute-start | bytes 196616 | tf_op jit(solution)/shard_map/ppermute | solution.py:402
  18.4 1.5 %collective-permute-start.6 = (bf16[256,128]{1,0:T(8,128)(2,1)}, bf16[256,128]{1,0:T(8,128)(2,1)S(1)}, u32[]{:S(2)}, u32[]{:S(2)}) collective-permute-start(bf16[256,128]{1,0:T(8,128)(2,1)} %get-tuple-element.29), channel_id=1, source_target_pairs={{0,20},{4,16},{8,28},{12,24},{16,4},{20,0},{24,12},{28,8},{1,21},{... | collective-permute-start | bytes 196616 | tf_op jit(solution)/shard_map/ppermute | solution.py:402
  19.8 0.0 copy-done.5
  19.8 0.1 collective-permute-done.2.refs_1_
  19.9 4.2 %collective-permute-start.7 = (bf16[256,128]{1,0:T(8,128)(2,1)}, bf16[256,128]{1,0:T(8,128)(2,1)S(1)}, u32[]{:S(2)}, u32[]{:S(2)}) collective-permute-start(bf16[256,128]{1,0:T(8,128)(2,1)} %get-tuple-element.30), channel_id=1, source_target_pairs={{0,24},{4,28},{8,16},{12,20},{16,8},{20,12},{24,0},{28,4},{1,25},{... | collective-permute-start | bytes 196616 | tf_op jit(solution)/shard_map/ppermute | solution.py:402
  24.1 1.7 %collective-permute-done.3.refs_2_ = bf16[256,128]{1,0:T(8,128)(2,1)S(1)} collective-permute-done((bf16[256,128]{1,0:T(8,128)(2,1)}, bf16[256,128]{1,0:T(8,128)(2,1)S(1)}, u32[]{:S(2)}, u32[]{:S(2)}) %collective-permute-start.3) | collective-permute-done | bytes 65568 | tf_op jit(solution)/shard_map/ppermute | solution.py:402
  25.8 0.0 copy-done.4
  25.8 4.8 %collective-permute-start.8 = (bf16[256,128]{1,0:T(8,128)(2,1)S(1)}, bf16[256,128]{1,0:T(8,128)(2,1)S(1)}, u32[]{:S(2)}, u32[]{:S(2)}) collective-permute-start(bf16[256,128]{1,0:T(8,128)(2,1)S(1)} %copy-done.4), channel_id=1, source_target_pairs={{0,28},{4,24},{8,20},{12,16},{16,12},{20,8},{24,4},{28,0},{1,29},{... | collective-permute-start | bytes 196616 | tf_op jit(solution)/shard_map/ppermute | solution.py:402
  30.6 6.4 %all-to-all-done.refs_0_ = bf16[8,336,128]{2,1,0:T(8,128)(2,1)S(1)} async-done(((bf16[8,336,128]{2,1,0:T(8,128)(2,1)}), bf16[8,336,128]{2,1,0:T(8,128)(2,1)S(1)}, u32[]{:S(2)}, u32[]{:S(2)}) %all-to-all-start) | async-done | bytes 688160 | tf_op jit(solution)/shard_map/all_to_all | solution.py:397
  37.0 0.0 copy-done
  37.0 0.0 copy-done.1
  37.0 0.0 copy-done.2
  37.0 0.0 copy-start.3
  37.0 11.6 %shard_map.92 = (bf16[2,12,40,128]{3,2,1,0:T(8,128)(2,1)S(1)}, bf16[2,12,40,128]{3,2,1,0:T(8,128)(2,1)S(1)}, f32[8,512]{1,0:T(8,128)S(1)}, bf16[512,128]{1,0:T(8,128)(2,1)S(1)}, bf16[512,128]{1,0:T(8,128)(2,1)S(1)}) custom-call(bf16[8,336,128]{2,1,0:T(8,128)(2,1)S(1)} %all-to-all-done.refs_0_, bf16[256,256]{1,0:T(8,128)(2,1)S(1)} %copy-done.2, ...), custom_call_target="tpu_custom_call" | custom-call | flops 16000000000 | bytes 1048576 | tf_op jit(solution)/shard_map/pallas_call | solution.py:427
  48.6 0.0 collective-permute-done.4.refs_3_
  48.6 0.0 collective-permute-done.5.refs_4_
  48.6 0.0 collective-permute-done.6.refs_5_
  48.6 0.0 collective-permute-done.7.refs_6_
  48.7 0.0 collective-permute-done.8.refs_7_
  48.7 0.0 copy-done.3
  48.7 9.3 %shard_map.93 = (bf16[2,9,40,128]{3,2,1,0:T(8,128)(2,1)S(1)}, bf16[2,9,40,128]{3,2,1,0:T(8,128)(2,1)S(1)}) custom-call(bf16[256,128]{1,0:T(8,128)(2,1)S(1)} %copy-done.3, bf16[256,128]{1,0:T(8,128)(2,1)S(1)} %collective-permute-done.2.refs_1_, bf16[256,128]{1,0:T(8,128)(2,1)S(1)} %collective-permute-done.3.refs_2_, ...), custom_call_target="tpu_custom_call" | custom-call | flops 16000000000 | bytes 1048576 | tf_op jit(solution)/shard_map/pallas_call | solution.py:427
  58.0 0.1 collective-permute-start.9
  58.1 0.5 collective-permute-start
  58.6 0.9 %collective-permute-done.9 = bf16[2,9,40,128]{3,2,1,0:T(8,128)(2,1)S(1)} collective-permute-done((bf16[2,9,40,128]{3,2,1,0:T(8,128)(2,1)S(1)}, bf16[2,9,40,128]{3,2,1,0:T(8,128)(2,1)S(1)}, u32[]{:S(2)}, u32[]{:S(2)}) %collective-permute-start.9) | collective-permute-done | bytes 184352 | tf_op jit(solution)/shard_map/ppermute | solution.py:339
  59.5 0.1 add_convert_fusion.1
  59.6 0.3 collective-permute-done
  59.9 0.1 add_convert_fusion
  60.0 1.6 %collective-permute-start.1 = (bf16[1,12,40,128]{3,2,1,0:T(8,128)(2,1)S(1)}, bf16[1,12,40,128]{3,2,1,0:T(8,128)(2,1)S(1)}, u32[]{:S(2)}, u32[]{:S(2)}) collective-permute-start(bf16[1,12,40,128]{3,2,1,0:T(8,128)(2,1)S(1)} %get-tuple-element.37), channel_id=1, source_target_pairs={{0,2},{1,3},{2,0},{3,1},{4,6},{5,7},{6,4},{7,5},{8,10},{9,11},{10,... | collective-permute-start | bytes 368648 | tf_op jit(solution)/shard_map/ppermute | solution.py:339
  61.5 0.6 collective-permute-start.10
  62.2 5.3 %collective-permute-done.10 = bf16[1,9,40,128]{3,2,1,0:T(8,128)(2,1)S(1)} collective-permute-done((bf16[1,9,40,128]{3,2,1,0:T(8,128)(2,1)S(1)}, bf16[1,9,40,128]{3,2,1,0:T(8,128)(2,1)S(1)}, u32[]{:S(2)}, u32[]{:S(2)}) %collective-permute-start.10) | collective-permute-done | bytes 92192 | tf_op jit(solution)/shard_map/ppermute | solution.py:339
  67.5 0.0 collective-permute-done.1
  67.5 1.0 %shard_map.94 = f32[18,36,144]{2,1,0:T(8,128)} custom-call(bf16[12,40,128]{2,1,0:T(8,128)(2,1)S(1)} %get-tuple-element.38.refs_0_, bf16[12,40,128]{2,1,0:T(8,128)(2,1)S(1)} %bitcast.7, bf16[9,40,128]{2,1,0:T(8,128)(2,1)S(1)} %get-tuple-element.40.refs_2_, bf16[9,40,128]{2,1,0:T(8,128)(2,1)S(1)} %bitcast.8), custom_call_target="tpu_custom_call" | custom-call | flops 1 | bytes 1048576 | tf_op jit(solution)/shard_map/pallas_call | solution.py:431
  (3 shorter events, 0.1 us)
Async XLA Ops:
  0.7 19.2 %copy-start.5 = (f32[12]{0:T(128)S(1)}, f32[12]{0:T(128)}, u32[]{:S(2)}) copy-start(f32[12]{0:T(128)} %param.10) | copy-start | bytes 148
  4.5 32.5 %copy-start = (bf16[2048,256]{1,0:T(8,128)(2,1)S(1)}, bf16[2048,256]{1,0:T(8,128)(2,1)}, u32[]{:S(2)}) copy-start(bf16[2048,256]{1,0:T(8,128)(2,1)} %constant.34.clone.refs_2_.refs_9_) | copy-start | bytes 3145732
  4.5 21.3 %copy-start.4 = (bf16[256,128]{1,0:T(8,128)(2,1)S(1)}, bf16[256,128]{1,0:T(8,128)(2,1)}, u32[]{:S(2)}) copy-start(bf16[256,128]{1,0:T(8,128)(2,1)} %get-tuple-element.31) | copy-start | bytes 196612
  4.5 32.5 %copy-start.1 = (bf16[288,144]{1,0:T(8,128)(2,1)S(1)}, bf16[288,144]{1,0:T(8,128)(2,1)}, u32[]{:S(2)}) copy-start(bf16[288,144]{1,0:T(8,128)(2,1)} %constant.35.clone.refs_3_.refs_10_) | copy-start | bytes 248836
  4.5 32.5 %copy-start.2 = (bf16[256,256]{1,0:T(8,128)(2,1)S(1)}, bf16[256,256]{1,0:T(8,128)(2,1)}, u32[]{:S(2)}) copy-start(bf16[256,256]{1,0:T(8,128)(2,1)} %constant.33.clone.refs_1_.refs_8_) | copy-start | bytes 393220
  4.5 32.5 %all-to-all-start = ((bf16[8,336,128]{2,1,0:T(8,128)(2,1)}), bf16[8,336,128]{2,1,0:T(8,128)(2,1)S(1)}, u32[]{:S(2)}, u32[]{:S(2)}) async-start(bf16[8,336,128]{2,1,0:T(8,128)(2,1)} %get-tuple-element.21), calls=%async_computation | async-start | bytes 1376256 | tf_op jit(solution)/shard_map/all_to_all | solution.py:397
  12.0 8.0 %collective-permute-start.2 = (bf16[256,128]{1,0:T(8,128)(2,1)}, bf16[256,128]{1,0:T(8,128)(2,1)S(1)}, u32[]{:S(2)}, u32[]{:S(2)}) collective-permute-start(bf16[256,128]{1,0:T(8,128)(2,1)} %get-tuple-element.25), channel_id=1, source_target_pairs={{0,4},{4,0},{8,12},{12,8},{16,20},{20,16},{24,28},{28,24},{1,5},{5... | collective-permute-start | bytes 196616 | tf_op jit(solution)/shard_map/ppermute | solution.py:402
  14.0 11.8 %collective-permute-start.3 = (bf16[256,128]{1,0:T(8,128)(2,1)}, bf16[256,128]{1,0:T(8,128)(2,1)S(1)}, u32[]{:S(2)}, u32[]{:S(2)}) collective-permute-start(bf16[256,128]{1,0:T(8,128)(2,1)} %get-tuple-element.26), channel_id=1, source_target_pairs={{0,8},{4,12},{8,0},{12,4},{16,24},{20,28},{24,16},{28,20},{1,9},{5... | collective-permute-start | bytes 196616 | tf_op jit(solution)/shard_map/ppermute | solution.py:402
  15.4 33.2 %collective-permute-start.4 = (bf16[256,128]{1,0:T(8,128)(2,1)}, bf16[256,128]{1,0:T(8,128)(2,1)S(1)}, u32[]{:S(2)}, u32[]{:S(2)}) collective-permute-start(bf16[256,128]{1,0:T(8,128)(2,1)} %get-tuple-element.27), channel_id=1, source_target_pairs={{0,12},{4,8},{8,4},{12,0},{16,28},{20,24},{24,20},{28,16},{1,13},{... | collective-permute-start | bytes 196616 | tf_op jit(solution)/shard_map/ppermute | solution.py:402
  15.5 33.2 %collective-permute-start.5 = (bf16[256,128]{1,0:T(8,128)(2,1)}, bf16[256,128]{1,0:T(8,128)(2,1)S(1)}, u32[]{:S(2)}, u32[]{:S(2)}) collective-permute-start(bf16[256,128]{1,0:T(8,128)(2,1)} %get-tuple-element.28), channel_id=1, source_target_pairs={{0,16},{4,20},{8,24},{12,28},{16,0},{20,4},{24,8},{28,12},{1,17},{... | collective-permute-start | bytes 196616 | tf_op jit(solution)/shard_map/ppermute | solution.py:402
  18.4 30.3 %collective-permute-start.6 = (bf16[256,128]{1,0:T(8,128)(2,1)}, bf16[256,128]{1,0:T(8,128)(2,1)S(1)}, u32[]{:S(2)}, u32[]{:S(2)}) collective-permute-start(bf16[256,128]{1,0:T(8,128)(2,1)} %get-tuple-element.29), channel_id=1, source_target_pairs={{0,20},{4,16},{8,28},{12,24},{16,4},{20,0},{24,12},{28,8},{1,21},{... | collective-permute-start | bytes 196616 | tf_op jit(solution)/shard_map/ppermute | solution.py:402
  19.9 28.7 %collective-permute-start.7 = (bf16[256,128]{1,0:T(8,128)(2,1)}, bf16[256,128]{1,0:T(8,128)(2,1)S(1)}, u32[]{:S(2)}, u32[]{:S(2)}) collective-permute-start(bf16[256,128]{1,0:T(8,128)(2,1)} %get-tuple-element.30), channel_id=1, source_target_pairs={{0,24},{4,28},{8,16},{12,20},{16,8},{20,12},{24,0},{28,4},{1,25},{... | collective-permute-start | bytes 196616 | tf_op jit(solution)/shard_map/ppermute | solution.py:402
  25.8 22.8 %collective-permute-start.8 = (bf16[256,128]{1,0:T(8,128)(2,1)S(1)}, bf16[256,128]{1,0:T(8,128)(2,1)S(1)}, u32[]{:S(2)}, u32[]{:S(2)}) collective-permute-start(bf16[256,128]{1,0:T(8,128)(2,1)S(1)} %copy-done.4), channel_id=1, source_target_pairs={{0,28},{4,24},{8,20},{12,16},{16,12},{20,8},{24,4},{28,0},{1,29},{... | collective-permute-start | bytes 196616 | tf_op jit(solution)/shard_map/ppermute | solution.py:402
  37.0 11.7 %copy-start.3 = (bf16[256,128]{1,0:T(8,128)(2,1)S(1)}, bf16[256,128]{1,0:T(8,128)(2,1)}, u32[]{:S(2)}) copy-start(bf16[256,128]{1,0:T(8,128)(2,1)} %get-tuple-element.24.refs_0_) | copy-start | bytes 196612
  58.0 1.5 %collective-permute-start.9 = (bf16[2,9,40,128]{3,2,1,0:T(8,128)(2,1)S(1)}, bf16[2,9,40,128]{3,2,1,0:T(8,128)(2,1)S(1)}, u32[]{:S(2)}, u32[]{:S(2)}) collective-permute-start(bf16[2,9,40,128]{3,2,1,0:T(8,128)(2,1)S(1)} %get-tuple-element.36), channel_id=1, source_target_pairs={{0,1},{1,0},{2,3},{3,2},{4,5},{5,4},{6,7},{7,6},{8,9},{9,8},{10,11... | collective-permute-start | bytes 552968 | tf_op jit(solution)/shard_map/ppermute | solution.py:339
  58.1 1.8 %collective-permute-start = (bf16[2,12,40,128]{3,2,1,0:T(8,128)(2,1)S(1)}, bf16[2,12,40,128]{3,2,1,0:T(8,128)(2,1)S(1)}, u32[]{:S(2)}, u32[]{:S(2)}) collective-permute-start(bf16[2,12,40,128]{3,2,1,0:T(8,128)(2,1)S(1)} %get-tuple-element.23), channel_id=1, source_target_pairs={{0,1},{1,0},{2,3},{3,2},{4,5},{5,4},{6,7},{7,6},{8,9},{9,8},{10,11... | collective-permute-start | bytes 737288 | tf_op jit(solution)/shard_map/ppermute | solution.py:339
  60.0 7.5 %collective-permute-start.1 = (bf16[1,12,40,128]{3,2,1,0:T(8,128)(2,1)S(1)}, bf16[1,12,40,128]{3,2,1,0:T(8,128)(2,1)S(1)}, u32[]{:S(2)}, u32[]{:S(2)}) collective-permute-start(bf16[1,12,40,128]{3,2,1,0:T(8,128)(2,1)S(1)} %get-tuple-element.37), channel_id=1, source_target_pairs={{0,2},{1,3},{2,0},{3,1},{4,6},{5,7},{6,4},{7,5},{8,10},{9,11},{10,... | collective-permute-start | bytes 368648 | tf_op jit(solution)/shard_map/ppermute | solution.py:339
  61.5 5.9 %collective-permute-start.10 = (bf16[1,9,40,128]{3,2,1,0:T(8,128)(2,1)S(1)}, bf16[1,9,40,128]{3,2,1,0:T(8,128)(2,1)S(1)}, u32[]{:S(2)}, u32[]{:S(2)}) collective-permute-start(bf16[1,9,40,128]{3,2,1,0:T(8,128)(2,1)S(1)} %get-tuple-element.39), channel_id=1, source_target_pairs={{0,2},{1,3},{2,0},{3,1},{4,6},{5,7},{6,4},{7,5},{8,10},{9,11},{10,... | collective-permute-start | bytes 276488 | tf_op jit(solution)/shard_map/ppermute | solution.py:339

commit v6 on v5

--- a/solution.py
+++ b/solution.py
@@ -16,8 +16,8 @@
 TAIL = N - LANES
 SHARE = LANES // TAIL
 PAIRS = 12
-INFO = 16
-GROUPS = 3
+INFO = 8
+GROUPS = 4
 
 
 def wave_tables():
@@ -60,7 +60,7 @@
 
 def lane_group(rows, dtype):
     group = lax.broadcasted_iota(jnp.int32, (rows, LANES), 1) // 32
-    return [(group == g).astype(jnp.float32).astype(dtype) for g in range(GROUPS + 1)]
+    return [(group == g).astype(jnp.float32).astype(dtype) for g in range(GROUPS)]
 
 
 def stick_kernel(planes, ranks, *refs):
@@ -128,29 +128,25 @@
     gx = jnp.floor((c + 0.5) * (1.0 / GB))
     row = lax.broadcasted_iota(jnp.int32, (INFO, slots), 0)
     live = count_here[0].astype(jnp.float32)
-    info = jnp.where(
-        row == 0, gx, jnp.where(row == 1, c - GB * gx, jnp.where(row == 2, live, 0.0))
-    )
+    info = jnp.where(row % 3 == 0, gx, jnp.where(row % 3 == 1, c - GB * gx, live))
     ends[...] = jnp.zeros_like(ends)
     ends[:, : slots - LANES] = info[:, LANES:]
-    tail_info = pltpu.roll(ends[...], 96, 1)
-
-    for c, (main, rest) in enumerate(zip(mains, rests)):
-        rows = main.shape[1]
-        span = rows // GROUPS
+    row = lax.broadcasted_iota(jnp.int32, (INFO, LANES), 0)
+    info = jnp.where(row < 3, info[:, :LANES], jnp.where(row < 5, ends[...], 0.0))
+
+    for c, (main, rest, count) in enumerate(zip(mains, rests, planes)):
+        rows = 2 * count * bands
+        span = main.shape[1] // GROUPS
         masks = lane_group(span, jnp.float32)
         at = rows + (INFO if c == 0 else 0)
         for k in range(ranks):
             out, d = (outs[0].at[k], k) if c == 0 else (outs[1 + (c - 1) * ranks + k], me ^ k)
-            out[:rows, :] = main[d].astype(jnp.bfloat16)
+            out[:rows, :] = main[d, :rows, :].astype(jnp.bfloat16)
             packed = rest[d, :span, :] * masks[0]
             for g in range(1, GROUPS):
                 packed = packed + rest[d, g * span : (g + 1) * span, :] * masks[g]
             if c == 0:
-                out[rows:at, :] = info[:, :LANES].astype(jnp.bfloat16)
-                packed = packed + jnp.concatenate(
-                    [tail_info, jnp.zeros((span - INFO, LANES), jnp.float32)], axis=0
-                )
+                out[rows:at, :] = info.astype(jnp.bfloat16)
             out[at:, :] = packed.astype(jnp.bfloat16)
 
 
@@ -164,9 +160,9 @@
         me = lax.axis_index("fft")
         source = lambda k: pl.ds(me ^ k, 1)
     lhs, pick, sticks, real, imag, both, half, tail, acc, acc_tail = refs[11:]
-    rows = GROUPS * span
+    live = planes * bands
+    rows = 2 * live
     total = rows + INFO if first else rows
-    live = planes * bands
     cap = turn.shape[1]
 
     if first:
@@ -180,18 +176,26 @@
 
     masks = lane_group(span, jnp.bfloat16)
     k = lax.broadcasted_iota(jnp.int32, (2 * LANES, cap), 0)
-    slot = jnp.where(k < LANES, k, LANES + k % 32).astype(jnp.float32)
+    slot = jnp.where(k < LANES, k, LANES + k % 32).astype(jnp.float32).astype(jnp.bfloat16)
+    one, zero = jnp.ones((), jnp.bfloat16), jnp.zeros((), jnp.bfloat16)
+    if first:
+        info_row = lax.broadcasted_iota(jnp.int32, (INFO, LANES), 0)
+        info_main = (info_row < 3).astype(jnp.float32).astype(jnp.bfloat16)
     for src in range(ranks):
         at = src * 2 * LANES
-        pick[at : at + 2 * LANES, :] = jnp.where(slot == turn[source(src), :], 1.0, 0.0).astype(
-            jnp.bfloat16
-        )
-        packed = blocks[src][total : total + span, :]
-        pieces = [packed * masks[g] for g in range(GROUPS)]
+        wanted = jnp.broadcast_to(turn[source(src), :].astype(jnp.bfloat16), slot.shape)
+        pick[at : at + 2 * LANES, :] = jnp.where(slot == wanted, one, zero)
+        block, low, high = blocks[src], slice(at, at + LANES), slice(at + LANES, at + 2 * LANES)
+        lhs[:rows, low] = block[:rows, :]
+        packed = block[total : total + span, :]
+        for g in range(GROUPS):
+            here = slice(g * span, min(rows, (g + 1) * span))
+            if here.start < here.stop:
+                lhs[here, high] = (packed * masks[g])[: here.stop - here.start]
         if first:
-            pieces.append((packed * masks[GROUPS])[:INFO])
-        lhs[:, at : at + LANES] = blocks[src][:total, :]
-        lhs[:, at + LANES : at + 2 * LANES] = jnp.concatenate(pieces, axis=0)
+            info = block[rows:total, :]
+            lhs[rows:, low] = info * info_main
+            lhs[rows:, high] = info * (one - info_main)
     compact = jnp.dot(lhs[...], pick[...], preferred_element_type=jnp.float32)
     sticks[...] = compact[:rows].astype(jnp.bfloat16)
 
@@ -200,8 +204,9 @@
             [compact[rows:], jnp.zeros((LANES - INFO, cap), jnp.float32)], axis=0
         ).T
         lane = lax.broadcasted_iota(jnp.int32, (cap, LANES), 1).astype(jnp.float32)
-        gx_of[...] = jnp.broadcast_to(info[:, 0:1], (cap, LANES)).astype(jnp.bfloat16)
-        gy_hot[...] = jnp.where(info[:, 1:2] == lane, 1.0, 0.0).astype(jnp.bfloat16)
+        gx, gy = (info[:, i : i + 1] + info[:, i + 3 : i + 4] for i in range(2))
+        gx_of[...] = jnp.broadcast_to(gx, (cap, LANES)).astype(jnp.bfloat16)
+        gy_hot[...] = jnp.where(gy == lane, 1.0, 0.0).astype(jnp.bfloat16)
 
     def put(step, carry):
         for u in range(PAIRS):
@@ -252,7 +257,7 @@
         for b in range(bands):
             tail[t, b] = stacked(h[b * GB : (b + 1) * GB])
 
-    wide = largest(bands, 4)
+    wide = largest(bands, 6)
 
     def columns_of(step, carry):
         pieces = []
@@ -353,8 +358,7 @@
     owners = lax.axis_size("band")
     slots = columns.shape[0]
     held = plane_slot.shape[0] // ranks
-    last = min(SHARE, held // 2)
-    planes = (held - last, last)
+    planes = (held // 3, held - held // 3)
     cap = up(ranks * slots * 2 // 5, LANES)
     own_rows = N // owners
     bf16, f32 = jnp.bfloat16, jnp.float32
@@ -363,13 +367,14 @@
     core = (lax.axis_index("band") & 1)[None]
     tables = wave_tables()
 
-    spans = [up(-(-2 * count * bands // GROUPS), 16) for count in planes]
+    spans = [up(-(-2 * count * bands // GROUPS), 8) for count in planes]
+    rows = [2 * count * bands for count in planes]
     fixed = stick_constants(planes, ranks)
     stride = up(slots, 8) + 8
     outgoing = vmem_call(
         functools.partial(stick_kernel, planes, ranks),
-        [jax.ShapeDtypeStruct((ranks, 4 * spans[0] + INFO, LANES), bf16)]
-        + [jax.ShapeDtypeStruct((4 * spans[1], LANES), bf16)] * ranks,
+        [jax.ShapeDtypeStruct((ranks, rows[0] + spans[0] + INFO, LANES), bf16)]
+        + [jax.ShapeDtypeStruct((rows[1] + spans[1], LANES), bf16)] * ranks,
         5,
         [
             pltpu.SMEM(counts.shape, jnp.int32),
@@ -400,7 +405,6 @@
             for k in range(1, ranks):
                 pairs = [(i, i ^ k) for i in range(ranks)]
                 received.append(lax.ppermute(outgoing[1 + k], "fft", pairs))
-        rows = GROUPS * span
         tails = -(-count // SHARE)
         dens_shape = jax.ShapeDtypeStruct(
             (owners // 2, count + tails, up(own_rows, 8), LANES), bf16
@@ -410,9 +414,9 @@
             [dens_shape] * 2 + (kept_shapes if first else []),
             len(received) + (5 if first else 8),
             [
-                pltpu.VMEM((rows + (INFO if first else 0), ranks * 2 * LANES), bf16),
+                pltpu.VMEM((rows[c] + (INFO if first else 0), ranks * 2 * LANES), bf16),
                 pltpu.VMEM((ranks * 2 * LANES, cap), bf16),
-                pltpu.VMEM((rows, cap), bf16),
+                pltpu.VMEM((rows[c], cap), bf16),
                 pltpu.VMEM((count * bands * GB, LANES), f32),
                 pltpu.VMEM((count * bands * GB, LANES), f32),
                 pltpu.VMEM((count, bands * GB, 2 * LANES), bf16),

time: 68.7 us -> 61 us (0.89)
  waiting for transfers between devices: 14.7 us -> 10.7 us
  starting transfers between devices: 27 us -> 23.2 us
    all_to_all x1, waiting for transfers between devices: 6.4 us -> 0.01 us  [shards(): lax.all_to_all(outgoing[0], 'fft', split_axis=0, concat_axis=0, tiled=True)]
    ppermute x7, starting transfers between devices: 16.9 us -> 13.4 us  [shards(): received.append(lax.ppermute(outgoing[1 + k], 'fft', pairs))]
    ppermute x7, waiting for transfers between devices: 1.78 us -> 3.92 us  [shards(): received.append(lax.ppermute(outgoing[1 + k], 'fft', pairs))]
  transfers between devices with their start and end apart: 12 -> 12, of which waited for: 6 -> 4; matrix products, arithmetic and copies ran while one was open for 0% -> 0% of each run, Pallas kernels for 17% -> 34%
where the time goes in v6:
time: 61 us; the launch traced here: 60.3 us
  Pallas kernels  25.3 us (41%)
  starting transfers between devices  23.2 us (38%)
  waiting for transfers between devices  10.7 us (18%)
  between operations  0.85 us (1%)
    pallas_call x2, Pallas kernels, shards(): results = run(*received, *tables, weight, core, *kept)  20.5 us
    ppermute x7, starting transfers between devices, shards(): received.append(lax.ppermute(outgoing[1 + k], 'fft', pairs))  13.4 us
    all_to_all x1, starting transfers between devices, shards(): lax.all_to_all(outgoing[0], 'fft', split_axis=0, concat_axis=0, tiled=True)  7.45 us
    ppermute x4, waiting for transfers between devices, halve(): got = lax.ppermute(send, axis, partners(axis, bit))  6.73 us
    ppermute x7, waiting for transfers between devices, shards(): received.append(lax.ppermute(outgoing[1 + k], 'fft', pairs))  3.92 us
    pallas_call x1, Pallas kernels, shards(): vmem_call(functools.partial(stick_kernel, planes, ranks), [jax.ShapeDtype...  3.8 us
    ppermute x4, starting transfers between devices, halve(): got = lax.ppermute(send, axis, partners(axis, bit))  2.29 us
  transfers between devices with their start and end apart: 12, of which 4 were waited for; matrix products, arithmetic and copies ran while one was open for 0% of the time, Pallas kernels for 34%

profile of v6, /device:TPU:0, one launch (start us, length us, event | category | flops | bytes accessed | tf_op | source)
XLA Modules:
  0.0 60.3 jit_solution(7453278120861856602)
XLA Ops:
  0.7 0.0 copy-start
  0.7 3.8 %shard_map.91 = (bf16[8,192,128]{2,1,0:T(8,128)(2,1)}, bf16[360,128]{1,0:T(8,128)(2,1)}, bf16[360,128]{1,0:T(8,128)(2,1)}, bf16[360,128]{1,0:T(8,128)(2,1)}, bf1...) custom-call(s32[1]{0:T(128)S(6)} %copy.10.refs_0_, ...), custom_call_target="tpu_custom_call" | custom-call | flops 4000000000 | bytes 1048576 | tf_op jit(solution)/shard_map/pallas_call | solution.py:374
  4.5 0.0 copy-start.8
  4.5 0.0 copy-start.7
  4.5 0.0 copy-start.6
  4.5 0.0 copy-start.5
  4.5 0.0 copy-start.4
  4.5 0.0 copy-start.1
  4.5 0.0 copy-start.2
  4.5 7.5 %all-to-all-start = ((bf16[8,192,128]{2,1,0:T(8,128)(2,1)}), bf16[8,192,128]{2,1,0:T(8,128)(2,1)S(1)}, u32[]{:S(2)}, u32[]{:S(2)}) async-start(bf16[8,192,128]{2,1,0:T(8,128)(2,1)} %get-tuple-element.21), calls=%async_computation | async-start | bytes 786432 | tf_op jit(solution)/shard_map/all_to_all | solution.py:402
  12.0 2.0 %collective-permute-start.2 = (bf16[360,128]{1,0:T(8,128)(2,1)}, bf16[360,128]{1,0:T(8,128)(2,1)S(1)}, u32[]{:S(2)}, u32[]{:S(2)}) collective-permute-start(bf16[360,128]{1,0:T(8,128)(2,1)} %get-tuple-element.25), channel_id=1, source_target_pairs={{0,4},{4,0},{8,12},{12,8},{16,20},{20,16},{24,28},{28,24},{1,5},{5... | collective-permute-start | bytes 276488 | tf_op jit(solution)/shard_map/ppermute | solution.py:407
  14.0 1.5 %collective-permute-start.3 = (bf16[360,128]{1,0:T(8,128)(2,1)}, bf16[360,128]{1,0:T(8,128)(2,1)S(1)}, u32[]{:S(2)}, u32[]{:S(2)}) collective-permute-start(bf16[360,128]{1,0:T(8,128)(2,1)} %get-tuple-element.26), channel_id=1, source_target_pairs={{0,8},{4,12},{8,0},{12,4},{16,24},{20,28},{24,16},{28,20},{1,9},{5... | collective-permute-start | bytes 276488 | tf_op jit(solution)/shard_map/ppermute | solution.py:407
  15.5 0.0 copy-done.8
  15.5 0.0 collective-permute-start.4
  15.5 0.0 copy-done.7
  15.5 0.0 copy-start.9
  15.5 2.9 %collective-permute-start.5 = (bf16[360,128]{1,0:T(8,128)(2,1)S(1)}, bf16[360,128]{1,0:T(8,128)(2,1)S(1)}, u32[]{:S(2)}, u32[]{:S(2)}) collective-permute-start(bf16[360,128]{1,0:T(8,128)(2,1)S(1)} %copy-done.7), channel_id=1, source_target_pairs={{0,16},{4,20},{8,24},{12,28},{16,0},{20,4},{24,8},{28,12},{1,17},{... | collective-permute-start | bytes 276488 | tf_op jit(solution)/shard_map/ppermute | solution.py:407
  18.4 0.0 copy-done.6
  18.4 1.5 %collective-permute-start.6 = (bf16[360,128]{1,0:T(8,128)(2,1)S(1)}, bf16[360,128]{1,0:T(8,128)(2,1)S(1)}, u32[]{:S(2)}, u32[]{:S(2)}) collective-permute-start(bf16[360,128]{1,0:T(8,128)(2,1)S(1)} %copy-done.6), channel_id=1, source_target_pairs={{0,20},{4,16},{8,28},{12,24},{16,4},{20,0},{24,12},{28,8},{1,21},{... | collective-permute-start | bytes 276488 | tf_op jit(solution)/shard_map/ppermute | solution.py:407
  19.9 0.0 copy-done.9
  19.9 0.0 collective-permute-done.2.refs_1_
  19.9 0.0 copy-done.5
  19.9 3.9 %collective-permute-start.7 = (bf16[360,128]{1,0:T(8,128)(2,1)S(1)}, bf16[360,128]{1,0:T(8,128)(2,1)S(1)}, u32[]{:S(2)}, u32[]{:S(2)}) collective-permute-start(bf16[360,128]{1,0:T(8,128)(2,1)S(1)} %copy-done.5), channel_id=1, source_target_pairs={{0,24},{4,28},{8,16},{12,20},{16,8},{20,12},{24,0},{28,4},{1,25},{... | collective-permute-start | bytes 276488 | tf_op jit(solution)/shard_map/ppermute | solution.py:407
  23.8 1.9 %collective-permute-done.3.refs_2_ = bf16[360,128]{1,0:T(8,128)(2,1)S(1)} collective-permute-done((bf16[360,128]{1,0:T(8,128)(2,1)}, bf16[360,128]{1,0:T(8,128)(2,1)S(1)}, u32[]{:S(2)}, u32[]{:S(2)}) %collective-permute-start.3) | collective-permute-done | bytes 92192 | tf_op jit(solution)/shard_map/ppermute | solution.py:407
  25.7 0.0 copy-done.4
  25.7 1.7 %collective-permute-start.8 = (bf16[360,128]{1,0:T(8,128)(2,1)S(1)}, bf16[360,128]{1,0:T(8,128)(2,1)S(1)}, u32[]{:S(2)}, u32[]{:S(2)}) collective-permute-start(bf16[360,128]{1,0:T(8,128)(2,1)S(1)} %copy-done.4), channel_id=1, source_target_pairs={{0,28},{4,24},{8,20},{12,16},{16,12},{20,8},{24,4},{28,0},{1,29},{... | collective-permute-start | bytes 276488 | tf_op jit(solution)/shard_map/ppermute | solution.py:407
  27.4 0.0 all-to-all-done.refs_0_
  27.4 0.0 copy-done
  27.4 0.0 copy-done.1
  27.4 0.0 copy-done.2
  27.4 0.0 copy-start.3
  27.4 7.9 %shard_map.92 = (bf16[2,7,40,128]{3,2,1,0:T(8,128)(2,1)S(1)}, bf16[2,7,40,128]{3,2,1,0:T(8,128)(2,1)S(1)}, f32[8,512]{1,0:T(8,128)S(1)}, bf16[512,128]{1,0:T(8,128)(2,1)S(1)}, bf16[512,128]{1,0:T(8,128)(2,1)S(1)}) custom-call(bf16[8,192,128]{2,1,0:T(8,128)(2,1)S(1)} %all-to-all-done.refs_0_, bf16[256,256]{1,0:T(8,128)(2,1)S(1)} %copy-done.2, ...), custom_call_target="tpu_custom_call" | custom-call | flops 16000000000 | bytes 1048576 | tf_op jit(solution)/shard_map/pallas_call | solution.py:431
  35.3 0.0 collective-permute-done.4.refs_3_
  35.3 0.1 collective-permute-start
  35.4 0.0 collective-permute-done.5.refs_4_
  35.4 2.0 %collective-permute-done.6.refs_5_ = bf16[360,128]{1,0:T(8,128)(2,1)S(1)} collective-permute-done((bf16[360,128]{1,0:T(8,128)(2,1)S(1)}, bf16[360,128]{1,0:T(8,128)(2,1)S(1)}, u32[]{:S(2)}, u32[]{:S(2)}) %collective-permute-start.6) | collective-permute-done | bytes 92192 | tf_op jit(solution)/shard_map/ppermute | solution.py:407
  37.4 0.0 collective-permute-done.7.refs_6_
  37.4 0.0 collective-permute-done.8.refs_7_
  37.4 0.0 copy-done.3
  37.4 12.6 %shard_map.93 = (bf16[2,14,40,128]{3,2,1,0:T(8,128)(2,1)S(1)}, bf16[2,14,40,128]{3,2,1,0:T(8,128)(2,1)S(1)}) custom-call(bf16[360,128]{1,0:T(8,128)(2,1)S(1)} %copy-done.3, bf16[360,128]{1,0:T(8,128)(2,1)S(1)} %collective-permute-done.2.refs_1_, bf16[360,128]{1,0:T(8,128)(2,1)S(1)} %collective-permute-done.3.refs_2_, ...), custom_call_target="tpu_custom_call" | custom-call | flops 16000000000 | bytes 1048576 | tf_op jit(solution)/shard_map/pallas_call | solution.py:431
  50.1 0.1 collective-permute-start.9
  50.2 0.0 collective-permute-done
  50.2 1.5 %collective-permute-done.9 = bf16[2,14,40,128]{3,2,1,0:T(8,128)(2,1)S(1)} collective-permute-done((bf16[2,14,40,128]{3,2,1,0:T(8,128)(2,1)S(1)}, bf16[2,14,40,128]{3,2,1,0:T(8,128)(2,1)S(1)}, u32[]{:S(2)}, u32[]{:S(2)}) %collective-permute-start.9) | collective-permute-done | bytes 286752 | tf_op jit(solution)/shard_map/ppermute | solution.py:344
  51.7 0.1 add_convert_fusion
  51.8 1.6 %collective-permute-start.10 = (bf16[1,14,40,128]{3,2,1,0:T(8,128)(2,1)S(1)}, bf16[1,14,40,128]{3,2,1,0:T(8,128)(2,1)S(1)}, u32[]{:S(2)}, u32[]{:S(2)}) collective-permute-start(bf16[1,14,40,128]{3,2,1,0:T(8,128)(2,1)S(1)} %get-tuple-element.37), channel_id=1, source_target_pairs={{0,2},{1,3},{2,0},{3,1},{4,6},{5,7},{6,4},{7,5},{8,10},{9,11},{10,... | collective-permute-start | bytes 430088 | tf_op jit(solution)/shard_map/ppermute | solution.py:344
  53.4 0.6 collective-permute-start.1
  54.0 5.2 %collective-permute-done.1 = bf16[1,7,40,128]{3,2,1,0:T(8,128)(2,1)S(1)} collective-permute-done((bf16[1,7,40,128]{3,2,1,0:T(8,128)(2,1)S(1)}, bf16[1,7,40,128]{3,2,1,0:T(8,128)(2,1)S(1)}, u32[]{:S(2)}, u32[]{:S(2)}) %collective-permute-start.1) | collective-permute-done | bytes 71712 | tf_op jit(solution)/shard_map/ppermute | solution.py:344
  59.2 0.0 collective-permute-done.10
  59.2 1.0 %shard_map.94 = f32[18,36,144]{2,1,0:T(8,128)} custom-call(bf16[7,40,128]{2,1,0:T(8,128)(2,1)S(1)} %get-tuple-element.40.refs_0_, bf16[7,40,128]{2,1,0:T(8,128)(2,1)S(1)} %bitcast.8, bf16[14,40,128]{2,1,0:T(8,128)(2,1)S(1)} %get-tuple-element.38.refs_2_, bf16[14,40,128]{2,1,0:T(8,128)(2,1)S(1)} %bitcast.7), custom_call_target="tpu_custom_call" | custom-call | flops 1 | bytes 1048576 | tf_op jit(solution)/shard_map/pallas_call | solution.py:435
  (4 shorter events, 0.1 us)
Async XLA Ops:
  0.7 26.7 %copy-start = (bf16[2048,256]{1,0:T(8,128)(2,1)S(1)}, bf16[2048,256]{1,0:T(8,128)(2,1)}, u32[]{:S(2)}) copy-start(bf16[2048,256]{1,0:T(8,128)(2,1)} %constant.34.clone.refs_2_.refs_9_) | copy-start | bytes 3145732
  4.5 11.0 %copy-start.8 = (bf16[360,128]{1,0:T(8,128)(2,1)S(1)}, bf16[360,128]{1,0:T(8,128)(2,1)}, u32[]{:S(2)}) copy-start(bf16[360,128]{1,0:T(8,128)(2,1)} %get-tuple-element.27) | copy-start | bytes 276484
  4.5 11.0 %copy-start.7 = (bf16[360,128]{1,0:T(8,128)(2,1)S(1)}, bf16[360,128]{1,0:T(8,128)(2,1)}, u32[]{:S(2)}) copy-start(bf16[360,128]{1,0:T(8,128)(2,1)} %get-tuple-element.28) | copy-start | bytes 276484
  4.5 13.9 %copy-start.6 = (bf16[360,128]{1,0:T(8,128)(2,1)S(1)}, bf16[360,128]{1,0:T(8,128)(2,1)}, u32[]{:S(2)}) copy-start(bf16[360,128]{1,0:T(8,128)(2,1)} %get-tuple-element.29) | copy-start | bytes 276484
  4.5 15.4 %copy-start.5 = (bf16[360,128]{1,0:T(8,128)(2,1)S(1)}, bf16[360,128]{1,0:T(8,128)(2,1)}, u32[]{:S(2)}) copy-start(bf16[360,128]{1,0:T(8,128)(2,1)} %get-tuple-element.30) | copy-start | bytes 276484
  4.5 21.2 %copy-start.4 = (bf16[360,128]{1,0:T(8,128)(2,1)S(1)}, bf16[360,128]{1,0:T(8,128)(2,1)}, u32[]{:S(2)}) copy-start(bf16[360,128]{1,0:T(8,128)(2,1)} %get-tuple-element.31) | copy-start | bytes 276484
  4.5 22.9 %copy-start.1 = (bf16[288,144]{1,0:T(8,128)(2,1)S(1)}, bf16[288,144]{1,0:T(8,128)(2,1)}, u32[]{:S(2)}) copy-start(bf16[288,144]{1,0:T(8,128)(2,1)} %constant.35.clone.refs_3_.refs_10_) | copy-start | bytes 248836
  4.5 22.8 %copy-start.2 = (bf16[256,256]{1,0:T(8,128)(2,1)S(1)}, bf16[256,256]{1,0:T(8,128)(2,1)}, u32[]{:S(2)}) copy-start(bf16[256,256]{1,0:T(8,128)(2,1)} %constant.33.clone.refs_1_.refs_8_) | copy-start | bytes 393220
  4.5 22.8 %all-to-all-start = ((bf16[8,192,128]{2,1,0:T(8,128)(2,1)}), bf16[8,192,128]{2,1,0:T(8,128)(2,1)S(1)}, u32[]{:S(2)}, u32[]{:S(2)}) async-start(bf16[8,192,128]{2,1,0:T(8,128)(2,1)} %get-tuple-element.21), calls=%async_computation | async-start | bytes 786432 | tf_op jit(solution)/shard_map/all_to_all | solution.py:402
  12.0 7.9 %collective-permute-start.2 = (bf16[360,128]{1,0:T(8,128)(2,1)}, bf16[360,128]{1,0:T(8,128)(2,1)S(1)}, u32[]{:S(2)}, u32[]{:S(2)}) collective-permute-start(bf16[360,128]{1,0:T(8,128)(2,1)} %get-tuple-element.25), channel_id=1, source_target_pairs={{0,4},{4,0},{8,12},{12,8},{16,20},{20,16},{24,28},{28,24},{1,5},{5... | collective-permute-start | bytes 276488 | tf_op jit(solution)/shard_map/ppermute | solution.py:407
  14.0 11.7 %collective-permute-start.3 = (bf16[360,128]{1,0:T(8,128)(2,1)}, bf16[360,128]{1,0:T(8,128)(2,1)S(1)}, u32[]{:S(2)}, u32[]{:S(2)}) collective-permute-start(bf16[360,128]{1,0:T(8,128)(2,1)} %get-tuple-element.26), channel_id=1, source_target_pairs={{0,8},{4,12},{8,0},{12,4},{16,24},{20,28},{24,16},{28,20},{1,9},{5... | collective-permute-start | bytes 276488 | tf_op jit(solution)/shard_map/ppermute | solution.py:407
  15.5 19.8 %collective-permute-start.4 = (bf16[360,128]{1,0:T(8,128)(2,1)S(1)}, bf16[360,128]{1,0:T(8,128)(2,1)S(1)}, u32[]{:S(2)}, u32[]{:S(2)}) collective-permute-start(bf16[360,128]{1,0:T(8,128)(2,1)S(1)} %copy-done.8), channel_id=1, source_target_pairs={{0,12},{4,8},{8,4},{12,0},{16,28},{20,24},{24,20},{28,16},{1,13},{... | collective-permute-start | bytes 276488 | tf_op jit(solution)/shard_map/ppermute | solution.py:407
  15.5 4.4 %copy-start.9 = (f32[12]{0:T(128)S(1)}, f32[12]{0:T(128)}, u32[]{:S(2)}) copy-start(f32[12]{0:T(128)} %param.10) | copy-start | bytes 148
  15.5 19.9 %collective-permute-start.5 = (bf16[360,128]{1,0:T(8,128)(2,1)S(1)}, bf16[360,128]{1,0:T(8,128)(2,1)S(1)}, u32[]{:S(2)}, u32[]{:S(2)}) collective-permute-start(bf16[360,128]{1,0:T(8,128)(2,1)S(1)} %copy-done.7), channel_id=1, source_target_pairs={{0,16},{4,20},{8,24},{12,28},{16,0},{20,4},{24,8},{28,12},{1,17},{... | collective-permute-start | bytes 276488 | tf_op jit(solution)/shard_map/ppermute | solution.py:407
  18.4 19.0 %collective-permute-start.6 = (bf16[360,128]{1,0:T(8,128)(2,1)S(1)}, bf16[360,128]{1,0:T(8,128)(2,1)S(1)}, u32[]{:S(2)}, u32[]{:S(2)}) collective-permute-start(bf16[360,128]{1,0:T(8,128)(2,1)S(1)} %copy-done.6), channel_id=1, source_target_pairs={{0,20},{4,16},{8,28},{12,24},{16,4},{20,0},{24,12},{28,8},{1,21},{... | collective-permute-start | bytes 276488 | tf_op jit(solution)/shard_map/ppermute | solution.py:407
  19.9 17.5 %collective-permute-start.7 = (bf16[360,128]{1,0:T(8,128)(2,1)S(1)}, bf16[360,128]{1,0:T(8,128)(2,1)S(1)}, u32[]{:S(2)}, u32[]{:S(2)}) collective-permute-start(bf16[360,128]{1,0:T(8,128)(2,1)S(1)} %copy-done.5), channel_id=1, source_target_pairs={{0,24},{4,28},{8,16},{12,20},{16,8},{20,12},{24,0},{28,4},{1,25},{... | collective-permute-start | bytes 276488 | tf_op jit(solution)/shard_map/ppermute | solution.py:407
  25.7 11.7 %collective-permute-start.8 = (bf16[360,128]{1,0:T(8,128)(2,1)S(1)}, bf16[360,128]{1,0:T(8,128)(2,1)S(1)}, u32[]{:S(2)}, u32[]{:S(2)}) collective-permute-start(bf16[360,128]{1,0:T(8,128)(2,1)S(1)} %copy-done.4), channel_id=1, source_target_pairs={{0,28},{4,24},{8,20},{12,16},{16,12},{20,8},{24,4},{28,0},{1,29},{... | collective-permute-start | bytes 276488 | tf_op jit(solution)/shard_map/ppermute | solution.py:407
  27.4 10.1 %copy-start.3 = (bf16[360,128]{1,0:T(8,128)(2,1)S(1)}, bf16[360,128]{1,0:T(8,128)(2,1)}, u32[]{:S(2)}) copy-start(bf16[360,128]{1,0:T(8,128)(2,1)} %get-tuple-element.24.refs_0_) | copy-start | bytes 276484
  35.3 14.8 %collective-permute-start = (bf16[2,7,40,128]{3,2,1,0:T(8,128)(2,1)S(1)}, bf16[2,7,40,128]{3,2,1,0:T(8,128)(2,1)S(1)}, u32[]{:S(2)}, u32[]{:S(2)}) collective-permute-start(bf16[2,7,40,128]{3,2,1,0:T(8,128)(2,1)S(1)} %get-tuple-element.23), channel_id=1, source_target_pairs={{0,1},{1,0},{2,3},{3,2},{4,5},{5,4},{6,7},{7,6},{8,9},{9,8},{10,11... | collective-permute-start | bytes 430088 | tf_op jit(solution)/shard_map/ppermute | solution.py:344
  50.1 1.6 %collective-permute-start.9 = (bf16[2,14,40,128]{3,2,1,0:T(8,128)(2,1)S(1)}, bf16[2,14,40,128]{3,2,1,0:T(8,128)(2,1)S(1)}, u32[]{:S(2)}, u32[]{:S(2)}) collective-permute-start(bf16[2,14,40,128]{3,2,1,0:T(8,128)(2,1)S(1)} %get-tuple-element.36), channel_id=1, source_target_pairs={{0,1},{1,0},{2,3},{3,2},{4,5},{5,4},{6,7},{7,6},{8,9},{9,8},{10,11... | collective-permute-start | bytes 860168 | tf_op jit(solution)/shard_map/ppermute | solution.py:344
  51.8 7.4 %collective-permute-start.10 = (bf16[1,14,40,128]{3,2,1,0:T(8,128)(2,1)S(1)}, bf16[1,14,40,128]{3,2,1,0:T(8,128)(2,1)S(1)}, u32[]{:S(2)}, u32[]{:S(2)}) collective-permute-start(bf16[1,14,40,128]{3,2,1,0:T(8,128)(2,1)S(1)} %get-tuple-element.37), channel_id=1, source_target_pairs={{0,2},{1,3},{2,0},{3,1},{4,6},{5,7},{6,4},{7,5},{8,10},{9,11},{10,... | collective-permute-start | bytes 430088 | tf_op jit(solution)/shard_map/ppermute | solution.py:344
  53.4 5.8 %collective-permute-start.1 = (bf16[1,7,40,128]{3,2,1,0:T(8,128)(2,1)S(1)}, bf16[1,7,40,128]{3,2,1,0:T(8,128)(2,1)S(1)}, u32[]{:S(2)}, u32[]{:S(2)}) collective-permute-start(bf16[1,7,40,128]{3,2,1,0:T(8,128)(2,1)S(1)} %get-tuple-element.39), channel_id=1, source_target_pairs={{0,2},{1,3},{2,0},{3,1},{4,6},{5,7},{6,4},{7,5},{8,10},{9,11},{10,... | collective-permute-start | bytes 215048 | tf_op jit(solution)/shard_map/ppermute | solution.py:344

commit v7 on v6

--- a/solution.py
+++ b/solution.py
@@ -233,10 +233,12 @@
     def stacked(piece):
         return jnp.concatenate([piece[:, :LANES], piece[:, LANES:]], axis=0).astype(jnp.bfloat16)
 
-    def rows_of(step, carry):
-        for u in range(deep):
-            j = step * deep + u
-            at = pl.ds(pl.multiple_of(j * (bands * GB), 8), bands * GB)
+    def rows_of(first_plane, count):
+        for u in range(count):
+            j = first_plane + u
+            at = j * (bands * GB)
+            at = at if isinstance(at, int) else pl.multiple_of(at, 8)
+            at = pl.ds(at, bands * GB)
             x = jnp.concatenate(
                 [real[at, :].astype(jnp.bfloat16), imag[at, :].astype(jnp.bfloat16)], axis=1
             )
@@ -244,10 +246,10 @@
             h = jnp.dot(x, row_tab[...], preferred_element_type=jnp.float32)
             for b in range(bands):
                 half[j, b] = stacked(h[b * GB : (b + 1) * GB])
-        return carry
-
-    deep = largest(planes, 3)
-    lax.fori_loop(0, planes // deep, rows_of, 0)
+
+    deep = min(planes, 3)
+    lax.fori_loop(0, planes // deep, lambda step, _: rows_of(step * deep, deep), None)
+    rows_of(planes - planes % deep, planes % deep)
 
     tails = tail.shape[0]
     for t in range(tails):

time: 61 us -> 61 us (level)
  no operation moved by 1% of the time
where the time goes in v7:
time: 61 us; the launch traced here: 60.3 us
  Pallas kernels  25.3 us (41%)
  starting transfers between devices  23.2 us (38%)
  waiting for transfers between devices  10.7 us (18%)
  between operations  0.85 us (1%)
    pallas_call x2, Pallas kernels, shards(): results = run(*received, *tables, weight, core, *kept)  20.5 us
    ppermute x7, starting transfers between devices, shards(): received.append(lax.ppermute(outgoing[1 + k], 'fft', pairs))  13.4 us
    all_to_all x1, starting transfers between devices, shards(): lax.all_to_all(outgoing[0], 'fft', split_axis=0, concat_axis=0, tiled=True)  7.45 us
    ppermute x4, waiting for transfers between devices, halve(): got = lax.ppermute(send, axis, partners(axis, bit))  6.73 us
    ppermute x7, waiting for transfers between devices, shards(): received.append(lax.ppermute(outgoing[1 + k], 'fft', pairs))  3.92 us
    pallas_call x1, Pallas kernels, shards(): vmem_call(functools.partial(stick_kernel, planes, ranks), [jax.ShapeDtype...  3.8 us
    ppermute x4, starting transfers between devices, halve(): got = lax.ppermute(send, axis, partners(axis, bit))  2.29 us
  transfers between devices with their start and end apart: 12, of which 4 were waited for; matrix products, arithmetic and copies ran while one was open for 0% of the time, Pallas kernels for 34%

profile of v7, /device:TPU:0, one launch (start us, length us, event | category | flops | bytes accessed | tf_op | source)
XLA Modules:
  0.0 60.3 jit_solution(7453278120861856602)
XLA Ops:
  0.7 0.0 copy-start
  0.7 3.8 %shard_map.91 = (bf16[8,192,128]{2,1,0:T(8,128)(2,1)}, bf16[360,128]{1,0:T(8,128)(2,1)}, bf16[360,128]{1,0:T(8,128)(2,1)}, bf16[360,128]{1,0:T(8,128)(2,1)}, bf1...) custom-call(s32[1]{0:T(128)S(6)} %copy.10.refs_0_, ...), custom_call_target="tpu_custom_call" | custom-call | flops 4000000000 | bytes 1048576 | tf_op jit(solution)/shard_map/pallas_call | solution.py:376
  4.5 0.0 copy-start.8
  4.5 0.0 copy-start.7
  4.5 0.0 copy-start.6
  4.5 0.0 copy-start.5
  4.5 0.0 copy-start.4
  4.5 0.0 copy-start.1
  4.5 0.0 copy-start.2
  4.5 7.5 %all-to-all-start = ((bf16[8,192,128]{2,1,0:T(8,128)(2,1)}), bf16[8,192,128]{2,1,0:T(8,128)(2,1)S(1)}, u32[]{:S(2)}, u32[]{:S(2)}) async-start(bf16[8,192,128]{2,1,0:T(8,128)(2,1)} %get-tuple-element.21), calls=%async_computation | async-start | bytes 786432 | tf_op jit(solution)/shard_map/all_to_all | solution.py:404
  12.0 2.0 %collective-permute-start.2 = (bf16[360,128]{1,0:T(8,128)(2,1)}, bf16[360,128]{1,0:T(8,128)(2,1)S(1)}, u32[]{:S(2)}, u32[]{:S(2)}) collective-permute-start(bf16[360,128]{1,0:T(8,128)(2,1)} %get-tuple-element.25), channel_id=1, source_target_pairs={{0,4},{4,0},{8,12},{12,8},{16,20},{20,16},{24,28},{28,24},{1,5},{5... | collective-permute-start | bytes 276488 | tf_op jit(solution)/shard_map/ppermute | solution.py:409
  14.0 1.5 %collective-permute-start.3 = (bf16[360,128]{1,0:T(8,128)(2,1)}, bf16[360,128]{1,0:T(8,128)(2,1)S(1)}, u32[]{:S(2)}, u32[]{:S(2)}) collective-permute-start(bf16[360,128]{1,0:T(8,128)(2,1)} %get-tuple-element.26), channel_id=1, source_target_pairs={{0,8},{4,12},{8,0},{12,4},{16,24},{20,28},{24,16},{28,20},{1,9},{5... | collective-permute-start | bytes 276488 | tf_op jit(solution)/shard_map/ppermute | solution.py:409
  15.5 0.0 copy-done.8
  15.5 0.0 collective-permute-start.4
  15.5 0.0 copy-done.7
  15.5 0.0 copy-start.9
  15.5 2.9 %collective-permute-start.5 = (bf16[360,128]{1,0:T(8,128)(2,1)S(1)}, bf16[360,128]{1,0:T(8,128)(2,1)S(1)}, u32[]{:S(2)}, u32[]{:S(2)}) collective-permute-start(bf16[360,128]{1,0:T(8,128)(2,1)S(1)} %copy-done.7), channel_id=1, source_target_pairs={{0,16},{4,20},{8,24},{12,28},{16,0},{20,4},{24,8},{28,12},{1,17},{... | collective-permute-start | bytes 276488 | tf_op jit(solution)/shard_map/ppermute | solution.py:409
  18.4 0.0 copy-done.6
  18.4 1.5 %collective-permute-start.6 = (bf16[360,128]{1,0:T(8,128)(2,1)S(1)}, bf16[360,128]{1,0:T(8,128)(2,1)S(1)}, u32[]{:S(2)}, u32[]{:S(2)}) collective-permute-start(bf16[360,128]{1,0:T(8,128)(2,1)S(1)} %copy-done.6), channel_id=1, source_target_pairs={{0,20},{4,16},{8,28},{12,24},{16,4},{20,0},{24,12},{28,8},{1,21},{... | collective-permute-start | bytes 276488 | tf_op jit(solution)/shard_map/ppermute | solution.py:409
  19.9 0.0 copy-done.9
  19.9 0.0 collective-permute-done.2.refs_1_
  19.9 0.0 copy-done.5
  19.9 3.9 %collective-permute-start.7 = (bf16[360,128]{1,0:T(8,128)(2,1)S(1)}, bf16[360,128]{1,0:T(8,128)(2,1)S(1)}, u32[]{:S(2)}, u32[]{:S(2)}) collective-permute-start(bf16[360,128]{1,0:T(8,128)(2,1)S(1)} %copy-done.5), channel_id=1, source_target_pairs={{0,24},{4,28},{8,16},{12,20},{16,8},{20,12},{24,0},{28,4},{1,25},{... | collective-permute-start | bytes 276488 | tf_op jit(solution)/shard_map/ppermute | solution.py:409
  23.8 1.9 %collective-permute-done.3.refs_2_ = bf16[360,128]{1,0:T(8,128)(2,1)S(1)} collective-permute-done((bf16[360,128]{1,0:T(8,128)(2,1)}, bf16[360,128]{1,0:T(8,128)(2,1)S(1)}, u32[]{:S(2)}, u32[]{:S(2)}) %collective-permute-start.3) | collective-permute-done | bytes 92192 | tf_op jit(solution)/shard_map/ppermute | solution.py:409
  25.7 0.0 copy-done.4
  25.7 1.7 %collective-permute-start.8 = (bf16[360,128]{1,0:T(8,128)(2,1)S(1)}, bf16[360,128]{1,0:T(8,128)(2,1)S(1)}, u32[]{:S(2)}, u32[]{:S(2)}) collective-permute-start(bf16[360,128]{1,0:T(8,128)(2,1)S(1)} %copy-done.4), channel_id=1, source_target_pairs={{0,28},{4,24},{8,20},{12,16},{16,12},{20,8},{24,4},{28,0},{1,29},{... | collective-permute-start | bytes 276488 | tf_op jit(solution)/shard_map/ppermute | solution.py:409
  27.4 0.0 all-to-all-done.refs_0_
  27.4 0.0 copy-done
  27.4 0.0 copy-done.1
  27.4 0.0 copy-done.2
  27.4 0.0 copy-start.3
  27.4 7.9 %shard_map.92 = (bf16[2,7,40,128]{3,2,1,0:T(8,128)(2,1)S(1)}, bf16[2,7,40,128]{3,2,1,0:T(8,128)(2,1)S(1)}, f32[8,512]{1,0:T(8,128)S(1)}, bf16[512,128]{1,0:T(8,128)(2,1)S(1)}, bf16[512,128]{1,0:T(8,128)(2,1)S(1)}) custom-call(bf16[8,192,128]{2,1,0:T(8,128)(2,1)S(1)} %all-to-all-done.refs_0_, bf16[256,256]{1,0:T(8,128)(2,1)S(1)} %copy-done.2, ...), custom_call_target="tpu_custom_call" | custom-call | flops 16000000000 | bytes 1048576 | tf_op jit(solution)/shard_map/pallas_call | solution.py:433
  35.3 0.0 collective-permute-done.4.refs_3_
  35.3 0.1 collective-permute-start
  35.4 0.0 collective-permute-done.5.refs_4_
  35.4 2.0 %collective-permute-done.6.refs_5_ = bf16[360,128]{1,0:T(8,128)(2,1)S(1)} collective-permute-done((bf16[360,128]{1,0:T(8,128)(2,1)S(1)}, bf16[360,128]{1,0:T(8,128)(2,1)S(1)}, u32[]{:S(2)}, u32[]{:S(2)}) %collective-permute-start.6) | collective-permute-done | bytes 92192 | tf_op jit(solution)/shard_map/ppermute | solution.py:409
  37.4 0.0 collective-permute-done.7.refs_6_
  37.4 0.0 collective-permute-done.8.refs_7_
  37.4 0.0 copy-done.3
  37.4 12.6 %shard_map.93 = (bf16[2,14,40,128]{3,2,1,0:T(8,128)(2,1)S(1)}, bf16[2,14,40,128]{3,2,1,0:T(8,128)(2,1)S(1)}) custom-call(bf16[360,128]{1,0:T(8,128)(2,1)S(1)} %copy-done.3, bf16[360,128]{1,0:T(8,128)(2,1)S(1)} %collective-permute-done.2.refs_1_, bf16[360,128]{1,0:T(8,128)(2,1)S(1)} %collective-permute-done.3.refs_2_, ...), custom_call_target="tpu_custom_call" | custom-call | flops 16000000000 | bytes 1048576 | tf_op jit(solution)/shard_map/pallas_call | solution.py:433
  50.1 0.1 collective-permute-start.9
  50.2 0.0 collective-permute-done
  50.2 1.5 %collective-permute-done.9 = bf16[2,14,40,128]{3,2,1,0:T(8,128)(2,1)S(1)} collective-permute-done((bf16[2,14,40,128]{3,2,1,0:T(8,128)(2,1)S(1)}, bf16[2,14,40,128]{3,2,1,0:T(8,128)(2,1)S(1)}, u32[]{:S(2)}, u32[]{:S(2)}) %collective-permute-start.9) | collective-permute-done | bytes 286752 | tf_op jit(solution)/shard_map/ppermute | solution.py:346
  51.7 0.1 add_convert_fusion
  51.8 1.6 %collective-permute-start.10 = (bf16[1,14,40,128]{3,2,1,0:T(8,128)(2,1)S(1)}, bf16[1,14,40,128]{3,2,1,0:T(8,128)(2,1)S(1)}, u32[]{:S(2)}, u32[]{:S(2)}) collective-permute-start(bf16[1,14,40,128]{3,2,1,0:T(8,128)(2,1)S(1)} %get-tuple-element.37), channel_id=1, source_target_pairs={{0,2},{1,3},{2,0},{3,1},{4,6},{5,7},{6,4},{7,5},{8,10},{9,11},{10,... | collective-permute-start | bytes 430088 | tf_op jit(solution)/shard_map/ppermute | solution.py:346
  53.4 0.6 collective-permute-start.1
  54.0 5.2 %collective-permute-done.1 = bf16[1,7,40,128]{3,2,1,0:T(8,128)(2,1)S(1)} collective-permute-done((bf16[1,7,40,128]{3,2,1,0:T(8,128)(2,1)S(1)}, bf16[1,7,40,128]{3,2,1,0:T(8,128)(2,1)S(1)}, u32[]{:S(2)}, u32[]{:S(2)}) %collective-permute-start.1) | collective-permute-done | bytes 71712 | tf_op jit(solution)/shard_map/ppermute | solution.py:346
  59.2 0.0 collective-permute-done.10
  59.2 1.0 %shard_map.94 = f32[18,36,144]{2,1,0:T(8,128)} custom-call(bf16[7,40,128]{2,1,0:T(8,128)(2,1)S(1)} %get-tuple-element.40.refs_0_, bf16[7,40,128]{2,1,0:T(8,128)(2,1)S(1)} %bitcast.8, bf16[14,40,128]{2,1,0:T(8,128)(2,1)S(1)} %get-tuple-element.38.refs_2_, bf16[14,40,128]{2,1,0:T(8,128)(2,1)S(1)} %bitcast.7), custom_call_target="tpu_custom_call" | custom-call | flops 1 | bytes 1048576 | tf_op jit(solution)/shard_map/pallas_call | solution.py:437
  (4 shorter events, 0.1 us)
Async XLA Ops:
  0.7 26.7 %copy-start = (bf16[2048,256]{1,0:T(8,128)(2,1)S(1)}, bf16[2048,256]{1,0:T(8,128)(2,1)}, u32[]{:S(2)}) copy-start(bf16[2048,256]{1,0:T(8,128)(2,1)} %constant.34.clone.refs_2_.refs_9_) | copy-start | bytes 3145732
  4.5 11.0 %copy-start.8 = (bf16[360,128]{1,0:T(8,128)(2,1)S(1)}, bf16[360,128]{1,0:T(8,128)(2,1)}, u32[]{:S(2)}) copy-start(bf16[360,128]{1,0:T(8,128)(2,1)} %get-tuple-element.27) | copy-start | bytes 276484
  4.5 11.0 %copy-start.7 = (bf16[360,128]{1,0:T(8,128)(2,1)S(1)}, bf16[360,128]{1,0:T(8,128)(2,1)}, u32[]{:S(2)}) copy-start(bf16[360,128]{1,0:T(8,128)(2,1)} %get-tuple-element.28) | copy-start | bytes 276484
  4.5 13.9 %copy-start.6 = (bf16[360,128]{1,0:T(8,128)(2,1)S(1)}, bf16[360,128]{1,0:T(8,128)(2,1)}, u32[]{:S(2)}) copy-start(bf16[360,128]{1,0:T(8,128)(2,1)} %get-tuple-element.29) | copy-start | bytes 276484
  4.5 15.4 %copy-start.5 = (bf16[360,128]{1,0:T(8,128)(2,1)S(1)}, bf16[360,128]{1,0:T(8,128)(2,1)}, u32[]{:S(2)}) copy-start(bf16[360,128]{1,0:T(8,128)(2,1)} %get-tuple-element.30) | copy-start | bytes 276484
  4.5 21.2 %copy-start.4 = (bf16[360,128]{1,0:T(8,128)(2,1)S(1)}, bf16[360,128]{1,0:T(8,128)(2,1)}, u32[]{:S(2)}) copy-start(bf16[360,128]{1,0:T(8,128)(2,1)} %get-tuple-element.31) | copy-start | bytes 276484
  4.5 22.9 %copy-start.1 = (bf16[288,144]{1,0:T(8,128)(2,1)S(1)}, bf16[288,144]{1,0:T(8,128)(2,1)}, u32[]{:S(2)}) copy-start(bf16[288,144]{1,0:T(8,128)(2,1)} %constant.35.clone.refs_3_.refs_10_) | copy-start | bytes 248836
  4.5 22.8 %copy-start.2 = (bf16[256,256]{1,0:T(8,128)(2,1)S(1)}, bf16[256,256]{1,0:T(8,128)(2,1)}, u32[]{:S(2)}) copy-start(bf16[256,256]{1,0:T(8,128)(2,1)} %constant.33.clone.refs_1_.refs_8_) | copy-start | bytes 393220
  4.5 22.8 %all-to-all-start = ((bf16[8,192,128]{2,1,0:T(8,128)(2,1)}), bf16[8,192,128]{2,1,0:T(8,128)(2,1)S(1)}, u32[]{:S(2)}, u32[]{:S(2)}) async-start(bf16[8,192,128]{2,1,0:T(8,128)(2,1)} %get-tuple-element.21), calls=%async_computation | async-start | bytes 786432 | tf_op jit(solution)/shard_map/all_to_all | solution.py:404
  12.0 7.9 %collective-permute-start.2 = (bf16[360,128]{1,0:T(8,128)(2,1)}, bf16[360,128]{1,0:T(8,128)(2,1)S(1)}, u32[]{:S(2)}, u32[]{:S(2)}) collective-permute-start(bf16[360,128]{1,0:T(8,128)(2,1)} %get-tuple-element.25), channel_id=1, source_target_pairs={{0,4},{4,0},{8,12},{12,8},{16,20},{20,16},{24,28},{28,24},{1,5},{5... | collective-permute-start | bytes 276488 | tf_op jit(solution)/shard_map/ppermute | solution.py:409
  14.0 11.7 %collective-permute-start.3 = (bf16[360,128]{1,0:T(8,128)(2,1)}, bf16[360,128]{1,0:T(8,128)(2,1)S(1)}, u32[]{:S(2)}, u32[]{:S(2)}) collective-permute-start(bf16[360,128]{1,0:T(8,128)(2,1)} %get-tuple-element.26), channel_id=1, source_target_pairs={{0,8},{4,12},{8,0},{12,4},{16,24},{20,28},{24,16},{28,20},{1,9},{5... | collective-permute-start | bytes 276488 | tf_op jit(solution)/shard_map/ppermute | solution.py:409
  15.5 19.8 %collective-permute-start.4 = (bf16[360,128]{1,0:T(8,128)(2,1)S(1)}, bf16[360,128]{1,0:T(8,128)(2,1)S(1)}, u32[]{:S(2)}, u32[]{:S(2)}) collective-permute-start(bf16[360,128]{1,0:T(8,128)(2,1)S(1)} %copy-done.8), channel_id=1, source_target_pairs={{0,12},{4,8},{8,4},{12,0},{16,28},{20,24},{24,20},{28,16},{1,13},{... | collective-permute-start | bytes 276488 | tf_op jit(solution)/shard_map/ppermute | solution.py:409
  15.5 4.4 %copy-start.9 = (f32[12]{0:T(128)S(1)}, f32[12]{0:T(128)}, u32[]{:S(2)}) copy-start(f32[12]{0:T(128)} %param.10) | copy-start | bytes 148
  15.5 19.9 %collective-permute-start.5 = (bf16[360,128]{1,0:T(8,128)(2,1)S(1)}, bf16[360,128]{1,0:T(8,128)(2,1)S(1)}, u32[]{:S(2)}, u32[]{:S(2)}) collective-permute-start(bf16[360,128]{1,0:T(8,128)(2,1)S(1)} %copy-done.7), channel_id=1, source_target_pairs={{0,16},{4,20},{8,24},{12,28},{16,0},{20,4},{24,8},{28,12},{1,17},{... | collective-permute-start | bytes 276488 | tf_op jit(solution)/shard_map/ppermute | solution.py:409
  18.4 19.0 %collective-permute-start.6 = (bf16[360,128]{1,0:T(8,128)(2,1)S(1)}, bf16[360,128]{1,0:T(8,128)(2,1)S(1)}, u32[]{:S(2)}, u32[]{:S(2)}) collective-permute-start(bf16[360,128]{1,0:T(8,128)(2,1)S(1)} %copy-done.6), channel_id=1, source_target_pairs={{0,20},{4,16},{8,28},{12,24},{16,4},{20,0},{24,12},{28,8},{1,21},{... | collective-permute-start | bytes 276488 | tf_op jit(solution)/shard_map/ppermute | solution.py:409
  19.9 17.5 %collective-permute-start.7 = (bf16[360,128]{1,0:T(8,128)(2,1)S(1)}, bf16[360,128]{1,0:T(8,128)(2,1)S(1)}, u32[]{:S(2)}, u32[]{:S(2)}) collective-permute-start(bf16[360,128]{1,0:T(8,128)(2,1)S(1)} %copy-done.5), channel_id=1, source_target_pairs={{0,24},{4,28},{8,16},{12,20},{16,8},{20,12},{24,0},{28,4},{1,25},{... | collective-permute-start | bytes 276488 | tf_op jit(solution)/shard_map/ppermute | solution.py:409
  25.7 11.7 %collective-permute-start.8 = (bf16[360,128]{1,0:T(8,128)(2,1)S(1)}, bf16[360,128]{1,0:T(8,128)(2,1)S(1)}, u32[]{:S(2)}, u32[]{:S(2)}) collective-permute-start(bf16[360,128]{1,0:T(8,128)(2,1)S(1)} %copy-done.4), channel_id=1, source_target_pairs={{0,28},{4,24},{8,20},{12,16},{16,12},{20,8},{24,4},{28,0},{1,29},{... | collective-permute-start | bytes 276488 | tf_op jit(solution)/shard_map/ppermute | solution.py:409
  27.4 10.1 %copy-start.3 = (bf16[360,128]{1,0:T(8,128)(2,1)S(1)}, bf16[360,128]{1,0:T(8,128)(2,1)}, u32[]{:S(2)}) copy-start(bf16[360,128]{1,0:T(8,128)(2,1)} %get-tuple-element.24.refs_0_) | copy-start | bytes 276484
  35.3 14.8 %collective-permute-start = (bf16[2,7,40,128]{3,2,1,0:T(8,128)(2,1)S(1)}, bf16[2,7,40,128]{3,2,1,0:T(8,128)(2,1)S(1)}, u32[]{:S(2)}, u32[]{:S(2)}) collective-permute-start(bf16[2,7,40,128]{3,2,1,0:T(8,128)(2,1)S(1)} %get-tuple-element.23), channel_id=1, source_target_pairs={{0,1},{1,0},{2,3},{3,2},{4,5},{5,4},{6,7},{7,6},{8,9},{9,8},{10,11... | collective-permute-start | bytes 430088 | tf_op jit(solution)/shard_map/ppermute | solution.py:346
  50.1 1.6 %collective-permute-start.9 = (bf16[2,14,40,128]{3,2,1,0:T(8,128)(2,1)S(1)}, bf16[2,14,40,128]{3,2,1,0:T(8,128)(2,1)S(1)}, u32[]{:S(2)}, u32[]{:S(2)}) collective-permute-start(bf16[2,14,40,128]{3,2,1,0:T(8,128)(2,1)S(1)} %get-tuple-element.36), channel_id=1, source_target_pairs={{0,1},{1,0},{2,3},{3,2},{4,5},{5,4},{6,7},{7,6},{8,9},{9,8},{10,11... | collective-permute-start | bytes 860168 | tf_op jit(solution)/shard_map/ppermute | solution.py:346
  51.8 7.4 %collective-permute-start.10 = (bf16[1,14,40,128]{3,2,1,0:T(8,128)(2,1)S(1)}, bf16[1,14,40,128]{3,2,1,0:T(8,128)(2,1)S(1)}, u32[]{:S(2)}, u32[]{:S(2)}) collective-permute-start(bf16[1,14,40,128]{3,2,1,0:T(8,128)(2,1)S(1)} %get-tuple-element.37), channel_id=1, source_target_pairs={{0,2},{1,3},{2,0},{3,1},{4,6},{5,7},{6,4},{7,5},{8,10},{9,11},{10,... | collective-permute-start | bytes 430088 | tf_op jit(solution)/shard_map/ppermute | solution.py:346
  53.4 5.8 %collective-permute-start.1 = (bf16[1,7,40,128]{3,2,1,0:T(8,128)(2,1)S(1)}, bf16[1,7,40,128]{3,2,1,0:T(8,128)(2,1)S(1)}, u32[]{:S(2)}, u32[]{:S(2)}) collective-permute-start(bf16[1,7,40,128]{3,2,1,0:T(8,128)(2,1)S(1)} %get-tuple-element.39), channel_id=1, source_target_pairs={{0,2},{1,3},{2,0},{3,1},{4,6},{5,7},{6,4},{7,5},{8,10},{9,11},{10,... | collective-permute-start | bytes 215048 | tf_op jit(solution)/shard_map/ppermute | solution.py:346

commit v8 on v7

--- a/solution.py
+++ b/solution.py
@@ -15,7 +15,7 @@
 LANES = 128
 TAIL = N - LANES
 SHARE = LANES // TAIL
-PAIRS = 12
+PAIRS = 18
 INFO = 8
 GROUPS = 4
 
@@ -247,7 +247,7 @@
             for b in range(bands):
                 half[j, b] = stacked(h[b * GB : (b + 1) * GB])
 
-    deep = min(planes, 3)
+    deep = min(planes, 12)
     lax.fori_loop(0, planes // deep, lambda step, _: rows_of(step * deep, deep), None)
     rows_of(planes - planes % deep, planes % deep)
 
@@ -259,7 +259,7 @@
         for b in range(bands):
             tail[t, b] = stacked(h[b * GB : (b + 1) * GB])
 
-    wide = largest(bands, 6)
+    wide = largest(bands, 12)
 
     def columns_of(step, carry):
         pieces = []

time: 61 us -> 59.6 us (0.977)
  Pallas kernels: 25.3 us -> 23.3 us
  waiting for transfers between devices: 10.7 us -> 11.4 us
    pallas_call x2, Pallas kernels: 20.5 us -> 18.4 us  [shards(): results = run(*received, *tables, weight, core, *kept)]
    ppermute x7, waiting for transfers between devices: 3.92 us -> 4.65 us  [shards(): received.append(lax.ppermute(outgoing[1 + k], 'fft', pairs))]
  transfers between devices with their start and end apart: 12 -> 12, of which waited for: 4 -> 5; matrix products, arithmetic and copies ran while one was open for 0% -> 0% of each run, Pallas kernels for 34% -> 31%
where the time goes in v8:
time: 59.6 us; the launch traced here: 58.9 us
  Pallas kernels  23.3 us (39%)
  starting transfers between devices  23.2 us (39%)
  waiting for transfers between devices  11.4 us (19%)
  between operations  0.84 us (1%)
    pallas_call x2, Pallas kernels, shards(): results = run(*received, *tables, weight, core, *kept)  18.4 us
    ppermute x7, starting transfers between devices, shards(): received.append(lax.ppermute(outgoing[1 + k], 'fft', pairs))  13.4 us
    all_to_all x1, starting transfers between devices, shards(): lax.all_to_all(outgoing[0], 'fft', split_axis=0, concat_axis=0, tiled=True)  7.45 us
    ppermute x4, waiting for transfers between devices, halve(): got = lax.ppermute(send, axis, partners(axis, bit))  6.73 us
    ppermute x7, waiting for transfers between devices, shards(): received.append(lax.ppermute(outgoing[1 + k], 'fft', pairs))  4.65 us
    pallas_call x1, Pallas kernels, shards(): vmem_call(functools.partial(stick_kernel, planes, ranks), [jax.ShapeDtype...  3.8 us
    ppermute x4, starting transfers between devices, halve(): got = lax.ppermute(send, axis, partners(axis, bit))  2.29 us
  transfers between devices with their start and end apart: 12, of which 5 were waited for; matrix products, arithmetic and copies ran while one was open for 0% of the time, Pallas kernels for 31%

profile of v8, /device:TPU:0, one launch (start us, length us, event | category | flops | bytes accessed | tf_op | source)
XLA Modules:
  0.0 58.9 jit_solution(12349162556450020102)
XLA Ops:
  0.7 0.0 copy-start
  0.7 3.8 %shard_map.91 = (bf16[8,192,128]{2,1,0:T(8,128)(2,1)}, bf16[360,128]{1,0:T(8,128)(2,1)}, bf16[360,128]{1,0:T(8,128)(2,1)}, bf16[360,128]{1,0:T(8,128)(2,1)}, bf1...) custom-call(s32[1]{0:T(128)S(6)} %copy.10.refs_0_, ...), custom_call_target="tpu_custom_call" | custom-call | flops 4000000000 | bytes 1048576 | tf_op jit(solution)/shard_map/pallas_call | solution.py:376
  4.5 0.0 copy-start.8
  4.5 0.0 copy-start.7
  4.5 0.0 copy-start.6
  4.5 0.0 copy-start.5
  4.5 0.0 copy-start.4
  4.5 0.0 copy-start.1
  4.5 0.0 copy-start.2
  4.5 7.5 %all-to-all-start = ((bf16[8,192,128]{2,1,0:T(8,128)(2,1)}), bf16[8,192,128]{2,1,0:T(8,128)(2,1)S(1)}, u32[]{:S(2)}, u32[]{:S(2)}) async-start(bf16[8,192,128]{2,1,0:T(8,128)(2,1)} %get-tuple-element.21), calls=%async_computation | async-start | bytes 786432 | tf_op jit(solution)/shard_map/all_to_all | solution.py:404
  12.0 2.0 %collective-permute-start.2 = (bf16[360,128]{1,0:T(8,128)(2,1)}, bf16[360,128]{1,0:T(8,128)(2,1)S(1)}, u32[]{:S(2)}, u32[]{:S(2)}) collective-permute-start(bf16[360,128]{1,0:T(8,128)(2,1)} %get-tuple-element.25), channel_id=1, source_target_pairs={{0,4},{4,0},{8,12},{12,8},{16,20},{20,16},{24,28},{28,24},{1,5},{5... | collective-permute-start | bytes 276488 | tf_op jit(solution)/shard_map/ppermute | solution.py:409
  14.0 1.5 %collective-permute-start.3 = (bf16[360,128]{1,0:T(8,128)(2,1)}, bf16[360,128]{1,0:T(8,128)(2,1)S(1)}, u32[]{:S(2)}, u32[]{:S(2)}) collective-permute-start(bf16[360,128]{1,0:T(8,128)(2,1)} %get-tuple-element.26), channel_id=1, source_target_pairs={{0,8},{4,12},{8,0},{12,4},{16,24},{20,28},{24,16},{28,20},{1,9},{5... | collective-permute-start | bytes 276488 | tf_op jit(solution)/shard_map/ppermute | solution.py:409
  15.5 0.0 copy-done.8
  15.5 0.0 collective-permute-start.4
  15.5 0.0 copy-done.7
  15.5 0.0 copy-start.9
  15.5 2.9 %collective-permute-start.5 = (bf16[360,128]{1,0:T(8,128)(2,1)S(1)}, bf16[360,128]{1,0:T(8,128)(2,1)S(1)}, u32[]{:S(2)}, u32[]{:S(2)}) collective-permute-start(bf16[360,128]{1,0:T(8,128)(2,1)S(1)} %copy-done.7), channel_id=1, source_target_pairs={{0,16},{4,20},{8,24},{12,28},{16,0},{20,4},{24,8},{28,12},{1,17},{... | collective-permute-start | bytes 276488 | tf_op jit(solution)/shard_map/ppermute | solution.py:409
  18.4 0.0 copy-done.6
  18.4 1.5 %collective-permute-start.6 = (bf16[360,128]{1,0:T(8,128)(2,1)S(1)}, bf16[360,128]{1,0:T(8,128)(2,1)S(1)}, u32[]{:S(2)}, u32[]{:S(2)}) collective-permute-start(bf16[360,128]{1,0:T(8,128)(2,1)S(1)} %copy-done.6), channel_id=1, source_target_pairs={{0,20},{4,16},{8,28},{12,24},{16,4},{20,0},{24,12},{28,8},{1,21},{... | collective-permute-start | bytes 276488 | tf_op jit(solution)/shard_map/ppermute | solution.py:409
  19.9 0.0 copy-done.9
  19.9 0.0 collective-permute-done.2.refs_1_
  19.9 0.0 copy-done.5
  19.9 3.9 %collective-permute-start.7 = (bf16[360,128]{1,0:T(8,128)(2,1)S(1)}, bf16[360,128]{1,0:T(8,128)(2,1)S(1)}, u32[]{:S(2)}, u32[]{:S(2)}) collective-permute-start(bf16[360,128]{1,0:T(8,128)(2,1)S(1)} %copy-done.5), channel_id=1, source_target_pairs={{0,24},{4,28},{8,16},{12,20},{16,8},{20,12},{24,0},{28,4},{1,25},{... | collective-permute-start | bytes 276488 | tf_op jit(solution)/shard_map/ppermute | solution.py:409
  23.8 1.9 %collective-permute-done.3.refs_2_ = bf16[360,128]{1,0:T(8,128)(2,1)S(1)} collective-permute-done((bf16[360,128]{1,0:T(8,128)(2,1)}, bf16[360,128]{1,0:T(8,128)(2,1)S(1)}, u32[]{:S(2)}, u32[]{:S(2)}) %collective-permute-start.3) | collective-permute-done | bytes 92192 | tf_op jit(solution)/shard_map/ppermute | solution.py:409
  25.7 0.0 copy-done.4
  25.7 1.7 %collective-permute-start.8 = (bf16[360,128]{1,0:T(8,128)(2,1)S(1)}, bf16[360,128]{1,0:T(8,128)(2,1)S(1)}, u32[]{:S(2)}, u32[]{:S(2)}) collective-permute-start(bf16[360,128]{1,0:T(8,128)(2,1)S(1)} %copy-done.4), channel_id=1, source_target_pairs={{0,28},{4,24},{8,20},{12,16},{16,12},{20,8},{24,4},{28,0},{1,29},{... | collective-permute-start | bytes 276488 | tf_op jit(solution)/shard_map/ppermute | solution.py:409
  27.4 0.0 all-to-all-done.refs_0_
  27.4 0.0 copy-done
  27.4 0.0 copy-done.1
  27.4 0.0 copy-done.2
  27.4 0.0 copy-start.3
  27.4 7.2 %shard_map.92 = (bf16[2,7,40,128]{3,2,1,0:T(8,128)(2,1)S(1)}, bf16[2,7,40,128]{3,2,1,0:T(8,128)(2,1)S(1)}, f32[8,512]{1,0:T(8,128)S(1)}, bf16[512,128]{1,0:T(8,128)(2,1)S(1)}, bf16[512,128]{1,0:T(8,128)(2,1)S(1)}) custom-call(bf16[8,192,128]{2,1,0:T(8,128)(2,1)S(1)} %all-to-all-done.refs_0_, bf16[256,256]{1,0:T(8,128)(2,1)S(1)} %copy-done.2, ...), custom_call_target="tpu_custom_call" | custom-call | flops 16000000000 | bytes 1048576 | tf_op jit(solution)/shard_map/pallas_call | solution.py:433
  34.6 0.0 collective-permute-done.4.refs_3_
  34.6 0.1 collective-permute-start
  34.7 0.3 collective-permute-done.5.refs_4_
  35.0 2.5 %collective-permute-done.6.refs_5_ = bf16[360,128]{1,0:T(8,128)(2,1)S(1)} collective-permute-done((bf16[360,128]{1,0:T(8,128)(2,1)S(1)}, bf16[360,128]{1,0:T(8,128)(2,1)S(1)}, u32[]{:S(2)}, u32[]{:S(2)}) %collective-permute-start.6) | collective-permute-done | bytes 92192 | tf_op jit(solution)/shard_map/ppermute | solution.py:409
  37.4 0.0 collective-permute-done.7.refs_6_
  37.4 0.0 collective-permute-done.8.refs_7_
  37.4 0.0 copy-done.3
  37.4 11.3 %shard_map.93 = (bf16[2,14,40,128]{3,2,1,0:T(8,128)(2,1)S(1)}, bf16[2,14,40,128]{3,2,1,0:T(8,128)(2,1)S(1)}) custom-call(bf16[360,128]{1,0:T(8,128)(2,1)S(1)} %copy-done.3, bf16[360,128]{1,0:T(8,128)(2,1)S(1)} %collective-permute-done.2.refs_1_, bf16[360,128]{1,0:T(8,128)(2,1)S(1)} %collective-permute-done.3.refs_2_, ...), custom_call_target="tpu_custom_call" | custom-call | flops 16000000000 | bytes 1048576 | tf_op jit(solution)/shard_map/pallas_call | solution.py:433
  48.7 0.1 collective-permute-start.9
  48.8 0.0 collective-permute-done
  48.9 1.5 %collective-permute-done.9 = bf16[2,14,40,128]{3,2,1,0:T(8,128)(2,1)S(1)} collective-permute-done((bf16[2,14,40,128]{3,2,1,0:T(8,128)(2,1)S(1)}, bf16[2,14,40,128]{3,2,1,0:T(8,128)(2,1)S(1)}, u32[]{:S(2)}, u32[]{:S(2)}) %collective-permute-start.9) | collective-permute-done | bytes 286752 | tf_op jit(solution)/shard_map/ppermute | solution.py:346
  50.4 0.1 add_convert_fusion
  50.5 1.6 %collective-permute-start.10 = (bf16[1,14,40,128]{3,2,1,0:T(8,128)(2,1)S(1)}, bf16[1,14,40,128]{3,2,1,0:T(8,128)(2,1)S(1)}, u32[]{:S(2)}, u32[]{:S(2)}) collective-permute-start(bf16[1,14,40,128]{3,2,1,0:T(8,128)(2,1)S(1)} %get-tuple-element.37), channel_id=1, source_target_pairs={{0,2},{1,3},{2,0},{3,1},{4,6},{5,7},{6,4},{7,5},{8,10},{9,11},{10,... | collective-permute-start | bytes 430088 | tf_op jit(solution)/shard_map/ppermute | solution.py:346
  52.1 0.6 %collective-permute-start.1 = (bf16[1,7,40,128]{3,2,1,0:T(8,128)(2,1)S(1)}, bf16[1,7,40,128]{3,2,1,0:T(8,128)(2,1)S(1)}, u32[]{:S(2)}, u32[]{:S(2)}) collective-permute-start(bf16[1,7,40,128]{3,2,1,0:T(8,128)(2,1)S(1)} %get-tuple-element.39), channel_id=1, source_target_pairs={{0,2},{1,3},{2,0},{3,1},{4,6},{5,7},{6,4},{7,5},{8,10},{9,11},{10,... | collective-permute-start | bytes 215048 | tf_op jit(solution)/shard_map/ppermute | solution.py:346
  52.7 5.2 %collective-permute-done.1 = bf16[1,7,40,128]{3,2,1,0:T(8,128)(2,1)S(1)} collective-permute-done((bf16[1,7,40,128]{3,2,1,0:T(8,128)(2,1)S(1)}, bf16[1,7,40,128]{3,2,1,0:T(8,128)(2,1)S(1)}, u32[]{:S(2)}, u32[]{:S(2)}) %collective-permute-start.1) | collective-permute-done | bytes 71712 | tf_op jit(solution)/shard_map/ppermute | solution.py:346
  57.9 0.0 collective-permute-done.10
  57.9 1.0 %shard_map.94 = f32[18,36,144]{2,1,0:T(8,128)} custom-call(bf16[7,40,128]{2,1,0:T(8,128)(2,1)S(1)} %get-tuple-element.40.refs_0_, bf16[7,40,128]{2,1,0:T(8,128)(2,1)S(1)} %bitcast.8, bf16[14,40,128]{2,1,0:T(8,128)(2,1)S(1)} %get-tuple-element.38.refs_2_, bf16[14,40,128]{2,1,0:T(8,128)(2,1)S(1)} %bitcast.7), custom_call_target="tpu_custom_call" | custom-call | flops 1 | bytes 1048576 | tf_op jit(solution)/shard_map/pallas_call | solution.py:437
  (4 shorter events, 0.1 us)
Async XLA Ops:
  0.7 26.7 %copy-start = (bf16[2048,256]{1,0:T(8,128)(2,1)S(1)}, bf16[2048,256]{1,0:T(8,128)(2,1)}, u32[]{:S(2)}) copy-start(bf16[2048,256]{1,0:T(8,128)(2,1)} %constant.34.clone.refs_2_.refs_9_) | copy-start | bytes 3145732
  4.5 11.0 %copy-start.8 = (bf16[360,128]{1,0:T(8,128)(2,1)S(1)}, bf16[360,128]{1,0:T(8,128)(2,1)}, u32[]{:S(2)}) copy-start(bf16[360,128]{1,0:T(8,128)(2,1)} %get-tuple-element.27) | copy-start | bytes 276484
  4.5 11.0 %copy-start.7 = (bf16[360,128]{1,0:T(8,128)(2,1)S(1)}, bf16[360,128]{1,0:T(8,128)(2,1)}, u32[]{:S(2)}) copy-start(bf16[360,128]{1,0:T(8,128)(2,1)} %get-tuple-element.28) | copy-start | bytes 276484
  4.5 13.9 %copy-start.6 = (bf16[360,128]{1,0:T(8,128)(2,1)S(1)}, bf16[360,128]{1,0:T(8,128)(2,1)}, u32[]{:S(2)}) copy-start(bf16[360,128]{1,0:T(8,128)(2,1)} %get-tuple-element.29) | copy-start | bytes 276484
  4.5 15.4 %copy-start.5 = (bf16[360,128]{1,0:T(8,128)(2,1)S(1)}, bf16[360,128]{1,0:T(8,128)(2,1)}, u32[]{:S(2)}) copy-start(bf16[360,128]{1,0:T(8,128)(2,1)} %get-tuple-element.30) | copy-start | bytes 276484
  4.5 21.2 %copy-start.4 = (bf16[360,128]{1,0:T(8,128)(2,1)S(1)}, bf16[360,128]{1,0:T(8,128)(2,1)}, u32[]{:S(2)}) copy-start(bf16[360,128]{1,0:T(8,128)(2,1)} %get-tuple-element.31) | copy-start | bytes 276484
  4.5 22.9 %copy-start.1 = (bf16[288,144]{1,0:T(8,128)(2,1)S(1)}, bf16[288,144]{1,0:T(8,128)(2,1)}, u32[]{:S(2)}) copy-start(bf16[288,144]{1,0:T(8,128)(2,1)} %constant.35.clone.refs_3_.refs_10_) | copy-start | bytes 248836
  4.5 22.8 %copy-start.2 = (bf16[256,256]{1,0:T(8,128)(2,1)S(1)}, bf16[256,256]{1,0:T(8,128)(2,1)}, u32[]{:S(2)}) copy-start(bf16[256,256]{1,0:T(8,128)(2,1)} %constant.33.clone.refs_1_.refs_8_) | copy-start | bytes 393220
  4.5 22.8 %all-to-all-start = ((bf16[8,192,128]{2,1,0:T(8,128)(2,1)}), bf16[8,192,128]{2,1,0:T(8,128)(2,1)S(1)}, u32[]{:S(2)}, u32[]{:S(2)}) async-start(bf16[8,192,128]{2,1,0:T(8,128)(2,1)} %get-tuple-element.21), calls=%async_computation | async-start | bytes 786432 | tf_op jit(solution)/shard_map/all_to_all | solution.py:404
  12.0 7.9 %collective-permute-start.2 = (bf16[360,128]{1,0:T(8,128)(2,1)}, bf16[360,128]{1,0:T(8,128)(2,1)S(1)}, u32[]{:S(2)}, u32[]{:S(2)}) collective-permute-start(bf16[360,128]{1,0:T(8,128)(2,1)} %get-tuple-element.25), channel_id=1, source_target_pairs={{0,4},{4,0},{8,12},{12,8},{16,20},{20,16},{24,28},{28,24},{1,5},{5... | collective-permute-start | bytes 276488 | tf_op jit(solution)/shard_map/ppermute | solution.py:409
  14.0 11.7 %collective-permute-start.3 = (bf16[360,128]{1,0:T(8,128)(2,1)}, bf16[360,128]{1,0:T(8,128)(2,1)S(1)}, u32[]{:S(2)}, u32[]{:S(2)}) collective-permute-start(bf16[360,128]{1,0:T(8,128)(2,1)} %get-tuple-element.26), channel_id=1, source_target_pairs={{0,8},{4,12},{8,0},{12,4},{16,24},{20,28},{24,16},{28,20},{1,9},{5... | collective-permute-start | bytes 276488 | tf_op jit(solution)/shard_map/ppermute | solution.py:409
  15.5 19.1 %collective-permute-start.4 = (bf16[360,128]{1,0:T(8,128)(2,1)S(1)}, bf16[360,128]{1,0:T(8,128)(2,1)S(1)}, u32[]{:S(2)}, u32[]{:S(2)}) collective-permute-start(bf16[360,128]{1,0:T(8,128)(2,1)S(1)} %copy-done.8), channel_id=1, source_target_pairs={{0,12},{4,8},{8,4},{12,0},{16,28},{20,24},{24,20},{28,16},{1,13},{... | collective-permute-start | bytes 276488 | tf_op jit(solution)/shard_map/ppermute | solution.py:409
  15.5 4.4 %copy-start.9 = (f32[12]{0:T(128)S(1)}, f32[12]{0:T(128)}, u32[]{:S(2)}) copy-start(f32[12]{0:T(128)} %param.10) | copy-start | bytes 148
  15.5 19.4 %collective-permute-start.5 = (bf16[360,128]{1,0:T(8,128)(2,1)S(1)}, bf16[360,128]{1,0:T(8,128)(2,1)S(1)}, u32[]{:S(2)}, u32[]{:S(2)}) collective-permute-start(bf16[360,128]{1,0:T(8,128)(2,1)S(1)} %copy-done.7), channel_id=1, source_target_pairs={{0,16},{4,20},{8,24},{12,28},{16,0},{20,4},{24,8},{28,12},{1,17},{... | collective-permute-start | bytes 276488 | tf_op jit(solution)/shard_map/ppermute | solution.py:409
  18.4 19.0 %collective-permute-start.6 = (bf16[360,128]{1,0:T(8,128)(2,1)S(1)}, bf16[360,128]{1,0:T(8,128)(2,1)S(1)}, u32[]{:S(2)}, u32[]{:S(2)}) collective-permute-start(bf16[360,128]{1,0:T(8,128)(2,1)S(1)} %copy-done.6), channel_id=1, source_target_pairs={{0,20},{4,16},{8,28},{12,24},{16,4},{20,0},{24,12},{28,8},{1,21},{... | collective-permute-start | bytes 276488 | tf_op jit(solution)/shard_map/ppermute | solution.py:409
  19.9 17.5 %collective-permute-start.7 = (bf16[360,128]{1,0:T(8,128)(2,1)S(1)}, bf16[360,128]{1,0:T(8,128)(2,1)S(1)}, u32[]{:S(2)}, u32[]{:S(2)}) collective-permute-start(bf16[360,128]{1,0:T(8,128)(2,1)S(1)} %copy-done.5), channel_id=1, source_target_pairs={{0,24},{4,28},{8,16},{12,20},{16,8},{20,12},{24,0},{28,4},{1,25},{... | collective-permute-start | bytes 276488 | tf_op jit(solution)/shard_map/ppermute | solution.py:409
  25.7 11.7 %collective-permute-start.8 = (bf16[360,128]{1,0:T(8,128)(2,1)S(1)}, bf16[360,128]{1,0:T(8,128)(2,1)S(1)}, u32[]{:S(2)}, u32[]{:S(2)}) collective-permute-start(bf16[360,128]{1,0:T(8,128)(2,1)S(1)} %copy-done.4), channel_id=1, source_target_pairs={{0,28},{4,24},{8,20},{12,16},{16,12},{20,8},{24,4},{28,0},{1,29},{... | collective-permute-start | bytes 276488 | tf_op jit(solution)/shard_map/ppermute | solution.py:409
  27.4 10.1 %copy-start.3 = (bf16[360,128]{1,0:T(8,128)(2,1)S(1)}, bf16[360,128]{1,0:T(8,128)(2,1)}, u32[]{:S(2)}) copy-start(bf16[360,128]{1,0:T(8,128)(2,1)} %get-tuple-element.24.refs_0_) | copy-start | bytes 276484
  34.6 14.2 %collective-permute-start = (bf16[2,7,40,128]{3,2,1,0:T(8,128)(2,1)S(1)}, bf16[2,7,40,128]{3,2,1,0:T(8,128)(2,1)S(1)}, u32[]{:S(2)}, u32[]{:S(2)}) collective-permute-start(bf16[2,7,40,128]{3,2,1,0:T(8,128)(2,1)S(1)} %get-tuple-element.23), channel_id=1, source_target_pairs={{0,1},{1,0},{2,3},{3,2},{4,5},{5,4},{6,7},{7,6},{8,9},{9,8},{10,11... | collective-permute-start | bytes 430088 | tf_op jit(solution)/shard_map/ppermute | solution.py:346
  48.7 1.6 %collective-permute-start.9 = (bf16[2,14,40,128]{3,2,1,0:T(8,128)(2,1)S(1)}, bf16[2,14,40,128]{3,2,1,0:T(8,128)(2,1)S(1)}, u32[]{:S(2)}, u32[]{:S(2)}) collective-permute-start(bf16[2,14,40,128]{3,2,1,0:T(8,128)(2,1)S(1)} %get-tuple-element.36), channel_id=1, source_target_pairs={{0,1},{1,0},{2,3},{3,2},{4,5},{5,4},{6,7},{7,6},{8,9},{9,8},{10,11... | collective-permute-start | bytes 860168 | tf_op jit(solution)/shard_map/ppermute | solution.py:346
  50.5 7.4 %collective-permute-start.10 = (bf16[1,14,40,128]{3,2,1,0:T(8,128)(2,1)S(1)}, bf16[1,14,40,128]{3,2,1,0:T(8,128)(2,1)S(1)}, u32[]{:S(2)}, u32[]{:S(2)}) collective-permute-start(bf16[1,14,40,128]{3,2,1,0:T(8,128)(2,1)S(1)} %get-tuple-element.37), channel_id=1, source_target_pairs={{0,2},{1,3},{2,0},{3,1},{4,6},{5,7},{6,4},{7,5},{8,10},{9,11},{10,... | collective-permute-start | bytes 430088 | tf_op jit(solution)/shard_map/ppermute | solution.py:346
  52.1 5.8 %collective-permute-start.1 = (bf16[1,7,40,128]{3,2,1,0:T(8,128)(2,1)S(1)}, bf16[1,7,40,128]{3,2,1,0:T(8,128)(2,1)S(1)}, u32[]{:S(2)}, u32[]{:S(2)}) collective-permute-start(bf16[1,7,40,128]{3,2,1,0:T(8,128)(2,1)S(1)} %get-tuple-element.39), channel_id=1, source_target_pairs={{0,2},{1,3},{2,0},{3,1},{4,6},{5,7},{6,4},{7,5},{8,10},{9,11},{10,... | collective-permute-start | bytes 215048 | tf_op jit(solution)/shard_map/ppermute | solution.py:346

commit v9 on v8

--- a/solution.py
+++ b/solution.py
@@ -159,7 +159,7 @@
         _, row_tab, end_tab, col_tab, weight, core, turn, gx_of, gy_hot, keep, send = refs[:11]
         me = lax.axis_index("fft")
         source = lambda k: pl.ds(me ^ k, 1)
-    lhs, pick, sticks, real, imag, both, half, tail, acc, acc_tail = refs[11:]
+    lhs, pick, sticks, real, imag, both, half, tail, acc, acc_tail, share = refs[11:]
     live = planes * bands
     rows = 2 * live
     total = rows + INFO if first else rows
@@ -284,10 +284,14 @@
         for o in range(owners):
             to = keep if o % 2 == mine_bit else send
             mine = slice(o * own_rows, (o + 1) * own_rows)
-            for j in range(planes):
-                to[o // 2, j, :own_rows, :] = acc[j, mine, :].astype(jnp.bfloat16)
-            for t in range(tails):
-                to[o // 2, planes + t, :own_rows, :] = acc_tail[t, mine, :].astype(jnp.bfloat16)
+            pieces = [acc[j, mine, :] for j in range(planes)]
+            pieces += [acc_tail[t, mine, :] for t in range(tails)]
+            for i, piece in enumerate(pieces):
+                share[i * own_rows : (i + 1) * own_rows, :] = piece
+            to[o // 2] = share[...].astype(jnp.bfloat16)
+
+    if share.shape[0] > (planes + tails) * own_rows:
+        share[...] = jnp.zeros_like(share)
 
     @pl.when(core[0] == 0)
     def _():
@@ -305,8 +309,9 @@
         total = parts[2 * c][...].astype(jnp.float32) + parts[2 * c + 1][...].astype(jnp.float32)
         for j in range(count):
             at = j % SHARE * TAIL
-            out[base + j, :, :LANES] = total[j, :own_rows]
-            out[base + j, :, LANES:] = total[count + j // SHARE, :own_rows, at : at + TAIL]
+            main, end = (i * own_rows for i in (j, count + j // SHARE))
+            out[base + j, :, :LANES] = total[main : main + own_rows]
+            out[base + j, :, LANES:] = total[end : end + own_rows, at : at + TAIL]
         base += count
 
 
@@ -331,7 +336,7 @@
         in_specs=[scalar if i in smem else hbm if i in far else vmem for i in range(n_in)],
         out_specs=[vmem] * len(out_shape) if many else vmem,
         scratch_shapes=list(scratch),
-        compiler_params=pltpu.CompilerParams(vmem_limit_bytes=62 * 2**20 if far else min(62 * 2**20, used + 12 * 2**20)),
+        compiler_params=pltpu.CompilerParams(vmem_limit_bytes=min(62 * 2**20, used + 12 * 2**20)),
         cost_estimate=pl.CostEstimate(flops=flops, bytes_accessed=1 << 20, transcendentals=0),
     )
 
@@ -391,7 +396,7 @@
         + [pltpu.VMEM((ranks, GROUPS * span, LANES), f32) for span in spans * 2],
         flops=4 * 10**9,
         far=range(5),
-    )(counts, plane_slot, fixed, coefficients, columns)
+    )(counts, *[pltpu.with_memory_space_constraint(x, pltpu.HBM) for x in (plane_slot, fixed, coefficients, columns)])
     kept_shapes = [
         jax.ShapeDtypeStruct((ranks, cap), f32),
         jax.ShapeDtypeStruct((cap, LANES), bf16),
@@ -408,9 +413,8 @@
                 pairs = [(i, i ^ k) for i in range(ranks)]
                 received.append(lax.ppermute(outgoing[1 + k], "fft", pairs))
         tails = -(-count // SHARE)
-        dens_shape = jax.ShapeDtypeStruct(
-            (owners // 2, count + tails, up(own_rows, 8), LANES), bf16
-        )
+        dealt = up((count + tails) * own_rows, 8)
+        dens_shape = jax.ShapeDtypeStruct((owners // 2, dealt, LANES), bf16)
         run = vmem_call(
             functools.partial(plane_kernel, first, bands, ranks, count, span, owners, own_rows),
             [dens_shape] * 2 + (kept_shapes if first else []),
@@ -426,6 +430,7 @@
                 pltpu.VMEM((tails, bands, 2 * GB, LANES), bf16),
                 pltpu.VMEM((count, N, LANES), f32),
                 pltpu.VMEM((tails, N, LANES), f32),
+                pltpu.VMEM((dealt, LANES), f32),
             ],
             flops=16 * 10**9,
             smem=(len(received) + 3, len(received) + 4),

time: 59.6 us -> 59.2 us (level)
  waiting for transfers between devices: 11.4 us -> 10.5 us
  transfers between devices with their start and end apart: 12 -> 12, of which waited for: 5 -> 5; matrix products, arithmetic and copies ran while one was open for 0% -> 0% of each run, Pallas kernels for 31% -> 32%
where the time goes in v9:
time: 59.2 us; the launch traced here: 58.5 us
  Pallas kernels  23.5 us (40%)
  starting transfers between devices  23.5 us (40%)
  waiting for transfers between devices  10.5 us (18%)
  between operations  0.78 us (1%)
    pallas_call x2, Pallas kernels, shards(): results = run(*received, *tables, weight, core, *kept)  18.8 us
    ppermute x7, starting transfers between devices, shards(): received.append(lax.ppermute(outgoing[1 + k], 'fft', pairs))  13.8 us
    all_to_all x1, starting transfers between devices, shards(): lax.all_to_all(outgoing[0], 'fft', split_axis=0, concat_axis=0, tiled=True)  7.45 us
    ppermute x4, waiting for transfers between devices, halve(): got = lax.ppermute(send, axis, partners(axis, bit))  6.25 us
    ppermute x7, waiting for transfers between devices, shards(): received.append(lax.ppermute(outgoing[1 + k], 'fft', pairs))  4.23 us
    pallas_call x1, Pallas kernels, shards(): vmem_call(functools.partial(stick_kernel, planes, ranks), [jax.ShapeDtype...  3.69 us
    ppermute x4, starting transfers between devices, halve(): got = lax.ppermute(send, axis, partners(axis, bit))  2.29 us
  transfers between devices with their start and end apart: 12, of which 5 were waited for; matrix products, arithmetic and copies ran while one was open for 0% of the time, Pallas kernels for 32%

profile of v9, /device:TPU:0, one launch (start us, length us, event | category | flops | bytes accessed | tf_op | source)
XLA Modules:
  0.0 58.5 jit_solution(10030843099232450935)
XLA Ops:
  0.7 0.0 copy-start
  0.7 3.7 %shard_map.91 = (bf16[8,192,128]{2,1,0:T(8,128)(2,1)}, bf16[360,128]{1,0:T(8,128)(2,1)S(1)}, bf16[360,128]{1,0:T(8,128)(2,1)S(1)}, bf16[360,128]{1,0:T(8,128)(2,...) custom-call(s32[1]{0:T(128)S(6)} %copy.10.refs_0_, ...), custom_call_target="tpu_custom_call" | custom-call | flops 4000000000 | bytes 1048576 | tf_op jit(solution)/shard_map/pallas_call | solution.py:381
  4.4 0.0 copy-start.1
  4.4 0.0 copy-start.2
  4.4 7.5 %all-to-all-start = ((bf16[8,192,128]{2,1,0:T(8,128)(2,1)}), bf16[8,192,128]{2,1,0:T(8,128)(2,1)S(1)}, u32[]{:S(2)}, u32[]{:S(2)}) async-start(bf16[8,192,128]{2,1,0:T(8,128)(2,1)} %get-tuple-element.21), calls=%async_computation | async-start | bytes 786432 | tf_op jit(solution)/shard_map/all_to_all | solution.py:409
  11.8 2.0 %collective-permute-start.2 = (bf16[360,128]{1,0:T(8,128)(2,1)S(1)}, bf16[360,128]{1,0:T(8,128)(2,1)S(1)}, u32[]{:S(2)}, u32[]{:S(2)}) collective-permute-start(bf16[360,128]{1,0:T(8,128)(2,1)S(1)} %get-tuple-element.25), channel_id=1, source_target_pairs={{0,4},{4,0},{8,12},{12,8},{16,20},{20,16},{24,28},{28,24},{1,5},{5... | collective-permute-start | bytes 276488 | tf_op jit(solution)/shard_map/ppermute | solution.py:414
  13.9 1.5 %collective-permute-start.3 = (bf16[360,128]{1,0:T(8,128)(2,1)S(1)}, bf16[360,128]{1,0:T(8,128)(2,1)S(1)}, u32[]{:S(2)}, u32[]{:S(2)}) collective-permute-start(bf16[360,128]{1,0:T(8,128)(2,1)S(1)} %get-tuple-element.26), channel_id=1, source_target_pairs={{0,8},{4,12},{8,0},{12,4},{16,24},{20,28},{24,16},{28,20},{1,9},{5... | collective-permute-start | bytes 276488 | tf_op jit(solution)/shard_map/ppermute | solution.py:414
  15.3 0.0 collective-permute-start.4
  15.3 0.0 copy-start.3
  15.4 2.9 %collective-permute-start.5 = (bf16[360,128]{1,0:T(8,128)(2,1)S(1)}, bf16[360,128]{1,0:T(8,128)(2,1)S(1)}, u32[]{:S(2)}, u32[]{:S(2)}) collective-permute-start(bf16[360,128]{1,0:T(8,128)(2,1)S(1)} %get-tuple-element.28), channel_id=1, source_target_pairs={{0,16},{4,20},{8,24},{12,28},{16,0},{20,4},{24,8},{28,12},{1,17},{... | collective-permute-start | bytes 276488 | tf_op jit(solution)/shard_map/ppermute | solution.py:414
  18.3 1.5 %collective-permute-start.6 = (bf16[360,128]{1,0:T(8,128)(2,1)S(1)}, bf16[360,128]{1,0:T(8,128)(2,1)S(1)}, u32[]{:S(2)}, u32[]{:S(2)}) collective-permute-start(bf16[360,128]{1,0:T(8,128)(2,1)S(1)} %get-tuple-element.29), channel_id=1, source_target_pairs={{0,20},{4,16},{8,28},{12,24},{16,4},{20,0},{24,12},{28,8},{1,21},{... | collective-permute-start | bytes 276488 | tf_op jit(solution)/shard_map/ppermute | solution.py:414
  19.7 0.0 copy-done.3
  19.7 0.0 collective-permute-done.2.refs_1_
  19.7 3.9 %collective-permute-start.7 = (bf16[360,128]{1,0:T(8,128)(2,1)S(1)}, bf16[360,128]{1,0:T(8,128)(2,1)S(1)}, u32[]{:S(2)}, u32[]{:S(2)}) collective-permute-start(bf16[360,128]{1,0:T(8,128)(2,1)S(1)} %get-tuple-element.30), channel_id=1, source_target_pairs={{0,24},{4,28},{8,16},{12,20},{16,8},{20,12},{24,0},{28,4},{1,25},{... | collective-permute-start | bytes 276488 | tf_op jit(solution)/shard_map/ppermute | solution.py:414
  23.6 1.6 %collective-permute-done.3.refs_2_ = bf16[360,128]{1,0:T(8,128)(2,1)S(1)} collective-permute-done((bf16[360,128]{1,0:T(8,128)(2,1)S(1)}, bf16[360,128]{1,0:T(8,128)(2,1)S(1)}, u32[]{:S(2)}, u32[]{:S(2)}) %collective-permute-start.3) | collective-permute-done | bytes 92192 | tf_op jit(solution)/shard_map/ppermute | solution.py:414
  25.2 2.0 %collective-permute-start.8 = (bf16[360,128]{1,0:T(8,128)(2,1)S(1)}, bf16[360,128]{1,0:T(8,128)(2,1)S(1)}, u32[]{:S(2)}, u32[]{:S(2)}) collective-permute-start(bf16[360,128]{1,0:T(8,128)(2,1)S(1)} %get-tuple-element.31), channel_id=1, source_target_pairs={{0,28},{4,24},{8,20},{12,16},{16,12},{20,8},{24,4},{28,0},{1,29},{... | collective-permute-start | bytes 276488 | tf_op jit(solution)/shard_map/ppermute | solution.py:414
  27.2 0.0 all-to-all-done.refs_0_
  27.2 0.0 copy-done
  27.2 0.0 copy-done.1
  27.2 0.0 copy-done.2
  27.2 7.3 %shard_map.92 = (bf16[2,256,128]{2,1,0:T(8,128)(2,1)S(1)}, bf16[2,256,128]{2,1,0:T(8,128)(2,1)S(1)}, f32[8,512]{1,0:T(8,128)S(1)}, bf16[512,128]{1,0:T(8,128)(2,1)S(1)}, bf16[512,128]{1,0:T(8,128)(2,1)S(1)}) custom-call(bf16[8,192,128]{2,1,0:T(8,128)(2,1)S(1)} %all-to-all-done.refs_0_, bf16[256,256]{1,0:T(8,128)(2,1)S(1)} %copy-done.2, ...), custom_call_target="tpu_custom_call" | custom-call | flops 16000000000 | bytes 1048576 | tf_op jit(solution)/shard_map/pallas_call | solution.py:438
  34.5 0.0 collective-permute-done.4.refs_3_
  34.5 0.1 collective-permute-start
  34.6 0.2 collective-permute-done.5.refs_4_
  34.8 2.5 %collective-permute-done.6.refs_5_ = bf16[360,128]{1,0:T(8,128)(2,1)S(1)} collective-permute-done((bf16[360,128]{1,0:T(8,128)(2,1)S(1)}, bf16[360,128]{1,0:T(8,128)(2,1)S(1)}, u32[]{:S(2)}, u32[]{:S(2)}) %collective-permute-start.6) | collective-permute-done | bytes 92192 | tf_op jit(solution)/shard_map/ppermute | solution.py:414
  37.3 0.0 collective-permute-done.7.refs_6_
  37.3 0.0 collective-permute-done.8.refs_7_
  37.3 11.5 %shard_map.93 = (bf16[2,504,128]{2,1,0:T(8,128)(2,1)S(1)}, bf16[2,504,128]{2,1,0:T(8,128)(2,1)S(1)}) custom-call(bf16[360,128]{1,0:T(8,128)(2,1)S(1)} %get-tuple-element.24.refs_0_, bf16[360,128]{1,0:T(8,128)(2,1)S(1)} %collective-permute-done.2.refs_1_, bf16[360,128]{1,0:T(8,128)(2,1)S(1)} %collective-permute-done.3.refs_2_, ...), custom_call_target="tpu_custom_call" | custom-call | flops 16000000000 | bytes 1048576 | tf_op jit(solution)/shard_map/pallas_call | solution.py:438
  48.8 0.1 collective-permute-start.9
  48.9 0.0 collective-permute-done
  48.9 1.5 %collective-permute-done.9 = bf16[2,504,128]{2,1,0:T(8,128)(2,1)S(1)} collective-permute-done((bf16[2,504,128]{2,1,0:T(8,128)(2,1)S(1)}, bf16[2,504,128]{2,1,0:T(8,128)(2,1)S(1)}, u32[]{:S(2)}, u32[]{:S(2)}) %collective-permute-start.9) | collective-permute-done | bytes 258080 | tf_op jit(solution)/shard_map/ppermute | solution.py:351
  50.4 0.1 add_convert_fusion
  50.5 1.5 %collective-permute-start.10 = (bf16[1,504,128]{2,1,0:T(8,128)(2,1)S(1)}, bf16[1,504,128]{2,1,0:T(8,128)(2,1)S(1)}, u32[]{:S(2)}, u32[]{:S(2)}) collective-permute-start(bf16[1,504,128]{2,1,0:T(8,128)(2,1)S(1)} %get-tuple-element.37), channel_id=1, source_target_pairs={{0,2},{1,3},{2,0},{3,1},{4,6},{5,7},{6,4},{7,5},{8,10},{9,11},{10,... | collective-permute-start | bytes 387080 | tf_op jit(solution)/shard_map/ppermute | solution.py:351
  52.0 0.6 %collective-permute-start.1 = (bf16[1,256,128]{2,1,0:T(8,128)(2,1)S(1)}, bf16[1,256,128]{2,1,0:T(8,128)(2,1)S(1)}, u32[]{:S(2)}, u32[]{:S(2)}) collective-permute-start(bf16[1,256,128]{2,1,0:T(8,128)(2,1)S(1)} %get-tuple-element.39), channel_id=1, source_target_pairs={{0,2},{1,3},{2,0},{3,1},{4,6},{5,7},{6,4},{7,5},{8,10},{9,11},{10,... | collective-permute-start | bytes 196616 | tf_op jit(solution)/shard_map/ppermute | solution.py:351
  52.7 4.8 %collective-permute-done.1 = bf16[1,256,128]{2,1,0:T(8,128)(2,1)S(1)} collective-permute-done((bf16[1,256,128]{2,1,0:T(8,128)(2,1)S(1)}, bf16[1,256,128]{2,1,0:T(8,128)(2,1)S(1)}, u32[]{:S(2)}, u32[]{:S(2)}) %collective-permute-start.1) | collective-permute-done | bytes 65568 | tf_op jit(solution)/shard_map/ppermute | solution.py:351
  57.5 0.0 collective-permute-done.10
  57.5 1.0 %shard_map.94 = f32[18,36,144]{2,1,0:T(8,128)} custom-call(bf16[256,128]{1,0:T(8,128)(2,1)S(1)} %get-tuple-element.40.refs_0_, bf16[256,128]{1,0:T(8,128)(2,1)S(1)} %bitcast.8, bf16[504,128]{1,0:T(8,128)(2,1)S(1)} %get-tuple-element.38.refs_2_, bf16[504,128]{1,0:T(8,128)(2,1)S(1)} %bitcast.7), custom_call_target="tpu_custom_call" | custom-call | flops 1 | bytes 1048576 | tf_op jit(solution)/shard_map/pallas_call | solution.py:442
  (4 shorter events, 0.1 us)
Async XLA Ops:
  0.7 26.6 %copy-start = (bf16[2048,256]{1,0:T(8,128)(2,1)S(1)}, bf16[2048,256]{1,0:T(8,128)(2,1)}, u32[]{:S(2)}) copy-start(bf16[2048,256]{1,0:T(8,128)(2,1)} %constant.34.clone.refs_2_.refs_9_) | copy-start | bytes 3145732
  4.4 22.8 %copy-start.1 = (bf16[288,144]{1,0:T(8,128)(2,1)S(1)}, bf16[288,144]{1,0:T(8,128)(2,1)}, u32[]{:S(2)}) copy-start(bf16[288,144]{1,0:T(8,128)(2,1)} %constant.35.clone.refs_3_.refs_10_) | copy-start | bytes 248836
  4.4 22.8 %copy-start.2 = (bf16[256,256]{1,0:T(8,128)(2,1)S(1)}, bf16[256,256]{1,0:T(8,128)(2,1)}, u32[]{:S(2)}) copy-start(bf16[256,256]{1,0:T(8,128)(2,1)} %constant.33.clone.refs_1_.refs_8_) | copy-start | bytes 393220
  4.4 22.8 %all-to-all-start = ((bf16[8,192,128]{2,1,0:T(8,128)(2,1)}), bf16[8,192,128]{2,1,0:T(8,128)(2,1)S(1)}, u32[]{:S(2)}, u32[]{:S(2)}) async-start(bf16[8,192,128]{2,1,0:T(8,128)(2,1)} %get-tuple-element.21), calls=%async_computation | async-start | bytes 786432 | tf_op jit(solution)/shard_map/all_to_all | solution.py:409
  11.8 7.9 %collective-permute-start.2 = (bf16[360,128]{1,0:T(8,128)(2,1)S(1)}, bf16[360,128]{1,0:T(8,128)(2,1)S(1)}, u32[]{:S(2)}, u32[]{:S(2)}) collective-permute-start(bf16[360,128]{1,0:T(8,128)(2,1)S(1)} %get-tuple-element.25), channel_id=1, source_target_pairs={{0,4},{4,0},{8,12},{12,8},{16,20},{20,16},{24,28},{28,24},{1,5},{5... | collective-permute-start | bytes 276488 | tf_op jit(solution)/shard_map/ppermute | solution.py:414
  13.9 11.4 %collective-permute-start.3 = (bf16[360,128]{1,0:T(8,128)(2,1)S(1)}, bf16[360,128]{1,0:T(8,128)(2,1)S(1)}, u32[]{:S(2)}, u32[]{:S(2)}) collective-permute-start(bf16[360,128]{1,0:T(8,128)(2,1)S(1)} %get-tuple-element.26), channel_id=1, source_target_pairs={{0,8},{4,12},{8,0},{12,4},{16,24},{20,28},{24,16},{28,20},{1,9},{5... | collective-permute-start | bytes 276488 | tf_op jit(solution)/shard_map/ppermute | solution.py:414
  15.3 19.2 %collective-permute-start.4 = (bf16[360,128]{1,0:T(8,128)(2,1)S(1)}, bf16[360,128]{1,0:T(8,128)(2,1)S(1)}, u32[]{:S(2)}, u32[]{:S(2)}) collective-permute-start(bf16[360,128]{1,0:T(8,128)(2,1)S(1)} %get-tuple-element.27), channel_id=1, source_target_pairs={{0,12},{4,8},{8,4},{12,0},{16,28},{20,24},{24,20},{28,16},{1,13},{... | collective-permute-start | bytes 276488 | tf_op jit(solution)/shard_map/ppermute | solution.py:414
  15.3 4.4 %copy-start.3 = (f32[12]{0:T(128)S(1)}, f32[12]{0:T(128)}, u32[]{:S(2)}) copy-start(f32[12]{0:T(128)} %param.10) | copy-start | bytes 148
  15.4 19.5 %collective-permute-start.5 = (bf16[360,128]{1,0:T(8,128)(2,1)S(1)}, bf16[360,128]{1,0:T(8,128)(2,1)S(1)}, u32[]{:S(2)}, u32[]{:S(2)}) collective-permute-start(bf16[360,128]{1,0:T(8,128)(2,1)S(1)} %get-tuple-element.28), channel_id=1, source_target_pairs={{0,16},{4,20},{8,24},{12,28},{16,0},{20,4},{24,8},{28,12},{1,17},{... | collective-permute-start | bytes 276488 | tf_op jit(solution)/shard_map/ppermute | solution.py:414
  18.3 19.0 %collective-permute-start.6 = (bf16[360,128]{1,0:T(8,128)(2,1)S(1)}, bf16[360,128]{1,0:T(8,128)(2,1)S(1)}, u32[]{:S(2)}, u32[]{:S(2)}) collective-permute-start(bf16[360,128]{1,0:T(8,128)(2,1)S(1)} %get-tuple-element.29), channel_id=1, source_target_pairs={{0,20},{4,16},{8,28},{12,24},{16,4},{20,0},{24,12},{28,8},{1,21},{... | collective-permute-start | bytes 276488 | tf_op jit(solution)/shard_map/ppermute | solution.py:414
  19.7 17.5 %collective-permute-start.7 = (bf16[360,128]{1,0:T(8,128)(2,1)S(1)}, bf16[360,128]{1,0:T(8,128)(2,1)S(1)}, u32[]{:S(2)}, u32[]{:S(2)}) collective-permute-start(bf16[360,128]{1,0:T(8,128)(2,1)S(1)} %get-tuple-element.30), channel_id=1, source_target_pairs={{0,24},{4,28},{8,16},{12,20},{16,8},{20,12},{24,0},{28,4},{1,25},{... | collective-permute-start | bytes 276488 | tf_op jit(solution)/shard_map/ppermute | solution.py:414
  25.2 12.1 %collective-permute-start.8 = (bf16[360,128]{1,0:T(8,128)(2,1)S(1)}, bf16[360,128]{1,0:T(8,128)(2,1)S(1)}, u32[]{:S(2)}, u32[]{:S(2)}) collective-permute-start(bf16[360,128]{1,0:T(8,128)(2,1)S(1)} %get-tuple-element.31), channel_id=1, source_target_pairs={{0,28},{4,24},{8,20},{12,16},{16,12},{20,8},{24,4},{28,0},{1,29},{... | collective-permute-start | bytes 276488 | tf_op jit(solution)/shard_map/ppermute | solution.py:414
  34.5 14.3 %collective-permute-start = (bf16[2,256,128]{2,1,0:T(8,128)(2,1)S(1)}, bf16[2,256,128]{2,1,0:T(8,128)(2,1)S(1)}, u32[]{:S(2)}, u32[]{:S(2)}) collective-permute-start(bf16[2,256,128]{2,1,0:T(8,128)(2,1)S(1)} %get-tuple-element.23), channel_id=1, source_target_pairs={{0,1},{1,0},{2,3},{3,2},{4,5},{5,4},{6,7},{7,6},{8,9},{9,8},{10,11... | collective-permute-start | bytes 393224 | tf_op jit(solution)/shard_map/ppermute | solution.py:351
  48.8 1.6 %collective-permute-start.9 = (bf16[2,504,128]{2,1,0:T(8,128)(2,1)S(1)}, bf16[2,504,128]{2,1,0:T(8,128)(2,1)S(1)}, u32[]{:S(2)}, u32[]{:S(2)}) collective-permute-start(bf16[2,504,128]{2,1,0:T(8,128)(2,1)S(1)} %get-tuple-element.36), channel_id=1, source_target_pairs={{0,1},{1,0},{2,3},{3,2},{4,5},{5,4},{6,7},{7,6},{8,9},{9,8},{10,11... | collective-permute-start | bytes 774152 | tf_op jit(solution)/shard_map/ppermute | solution.py:351
  50.5 7.0 %collective-permute-start.10 = (bf16[1,504,128]{2,1,0:T(8,128)(2,1)S(1)}, bf16[1,504,128]{2,1,0:T(8,128)(2,1)S(1)}, u32[]{:S(2)}, u32[]{:S(2)}) collective-permute-start(bf16[1,504,128]{2,1,0:T(8,128)(2,1)S(1)} %get-tuple-element.37), channel_id=1, source_target_pairs={{0,2},{1,3},{2,0},{3,1},{4,6},{5,7},{6,4},{7,5},{8,10},{9,11},{10,... | collective-permute-start | bytes 387080 | tf_op jit(solution)/shard_map/ppermute | solution.py:351
  52.0 5.4 %collective-permute-start.1 = (bf16[1,256,128]{2,1,0:T(8,128)(2,1)S(1)}, bf16[1,256,128]{2,1,0:T(8,128)(2,1)S(1)}, u32[]{:S(2)}, u32[]{:S(2)}) collective-permute-start(bf16[1,256,128]{2,1,0:T(8,128)(2,1)S(1)} %get-tuple-element.39), channel_id=1, source_target_pairs={{0,2},{1,3},{2,0},{3,1},{4,6},{5,7},{6,4},{7,5},{8,10},{9,11},{10,... | collective-permute-start | bytes 196616 | tf_op jit(solution)/shard_map/ppermute | solution.py:351
